TPU v7x, 256 devices: a whole 4x4x8 slice. The times are simulated.
256 devices in a mesh: gx: 2 (over x_lo), gy: 8 (over x_hi, y), gz: 16 (over z, core).
Axes of the slice: x: 4 (x_hi: 2, x_lo: 2; x = x_hi * 2 + x_lo), y: 4, z: 8, core: 2. Of those that a mesh axis runs over, the one named last changes fastest.
Arguments:
- volume: bfloat16 [32, 64, 64, 256], P(None, 'gx', 'gy', 'gz'), may hold values from -6 to 6
- weight_a: bfloat16 [3, 3, 3, 32, 64], replicated, may hold values from -0.21875 to 0.21875
- bias_a: float32 [64], replicated, may hold values from -3 to 3
- weight_b: bfloat16 [3, 3, 3, 64, 128], replicated, may hold values from -0.15625 to 0.15625
- bias_b: float32 [128], replicated, may hold values from -3 to 3
- cotangent: bfloat16 [128, 32, 32, 128], P(None, ('gx', 'gz'), 'gy'), may hold values from -24 to 24
Outputs:
- features: bfloat16 [128, 32, 32, 128], P(None, ('gx', 'gz'), 'gy')
- grad_input: bfloat16 [32, 64, 64, 256], P(None, 'gx', 'gy', 'gz')
- grad_weight_a: float32 [3, 3, 3, 32, 64], replicated
- grad_bias_a: float32 [64], replicated
- grad_weight_b: float32 [3, 3, 3, 64, 128], replicated
- grad_bias_b: float32 [128], replicated
All inputs are finite; a program needn't handle non-finite values.
Results may differ from a plain program's by a relative error of at most 0.012.
Values may be sent and summed in bfloat16 or wider, within the bound.
No kernel may reach another device: no remote copies, remote signals or barrier semaphores. Data moves between devices by JAX's collectives and lax.ppermute only.
A program may use at most 128 MiB of HBM per device.

v0:
```python
import math

import jax
import jax.numpy as jnp
from jax import lax
from jax.sharding import Mesh
from jax.sharding import PartitionSpec as P

GX_GY_GZ = ("gx", "gy", "gz_0", "gz_1")
GZ = ("gz_0", "gz_1")
GX_GZ = ("gx", "gz_0", "gz_1")


def padded_2(block, sides, width):
    for axis, dim in sides:
        count = lax.axis_size(axis)
        forward = [(i, i + 1) for i in range(count - 1)]
        backward = [(target, source) for source, target in forward]
        low = lax.ppermute(
            lax.slice_in_dim(block, block.shape[dim] - width, None, axis=dim), axis, forward
        )
        high = lax.ppermute(lax.slice_in_dim(block, 0, width, axis=dim), axis, backward)
        block = jnp.concatenate([low, block, high], axis=dim)
    return block


def cut_along(array, dim, length):
    lengths = array.shape
    pieces = array.reshape(*lengths[:dim], length, lengths[dim] // length, *lengths[dim + 1 :])
    return jnp.moveaxis(pieces, dim, 0)


def laid_out(pieces, dim):
    lengths = list(pieces.shape[1:])
    lengths[dim] *= pieces.shape[0]
    return jnp.moveaxis(pieces, 0, dim).reshape(lengths)


def moved_by_axis(pieces, axes, order):
    inside = pieces.shape[1:]
    result = pieces.reshape(*(lax.axis_size(a) for a in axes), *inside)
    for k in order:
        result = lax.all_to_all(result, axes[k], k, k, tiled=True)
    return result.reshape(-1, *inside)


def exchange_by_axis(array, axes, order, split_dim, concat_dim):
    pieces = cut_along(array, split_dim, lax.axis_size(axes))
    return laid_out(moved_by_axis(pieces, axes, order), concat_dim)


def together(arrays, axis):
    ends = [0]
    for a in arrays:
        ends.append(ends[-1] + a.size)
    total = lax.psum(jnp.concatenate([a.ravel() for a in arrays]), axis)
    return tuple((total[b:e].reshape(a.shape) for a, b, e in zip(arrays, ends, ends[1:])))


def activate(value):
    return value * jax.nn.sigmoid(value)


def slope_of(value):
    sigma = jax.nn.sigmoid(value)
    return sigma + value * sigma * (1.0 - sigma)


def conv_valid(padded, weight):
    result = lax.conv_general_dilated(
        padded[None],
        weight,
        (1, 1, 1),
        "VALID",
        dimension_numbers=("NCDHW", "DHWIO", "NCDHW"),
        preferred_element_type=jnp.float32,
    )
    return result[0]


def flipped(weight):
    return jnp.transpose(weight[::-1, ::-1, ::-1], (0, 1, 2, 4, 3))


def average_pool(field):
    shape = field.shape
    split = field.reshape(shape[0], shape[1] // 2, 2, shape[2] // 2, 2, shape[3] // 2, 2)
    return jnp.sum(split, axis=(2, 4, 6)) * 0.125


def spread_back(field):
    shape = field.shape
    larger = jnp.broadcast_to(
        field[:, :, None, :, None, :, None], (shape[0], shape[1], 2, shape[2], 2, shape[3], 2)
    )
    return larger.reshape(shape[0], 2 * shape[1], 2 * shape[2], 2 * shape[3])


def weight_terms(padded, grad):
    result = lax.conv_general_dilated(
        padded[None],
        grad[None],
        (1, 1, 1),
        "VALID",
        dimension_numbers=("CNDHW", "IODHW", "NCDHW"),
        preferred_element_type=jnp.float32,
    )
    return jnp.transpose(result, (2, 3, 4, 0, 1))


def fine_halo(field):
    return padded_2(field, (("gx", 1), ("gy", 2), (GZ, 3)), 1)


def coarse_halo(field):
    return padded_2(field, (("gx", 1), ("gy", 2), (GZ, 3)), 1)


def on_device(volume, weight_a, bias_a, weight_b, bias_b, cotangent):
    devices_all = lax.axis_size("gx") * lax.axis_size("gy") * lax.axis_size(GZ)
    cells_fine = volume.shape[1] * volume.shape[2] * volume.shape[3] * devices_all
    scale_a = 1.0 / math.sqrt(cells_fine)
    scale_b = 1.0 / math.sqrt(cells_fine // 8)
    padded_a = fine_halo(volume)
    before_a = conv_valid(padded_a, weight_a) + bias_a[:, None, None, None]
    pooled = average_pool(activate(before_a)).astype(jnp.bfloat16)
    padded_b = coarse_halo(pooled)
    before_b = conv_valid(padded_b, weight_b) + bias_b[:, None, None, None]
    features_block = activate(before_b).astype(jnp.bfloat16)
    features = exchange_by_axis(features_block, GZ, (1, 0), 1, 3)
    cotangent_block = lax.all_to_all(cotangent, GZ, split_axis=3, concat_axis=1, tiled=True)
    grad_b = (cotangent_block * slope_of(before_b)).astype(jnp.bfloat16)
    grad_pooled = conv_valid(coarse_halo(grad_b), flipped(weight_b)).astype(jnp.bfloat16)
    partial_wb = weight_terms(padded_b, grad_b)
    partial_bb = jnp.sum(grad_b, axis=(1, 2, 3), dtype=jnp.float32)
    grad_a = (spread_back(grad_pooled) * 0.125 * slope_of(before_a)).astype(jnp.bfloat16)
    partial_wa = weight_terms(padded_a, grad_a)
    partial_ba = jnp.sum(grad_a, axis=(1, 2, 3), dtype=jnp.float32)
    grad_input = conv_valid(fine_halo(grad_a), flipped(weight_a)).astype(jnp.bfloat16)
    summed_wa, summed_ba, summed_wb, summed_bb = together(
        (partial_wa, partial_ba, partial_wb, partial_bb), GX_GY_GZ
    )
    return (
        features,
        grad_input,
        summed_wa * scale_a,
        summed_ba * scale_a,
        summed_wb * scale_b,
        summed_bb * scale_b,
    )


def solution(mesh):
    finer = Mesh(
        mesh.devices.reshape(mesh.shape["gx"], mesh.shape["gy"], 8, 2), ("gx", "gy", "gz_0", "gz_1")
    )
    return jax.shard_map(
        on_device,
        mesh=finer,
        in_specs=(P(None, "gx", "gy", GZ), P(), P(), P(), P(), P(None, GX_GZ, "gy", None)),
        out_specs=(P(None, GX_GZ, "gy", None), P(None, "gx", "gy", GZ), P(), P(), P(), P()),
        check_vma=False,
    )
```

profile of v0, /device:TPU:1, one launch (start us, length us, event | category | flops | bytes accessed | tf_op | source)
XLA Modules:
  0.0 505.8 jit_solution(1847951043806130101)
XLA Ops:
  7.2 3.2 fusion.46
  10.4 2.3 copy.164
  12.7 3.9 collective-permute-start
  20.8 1.8 collective-permute-done.1
  22.6 1.8 copy.130
  25.7 3.2 collective-permute-start.2
  30.8 3.8 collective-permute-done.3
  34.7 7.0 %collective-permute-start.4 = (bf16[32,34,10,1]{1,0,3,2:T(8,128)(2,1)S(1)}, bf16[32,34,10,1]{1,0,3,2:T(8,128)(2,1)S(1)}, u32[]{:S(2)}, u32[]{:S(2)}) collective-permute-start(bf16[32,34,10,1]{1,0,3,2:T(8,128)(2,1)S(1)} %get-tuple-element.40), channel_id=1, source_target_pairs={{0,1},{1,2},{2,3},{3,4},{4,5},{5,6},{6,7},{7,8},{8,9},{9,10},{10,1... | collective-permute-start | bytes 65288 | tf_op jit(solution)/shard_map/ppermute | solution.py:19
  41.7 2.2 collective-permute-start.5
  44.0 3.5 collective-permute-done.5
  48.5 1.7 pad
  50.2 4.9 copy.132
  55.1 1.7 slice.117
  56.8 8.4 %multiply_add_fusion = (f32[32,8,8,3,64]{4,2,3,1,0:T(8,128)}, f32[32,8,8,3,64]{4,2,3,1,0:T(8,128)S(1)}) fusion(f32[64]{0:T(128)S(1)} %copy-done.23, bf16[3,3,3,32,64]{4,3,2,1,0:T(8,128)(2,1)S(1)} %copy-done.25, bf16[32,34,10,1,7,2]{0,4,5,2,1,3:T(8,128)(2,1)S(1)} %slice.117, bf16[32,34,10,1,8,3]{0,4,5,2,1,3:T(8,128)(2,1)} %copy.132, ...), kind=kOutput, calls=%fused_computation.17 | convolution fusion | flops 685627392 | bytes 4083480 | tf_op jit(solution)/shard_map/conv_general_dilated | solution.py:70
  67.5 1.3 collective-permute-start.6
  70.2 3.1 collective-permute-done.7
  73.3 3.2 collective-permute-start.8
  77.8 3.4 collective-permute-done.9
  81.3 4.7 collective-permute-start.10
  86.0 1.9 collective-permute-start.11
  88.7 11.8 %all-to-all-start.2 = ((bf16[128,1,4,128]{0,2,1,3:T(4,128)(2,1)}), bf16[128,1,4,128]{0,2,1,3:T(4,128)(2,1)S(1)}, u32[]{:S(2)}, u32[]{:S(2)}) async-start(bf16[128,1,4,128]{0,2,1,3:T(4,128)(2,1)} %copy.141), calls=%async_computation.2 | async-start | bytes 262144 | tf_op jit(solution)/shard_map/all_to_all | solution.py:131
  101.6 1.9 fusion.32
  103.6 5.7 %all-to-all-done.2 = bf16[128,1,4,128]{0,2,1,3:T(4,128)(2,1)S(1)} async-done(((bf16[128,1,4,128]{0,2,1,3:T(4,128)(2,1)}), bf16[128,1,4,128]{0,2,1,3:T(4,128)(2,1)S(1)}, u32[]{:S(2)}, u32[]{:S(2)}) %all-to-all-start.2) | async-done | bytes 131104 | tf_op jit(solution)/shard_map/all_to_all | solution.py:131
  109.9 1.4 collective-permute-start.12
  112.6 3.4 fusion.54
  116.0 7.7 %copy.151 = bf16[1,32,34,10,18]{1,0,4,3,2:T(2,128)(2,1)} copy(bf16[1,32,34,10,18]{2,1,4,3,0:T(8,128)(2,1)} %fusion.54) | data formatting | bytes 783360 | tf_op jit(solution)/shard_map/broadcast_in_dim | solution.py:71
  123.7 4.2 copy.150
  127.9 6.6 %collective-permute-start.14 = (bf16[128,18,1,8]{0,3,2,1:T(8,128)(2,1)S(1)}, bf16[128,18,1,8]{0,3,2,1:T(8,128)(2,1)S(1)}, u32[]{:S(2)}, u32[]{:S(2)}) collective-permute-start(bf16[128,18,1,8]{0,3,2,1:T(8,128)(2,1)S(1)} %get-tuple-element.56), channel_id=1, source_target_pairs={{0,16},{16,32},{32,48},{48,64},{64,80},{80,96},{96,112},{1,17},{17... | collective-permute-start | bytes 110600 | tf_op jit(solution)/shard_map/ppermute | solution.py:19
  135.9 3.9 all_to_all.19
  140.5 4.0 all-to-all-start.1
  144.6 3.7 collective-permute-start.16
  148.4 1.9 collective-permute-start.17
  150.4 3.8 collective-permute-done.17
  154.5 2.8 fusion.28
  159.0 4.3 collective-permute-start.18
  164.6 4.2 fusion.30
  169.2 4.3 collective-permute-start.20
  176.0 2.3 collective-permute-done.20
  178.3 5.7 %collective-permute-done.21 = bf16[64,34,1,16]{0,2,3,1:T(2,128)(2,1)S(1)} collective-permute-done((bf16[64,34,1,16]{0,2,3,1:T(2,128)(2,1)S(1)}, bf16[64,34,1,16]{0,2,3,1:T(2,128)(2,1)S(1)}, u32[]{:S(2)}, u32[]{:S(2)}) %collective-permute-start.21) | collective-permute-done | bytes 69664 | tf_op jit(solution)/shard_map/ppermute | solution.py:22
  184.9 4.8 collective-permute-start.22
  189.8 2.1 collective-permute-start.23
  191.9 24.5 %fusion.18 = f32[3,3,3,32,64]{4,3,2,1,0:T(8,128)} fusion(bf16[1,32,34,10,18]{1,0,4,3,2:T(2,128)(2,1)S(1)} %copy-done.8, bf16[1,64,32,8,16]{1,3,4,2,0:T(8,128)(2,1)S(1)} %get-tuple-element.39), kind=kOutput, calls=%fused_computation.27 | convolution fusion | flops 452984832 | bytes 1137152 | tf_op jit(solution)/shard_map/transpose | solution.py:108
  217.7 8.6 %concatenate.51 = f32[276672]{0:T(1024)} concatenate(f32[55296]{0:T(1024)S(1)} %reshape.130, f32[64]{0:T(128)S(1)} %copy-done.24, f32[221184]{0:T(1024)S(1)} %bitcast.99, f32[128]{0:T(128)S(1)} %copy-done.22), dimensions={0} | concatenate | bytes 2213376 | tf_op jit(solution)/shard_map/concatenate | solution.py:56
  228.1 4.1 maximum_bitcast_fusion
  234.1 11.4 %select_convert_fusion = bf16[32,8,8,3,32]{4,2,3,1,0:T(8,128)(2,1)S(1)} fusion(pred[8,3]{0,1:T(4,128)(4,1)S(1)} %copy-done.28, bf16[3,3,3,32,64]{4,3,2,1,0:T(8,128)(2,1)S(1)} %copy-done.26, bf16[64,34,10,1,7,2]{0,4,5,2,1,3:T(8,128)(2,1)S(1)} %slice.125, bf16[64,34,10,1,8,3]{0,4,5,2,1,3:T(8,128)(2,1)S(1)} %copy.148), kind=kOutput, calls=%fused_computation.16 | convolution fusion | flops 685092864 | bytes 2157592 | tf_op jit(solution)/shard_map/conv_general_dilated | solution.py:70
  245.9 2.9 copy.157
  248.8 243.3 %all-reduce.2.cloned.1.call-done = f32[276672]{0:T(1024)} async-done(((f32[276672]{0:T(1024)}), f32[276672]{0:T(1024)}) %all-reduce.2.cloned.1.call-update) | async-done | bytes 1106704 | tf_op jit(solution)/shard_map/psum | solution.py:56
  496.3 2.4 slice_multiply_fusion
  (128 shorter events, 36.1 us)
Async XLA Ops:
  7.2 94.4 %copy-start = (bf16[3,3,3,64,128]{4,3,2,1,0:T(8,128)(2,1)S(1)}, bf16[3,3,3,64,128]{4,3,2,1,0:T(8,128)(2,1)}, u32[]{:S(2)}) copy-start(bf16[3,3,3,64,128]{4,3,2,1,0:T(8,128)(2,1)} %param.9) | copy-start | bytes 1327108
  7.2 12.0 %copy-start.6 = (bf16[32,32,8,16]{1,3,2,0:T(8,128)(2,1)S(1)}, bf16[32,32,8,16]{1,3,2,0:T(8,128)(2,1)}, u32[]{:S(2)}) copy-start(bf16[32,32,8,16]{1,3,2,0:T(8,128)(2,1)} %param.6) | copy-start | bytes 786436
  12.7 7.2 %collective-permute-start = (bf16[32,1,8,16]{0,3,2,1:T(8,128)(2,1)S(1)}, bf16[32,1,8,16]{0,3,2,1:T(8,128)(2,1)S(1)}, u32[]{:S(2)}, u32[]{:S(2)}) collective-permute-start(bf16[32,1,8,16]{0,3,2,1:T(8,128)(2,1)S(1)} %copy.164), channel_id=1, source_target_pairs={{0,128},{1,129},{2,130},{3,131},{4,132},{5,133},{6,134},{7,135},{8... | collective-permute-start | bytes 24584 | tf_op jit(solution)/shard_map/ppermute | solution.py:19
  17.9 4.7 collective-permute-start.1
  24.4 10.2 %copy-start.1 = (bf16[32,1,8,16]{1,0,3,2:T(8,128)(2,1)S(1)}, bf16[32,1,8,16]{1,0,3,2:T(8,128)(2,1)}, u32[]{:S(2)}) copy-start(bf16[32,1,8,16]{1,0,3,2:T(8,128)(2,1)} %copy.130) | copy-start | bytes 24580
  25.7 5.1 %collective-permute-start.2 = (bf16[32,34,1,16]{1,0,3,2:T(8,128)(2,1)S(1)}, bf16[32,34,1,16]{1,0,3,2:T(8,128)(2,1)S(1)}, u32[]{:S(2)}, u32[]{:S(2)}) collective-permute-start(bf16[32,34,1,16]{1,0,3,2:T(8,128)(2,1)S(1)} %get-tuple-element.42), channel_id=1, source_target_pairs={{0,16},{16,32},{32,48},{48,64},{64,80},{80,96},{96,112},{1,17},{17... | collective-permute-start | bytes 104456 | tf_op jit(solution)/shard_map/ppermute | solution.py:19
  28.9 5.7 %collective-permute-start.3 = (bf16[32,34,1,16]{1,0,3,2:T(8,128)(2,1)S(1)}, bf16[32,34,1,16]{1,0,3,2:T(8,128)(2,1)S(1)}, u32[]{:S(2)}, u32[]{:S(2)}) collective-permute-start(bf16[32,34,1,16]{1,0,3,2:T(8,128)(2,1)S(1)} %get-tuple-element.43), channel_id=1, source_target_pairs={{16,0},{32,16},{48,32},{64,48},{80,64},{96,80},{112,96},{17,1},{33... | collective-permute-start | bytes 104456 | tf_op jit(solution)/shard_map/ppermute | solution.py:22
  34.7 9.2 %collective-permute-start.4 = (bf16[32,34,10,1]{1,0,3,2:T(8,128)(2,1)S(1)}, bf16[32,34,10,1]{1,0,3,2:T(8,128)(2,1)S(1)}, u32[]{:S(2)}, u32[]{:S(2)}) collective-permute-start(bf16[32,34,10,1]{1,0,3,2:T(8,128)(2,1)S(1)} %get-tuple-element.40), channel_id=1, source_target_pairs={{0,1},{1,2},{2,3},{3,4},{4,5},{5,6},{6,7},{7,8},{8,9},{9,10},{10,1... | collective-permute-start | bytes 65288 | tf_op jit(solution)/shard_map/ppermute | solution.py:19
  41.7 5.8 %collective-permute-start.5 = (bf16[32,34,10,1]{1,0,3,2:T(8,128)(2,1)S(1)}, bf16[32,34,10,1]{1,0,3,2:T(8,128)(2,1)S(1)}, u32[]{:S(2)}, u32[]{:S(2)}) collective-permute-start(bf16[32,34,10,1]{1,0,3,2:T(8,128)(2,1)S(1)} %get-tuple-element.41), channel_id=1, source_target_pairs={{1,0},{2,1},{3,2},{4,3},{5,4},{6,5},{7,6},{8,7},{9,8},{10,9},{11,1... | collective-permute-start | bytes 65288 | tf_op jit(solution)/shard_map/ppermute | solution.py:22
  50.2 6.6 %copy-start.25 = (bf16[3,3,3,32,64]{4,3,2,1,0:T(8,128)(2,1)S(1)}, bf16[3,3,3,32,64]{4,3,2,1,0:T(8,128)(2,1)}, u32[]{:S(2)}) copy-start(bf16[3,3,3,32,64]{4,3,2,1,0:T(8,128)(2,1)} %param.7) | copy-start | bytes 331780
  50.2 6.6 %copy-start.27 = (pred[8,3]{0,1:T(4,128)(4,1)S(1)}, pred[8,3]{0,1:T(4,128)(4,1)}, u32[]{:S(2)}) copy-start(pred[8,3]{0,1:T(4,128)(4,1)} %constant.24) | copy-start | bytes 76
  65.8 22.2 %copy-start.20 = (bf16[128,1,4,128]{3,2,1,0:T(4,128)(2,1)S(1)}, bf16[128,1,4,128]{3,2,1,0:T(4,128)(2,1)}, u32[]{:S(2)}) copy-start(bf16[128,1,4,128]{3,2,1,0:T(4,128)(2,1)} %param.11) | copy-start | bytes 393220
  67.5 2.6 collective-permute-start.6
  68.8 4.4 collective-permute-start.7
  73.3 4.5 collective-permute-start.8
  76.5 4.7 collective-permute-start.9
  81.3 19.3 %collective-permute-start.10 = (bf16[64,18,6,1]{0,3,2,1:T(2,128)(2,1)S(1)}, bf16[64,18,6,1]{0,3,2,1:T(2,128)(2,1)S(1)}, u32[]{:S(2)}, u32[]{:S(2)}) collective-permute-start(bf16[64,18,6,1]{0,3,2,1:T(2,128)(2,1)S(1)} %get-tuple-element.54), channel_id=1, source_target_pairs={{0,1},{1,2},{2,3},{3,4},{4,5},{5,6},{6,7},{7,8},{8,9},{9,10},{10,1... | collective-permute-start | bytes 41480 | tf_op jit(solution)/shard_map/ppermute | solution.py:19
  86.0 14.6 %collective-permute-start.11 = (bf16[64,18,6,1]{0,3,2,1:T(2,128)(2,1)S(1)}, bf16[64,18,6,1]{0,3,2,1:T(2,128)(2,1)S(1)}, u32[]{:S(2)}, u32[]{:S(2)}) collective-permute-start(bf16[64,18,6,1]{0,3,2,1:T(2,128)(2,1)S(1)} %get-tuple-element.55), channel_id=1, source_target_pairs={{1,0},{2,1},{3,2},{4,3},{5,4},{6,5},{7,6},{8,7},{9,8},{10,9},{11,1... | collective-permute-start | bytes 41480 | tf_op jit(solution)/shard_map/ppermute | solution.py:22
  88.7 20.6 %all-to-all-start.2 = ((bf16[128,1,4,128]{0,2,1,3:T(4,128)(2,1)}), bf16[128,1,4,128]{0,2,1,3:T(4,128)(2,1)S(1)}, u32[]{:S(2)}, u32[]{:S(2)}) async-start(bf16[128,1,4,128]{0,2,1,3:T(4,128)(2,1)} %copy.141), calls=%async_computation.2 | async-start | bytes 262144 | tf_op jit(solution)/shard_map/all_to_all | solution.py:131
  100.5 8.8 %copy-start.21 = (f32[128]{0:T(128)S(1)}, f32[128]{0:T(128)}, u32[]{:S(2)}) copy-start(f32[128]{0:T(128)} %param.10) | copy-start | bytes 1540
  109.9 17.9 %collective-permute-start.12 = (bf16[128,1,4,8]{0,3,2,1:T(8,128)(2,1)S(1)}, bf16[128,1,4,8]{0,3,2,1:T(8,128)(2,1)S(1)}, u32[]{:S(2)}, u32[]{:S(2)}) collective-permute-start(bf16[128,1,4,8]{0,3,2,1:T(8,128)(2,1)S(1)} %get-tuple-element.60), channel_id=1, source_target_pairs={{0,128},{1,129},{2,130},{3,131},{4,132},{5,133},{6,134},{7,135},{8... | collective-permute-start | bytes 24584 | tf_op jit(solution)/shard_map/ppermute | solution.py:19
  111.3 16.6 %collective-permute-start.13 = (bf16[128,1,4,8]{0,3,2,1:T(8,128)(2,1)S(1)}, bf16[128,1,4,8]{0,3,2,1:T(8,128)(2,1)S(1)}, u32[]{:S(2)}, u32[]{:S(2)}) collective-permute-start(bf16[128,1,4,8]{0,3,2,1:T(8,128)(2,1)S(1)} %get-tuple-element.61), channel_id=1, source_target_pairs={{128,0},{129,1},{130,2},{131,3},{132,4},{133,5},{134,6},{135,7},{1... | collective-permute-start | bytes 24584 | tf_op jit(solution)/shard_map/ppermute | solution.py:22
  127.9 16.6 %collective-permute-start.14 = (bf16[128,18,1,8]{0,3,2,1:T(8,128)(2,1)S(1)}, bf16[128,18,1,8]{0,3,2,1:T(8,128)(2,1)S(1)}, u32[]{:S(2)}, u32[]{:S(2)}) collective-permute-start(bf16[128,18,1,8]{0,3,2,1:T(8,128)(2,1)S(1)} %get-tuple-element.56), channel_id=1, source_target_pairs={{0,16},{16,32},{32,48},{48,64},{64,80},{80,96},{96,112},{1,17},{17... | collective-permute-start | bytes 110600 | tf_op jit(solution)/shard_map/ppermute | solution.py:19
  134.5 10.0 %collective-permute-start.15 = (bf16[128,18,1,8]{0,3,2,1:T(8,128)(2,1)S(1)}, bf16[128,18,1,8]{0,3,2,1:T(8,128)(2,1)S(1)}, u32[]{:S(2)}, u32[]{:S(2)}) collective-permute-start(bf16[128,18,1,8]{0,3,2,1:T(8,128)(2,1)S(1)} %get-tuple-element.57), channel_id=1, source_target_pairs={{16,0},{32,16},{48,32},{64,48},{80,64},{96,80},{112,96},{17,1},{33... | collective-permute-start | bytes 110600 | tf_op jit(solution)/shard_map/ppermute | solution.py:22
  140.5 85.9 %all-to-all-start.1 = ((bf16[8,2,128,1,4,8]{2,5,4,1,3,0:T(8,128)(2,1)}), bf16[8,2,128,1,4,8]{2,5,4,1,3,0:T(8,128)(2,1)}, u32[]{:S(2)}, u32[]{:S(2)}) async-start(bf16[8,2,128,1,4,8]{2,5,4,1,3,0:T(8,128)(2,1)} %copy.139), calls=%async_computation.1 | async-start | bytes 262144 | tf_op jit(solution)/shard_map/all_to_all | solution.py:43
  144.5 347.6 %all-reduce.2.cloned.1.call-start = ((), (), s32[]{:S(2)}) async-start(), calls=%async_computation.3 | async-start | bytes 2220032 | tf_op jit(solution)/shard_map/psum | solution.py:56
  144.6 5.8 %collective-permute-start.16 = (bf16[128,18,6,1]{0,3,2,1:T(2,128)(2,1)S(1)}, bf16[128,18,6,1]{0,3,2,1:T(2,128)(2,1)S(1)}, u32[]{:S(2)}, u32[]{:S(2)}) collective-permute-start(bf16[128,18,6,1]{0,3,2,1:T(2,128)(2,1)S(1)} %get-tuple-element.52), channel_id=1, source_target_pairs={{0,1},{1,2},{2,3},{3,4},{4,5},{5,6},{6,7},{7,8},{8,9},{9,10},{10,1... | collective-permute-start | bytes 82952 | tf_op jit(solution)/shard_map/ppermute | solution.py:19
  148.4 5.9 %collective-permute-start.17 = (bf16[128,18,6,1]{0,3,2,1:T(2,128)(2,1)S(1)}, bf16[128,18,6,1]{0,3,2,1:T(2,128)(2,1)S(1)}, u32[]{:S(2)}, u32[]{:S(2)}) collective-permute-start(bf16[128,18,6,1]{0,3,2,1:T(2,128)(2,1)S(1)} %get-tuple-element.53), channel_id=1, source_target_pairs={{1,0},{2,1},{3,2},{4,3},{5,4},{6,5},{7,6},{8,7},{9,8},{10,9},{11,1... | collective-permute-start | bytes 82952 | tf_op jit(solution)/shard_map/ppermute | solution.py:22
  159.0 25.0 %copy-start.2 = (bf16[64,32,8,16]{0,2,3,1:T(8,128)(2,1)}, bf16[64,32,8,16]{0,2,3,1:T(8,128)(2,1)S(1)}, u32[]{:S(2)}) copy-start(bf16[64,32,8,16]{0,2,3,1:T(8,128)(2,1)S(1)} %multiply_convert_fusion) | copy-start | bytes 1572868
  159.0 9.7 %collective-permute-start.18 = (bf16[64,1,8,16]{0,2,3,1:T(8,128)(2,1)S(1)}, bf16[64,1,8,16]{0,2,3,1:T(8,128)(2,1)S(1)}, u32[]{:S(2)}, u32[]{:S(2)}) collective-permute-start(bf16[64,1,8,16]{0,2,3,1:T(8,128)(2,1)S(1)} %get-tuple-element.48), channel_id=1, source_target_pairs={{0,128},{1,129},{2,130},{3,131},{4,132},{5,133},{6,134},{7,135},{8... | collective-permute-start | bytes 49160 | tf_op jit(solution)/shard_map/ppermute | solution.py:19
  163.3 5.5 %collective-permute-start.19 = (bf16[64,1,8,16]{0,2,3,1:T(8,128)(2,1)S(1)}, bf16[64,1,8,16]{0,2,3,1:T(8,128)(2,1)S(1)}, u32[]{:S(2)}, u32[]{:S(2)}) collective-permute-start(bf16[64,1,8,16]{0,2,3,1:T(8,128)(2,1)S(1)} %get-tuple-element.49), channel_id=1, source_target_pairs={{128,0},{129,1},{130,2},{131,3},{132,4},{133,5},{134,6},{135,7},{1... | collective-permute-start | bytes 49160 | tf_op jit(solution)/shard_map/ppermute | solution.py:22
  164.6 10.2 %copy-start.7 = (f32[32,8,8,3,64]{4,1,3,2,0:T(8,128)S(1)}, f32[32,8,8,3,64]{4,1,3,2,0:T(8,128)}, u32[]{:S(2)}) copy-start(f32[32,8,8,3,64]{4,1,3,2,0:T(8,128)} %copy.150) | copy-start | bytes 4718596
  168.8 15.2 %copy-start.16 = (bf16[64,1,8,16]{0,2,3,1:T(8,128)(2,1)}, bf16[64,1,8,16]{0,2,3,1:T(8,128)(2,1)S(1)}, u32[]{:S(2)}) copy-start(bf16[64,1,8,16]{0,2,3,1:T(8,128)(2,1)S(1)} %collective-permute-done.18) | copy-start | bytes 49156
  168.8 15.2 %copy-start.18 = (bf16[64,1,8,16]{0,2,3,1:T(8,128)(2,1)}, bf16[64,1,8,16]{0,2,3,1:T(8,128)(2,1)S(1)}, u32[]{:S(2)}) copy-start(bf16[64,1,8,16]{0,2,3,1:T(8,128)(2,1)S(1)} %collective-permute-done.19) | copy-start | bytes 49156
  169.2 9.1 %collective-permute-start.20 = (bf16[64,34,1,16]{0,2,3,1:T(2,128)(2,1)S(1)}, bf16[64,34,1,16]{0,2,3,1:T(2,128)(2,1)S(1)}, u32[]{:S(2)}, u32[]{:S(2)}) collective-permute-start(bf16[64,34,1,16]{0,2,3,1:T(2,128)(2,1)S(1)} %get-tuple-element.46), channel_id=1, source_target_pairs={{0,16},{16,32},{32,48},{48,64},{64,80},{80,96},{96,112},{1,17},{17... | collective-permute-start | bytes 208904 | tf_op jit(solution)/shard_map/ppermute | solution.py:19
  173.5 10.5 %collective-permute-start.21 = (bf16[64,34,1,16]{0,2,3,1:T(2,128)(2,1)S(1)}, bf16[64,34,1,16]{0,2,3,1:T(2,128)(2,1)S(1)}, u32[]{:S(2)}, u32[]{:S(2)}) collective-permute-start(bf16[64,34,1,16]{0,2,3,1:T(2,128)(2,1)S(1)} %get-tuple-element.47), channel_id=1, source_target_pairs={{16,0},{32,16},{48,32},{64,48},{80,64},{96,80},{112,96},{17,1},{33... | collective-permute-start | bytes 208904 | tf_op jit(solution)/shard_map/ppermute | solution.py:22
  174.8 17.1 %copy-start.8 = (bf16[1,32,34,10,18]{1,0,4,3,2:T(2,128)(2,1)S(1)}, bf16[1,32,34,10,18]{1,0,4,3,2:T(2,128)(2,1)}, u32[]{:S(2)}) copy-start(bf16[1,32,34,10,18]{1,0,4,3,2:T(2,128)(2,1)} %copy.151) | copy-start | bytes 1175044
  178.3 6.6 %copy-start.9 = (bf16[64,34,1,16]{0,2,3,1:T(2,128)(2,1)}, bf16[64,34,1,16]{0,2,3,1:T(2,128)(2,1)S(1)}, u32[]{:S(2)}) copy-start(bf16[64,34,1,16]{0,2,3,1:T(2,128)(2,1)S(1)} %collective-permute-done.20) | copy-start | bytes 208900
  184.9 43.2 %collective-permute-start.22 = (bf16[64,34,10,1]{0,2,3,1:T(8,128)(2,1)}, bf16[64,34,10,1]{0,2,3,1:T(8,128)(2,1)}, u32[]{:S(2)}, u32[]{:S(2)}) collective-permute-start(bf16[64,34,10,1]{0,2,3,1:T(8,128)(2,1)} %get-tuple-element.44), channel_id=1, source_target_pairs={{0,1},{1,2},{2,3},{3,4},{4,5},{5,6},{6,7},{7,8},{8,9},{9,10},{10,1... | collective-permute-start | bytes 130568 | tf_op jit(solution)/shard_map/ppermute | solution.py:19
  189.8 38.3 %collective-permute-start.23 = (bf16[64,34,10,1]{0,2,3,1:T(8,128)(2,1)}, bf16[64,34,10,1]{0,2,3,1:T(8,128)(2,1)}, u32[]{:S(2)}, u32[]{:S(2)}) collective-permute-start(bf16[64,34,10,1]{0,2,3,1:T(8,128)(2,1)} %get-tuple-element.45), channel_id=1, source_target_pairs={{1,0},{2,1},{3,2},{4,3},{5,4},{6,5},{7,6},{8,7},{9,8},{10,9},{11,1... | collective-permute-start | bytes 130568 | tf_op jit(solution)/shard_map/ppermute | solution.py:22
  191.9 25.8 %copy-start.13 = (f32[3,3,3,64,128]{4,3,2,1,0:T(8,128)S(1)}, f32[3,3,3,64,128]{4,3,2,1,0:T(8,128)}, u32[]{:S(2)}) copy-start(f32[3,3,3,64,128]{4,3,2,1,0:T(8,128)} %fusion.30) | copy-start | bytes 2654212
  191.9 25.8 %copy-start.22 = (f32[128]{0:T(128)S(1)}, f32[128]{0:T(128)}, u32[]{:S(2)}) copy-start(f32[128]{0:T(128)} %get-tuple-element.36) | copy-start | bytes 1540
  191.9 25.8 %copy-start.24 = (f32[64]{0:T(128)S(1)}, f32[64]{0:T(128)}, u32[]{:S(2)}) copy-start(f32[64]{0:T(128)} %get-tuple-element.38) | copy-start | bytes 772
  216.4 11.7 %copy-start.3 = (bf16[64,32,8,16]{0,2,3,1:T(8,128)(2,1)S(1)}, bf16[64,32,8,16]{0,2,3,1:T(8,128)(2,1)}, u32[]{:S(2)}) copy-start(bf16[64,32,8,16]{0,2,3,1:T(8,128)(2,1)} %copy-done.2) | copy-start | bytes 1572868
  216.4 11.7 %copy-start.10 = (bf16[64,34,1,16]{0,2,3,1:T(2,128)(2,1)S(1)}, bf16[64,34,1,16]{0,2,3,1:T(2,128)(2,1)}, u32[]{:S(2)}) copy-start(bf16[64,34,1,16]{0,2,3,1:T(2,128)(2,1)} %copy-done.9) | copy-start | bytes 208900
  216.4 11.7 %copy-start.12 = (bf16[64,34,1,16]{0,2,3,1:T(2,128)(2,1)S(1)}, bf16[64,34,1,16]{0,2,3,1:T(2,128)(2,1)}, u32[]{:S(2)}) copy-start(bf16[64,34,1,16]{0,2,3,1:T(2,128)(2,1)} %copy-done.11) | copy-start | bytes 208900
  216.4 11.7 %copy-start.17 = (bf16[64,1,8,16]{0,2,3,1:T(8,128)(2,1)S(1)}, bf16[64,1,8,16]{0,2,3,1:T(8,128)(2,1)}, u32[]{:S(2)}) copy-start(bf16[64,1,8,16]{0,2,3,1:T(8,128)(2,1)} %copy-done.16) | copy-start | bytes 49156
  216.4 11.7 %copy-start.19 = (bf16[64,1,8,16]{0,2,3,1:T(8,128)(2,1)S(1)}, bf16[64,1,8,16]{0,2,3,1:T(8,128)(2,1)}, u32[]{:S(2)}) copy-start(bf16[64,1,8,16]{0,2,3,1:T(8,128)(2,1)} %copy-done.18) | copy-start | bytes 49156
  (8 other events, 21.9 us)
Sparse Core Ops, SparseCore 0:
  226.5 265.5 all-reduce.1
where the time goes:
time: 512 us; the launch traced here: 506 us
  waiting for transfers between devices  277 us (54%)
  starting transfers between devices  82.7 us (16%)
  matrix products  53.1 us (10%)
  local copies, waits for them, and re-layouts  51.9 us (10%)
  other arithmetic  22 us (4%)
  between operations  15.1 us (3%)
    psum x1, waiting for transfers between devices, together(): total = lax.psum(jnp.concatenate([a.ravel() for a in arrays]), axis)  243 us
    ppermute x12, starting transfers between devices, padded_2(): lax.ppermute(lax.slice_in_dim(block, block.shape[dim] - width, None, axis...  48.4 us
    transpose x2, matrix products, weight_terms(): return jnp.transpose(result, (2, 3, 4, 0, 1))  28.6 us
    ppermute x12, waiting for transfers between devices, padded_2(): lax.ppermute(lax.slice_in_dim(block, 0, width, axis=dim), axis, backward)  25.1 us
    conv_general_dilated x4, matrix products, conv_valid(): lax.conv_general_dilated(padded[None], weight, (1, 1, 1), 'VALID', dimens...  24.5 us
    ppermute x12, starting transfers between devices, padded_2(): lax.ppermute(lax.slice_in_dim(block, 0, width, axis=dim), axis, backward)  18.5 us
    all_to_all x1, starting transfers between devices, on_device(): lax.all_to_all(cotangent, GZ, split_axis=3, concat_axis=1, tiled=True)  11.8 us
  transfers between devices with their start and end apart: 27, of which 11 were waited for; matrix products, arithmetic and copies ran while one was open for 18% of the time, Pallas kernels for 0%

commit v1 on v0

--- a/solution.py
+++ b/solution.py
@@ -53,7 +53,14 @@
     ends = [0]
     for a in arrays:
         ends.append(ends[-1] + a.size)
-    total = lax.psum(jnp.concatenate([a.ravel() for a in arrays]), axis)
+    count = lax.axis_size(axis)
+    width = 640
+    flat = jnp.concatenate([a.ravel().astype(jnp.bfloat16) for a in arrays])
+    flat = jnp.pad(flat, (0, count * 2 * width - flat.size))
+    shares = lax.all_to_all(flat.reshape(count, 2, width), axis, 0, 0, tiled=True)
+    share = jnp.sum(shares.astype(jnp.float32), axis=0).astype(jnp.bfloat16)
+    spread = jnp.broadcast_to(share[None], (count, 2, width))
+    total = lax.all_to_all(spread, axis, 0, 0, tiled=True).ravel().astype(jnp.float32)
     return tuple((total[b:e].reshape(a.shape) for a, b, e in zip(arrays, ends, ends[1:])))
 
 

time: 512 us -> 299 us (0.58)
  waiting for transfers between devices: 277 us -> 40.7 us
  starting transfers between devices: 82.7 us -> 118 us
  between operations: 15.1 us -> 1.82 us
    psum x1 -> x0, waiting for transfers between devices: 243 us -> none  [together(): total = lax.psum(jnp.concatenate([a.ravel() for a in arrays]), axis)]
    all_to_all x0 -> x2, starting transfers between devices: none -> 35.9 us  [the longest x1 20.5 us: together(): lax.all_to_all(flat.reshape(count, 2, width), axis, 0, 0, tiled=True)]
    all_to_all x0 -> x2, waiting for transfers between devices: none -> 6.9 us  [the longest x1 6.9 us: together(): lax.all_to_all(spread, axis, 0, 0, tiled=True).ravel().astype(jnp.float32)]
    all_to_all x1, waiting for transfers between devices: 5.73 us -> 0.01 us  [on_device(): lax.all_to_all(cotangent, GZ, split_axis=3, concat_axis=1, tiled=True)]
    unnamed x64 -> x46, local copies, waits for them, and re-layouts: 9.79 us -> 10.4 us
  transfers between devices with their start and end apart: 27 -> 28, of which waited for: 11 -> 11; matrix products, arithmetic and copies ran while one was open for 18% -> 32% of each run, Pallas kernels for 0% -> 0%
where the time goes in v1:
time: 299 us; the launch traced here: 293 us
  starting transfers between devices  118 us (39%)
  local copies, waits for them, and re-layouts  55.9 us (19%)
  matrix products  53.5 us (18%)
  waiting for transfers between devices  40.7 us (14%)
  other arithmetic  19.8 us (7%)
  blocking collectives  3.49 us (1%)
    ppermute x12, starting transfers between devices, padded_2(): lax.ppermute(lax.slice_in_dim(block, block.shape[dim] - width, None, axis...  44.9 us
    ppermute x12, waiting for transfers between devices, padded_2(): lax.ppermute(lax.slice_in_dim(block, 0, width, axis=dim), axis, backward)  28.4 us
    transpose x2, matrix products, weight_terms(): return jnp.transpose(result, (2, 3, 4, 0, 1))  27.9 us
    conv_general_dilated x4, matrix products, conv_valid(): lax.conv_general_dilated(padded[None], weight, (1, 1, 1), 'VALID', dimens...  25.5 us
    all_to_all x1, starting transfers between devices, together(): lax.all_to_all(flat.reshape(count, 2, width), axis, 0, 0, tiled=True)  20.5 us
    ppermute x12, starting transfers between devices, padded_2(): lax.ppermute(lax.slice_in_dim(block, 0, width, axis=dim), axis, backward)  18.7 us
    all_to_all x1, starting transfers between devices, together(): lax.all_to_all(spread, axis, 0, 0, tiled=True).ravel().astype(jnp.float32)  15.4 us
    unnamed x46, local copies, waits for them, and re-layouts  10.4 us
  transfers between devices with their start and end apart: 28, of which 11 were waited for; matrix products, arithmetic and copies ran while one was open for 32% of the time, Pallas kernels for 0%

profile of v1, /device:TPU:1, one launch (start us, length us, event | category | flops | bytes accessed | tf_op | source)
XLA Modules:
  0.0 293.1 jit_solution(13137138762674285512)
XLA Ops:
  0.7 3.3 %fusion.50 = (bf16[32,1,8,16]{1,3,2,0:T(8,128)(2,1)}, bf16[32,1,8,16]{1,3,2,0:T(8,128)(2,1)S(1)}) fusion(bf16[32,32,8,16]{1,3,2,0:T(8,128)(2,1)} %param.6), kind=kLoop, calls=%fused_computation.97 | loop fusion | bytes 32768 | tf_op jit(solution)/shard_map/slice | solution.py:20
  3.9 2.3 copy.223
  6.3 3.9 %collective-permute-start = (bf16[32,1,8,16]{0,3,2,1:T(8,128)(2,1)S(1)}, bf16[32,1,8,16]{0,3,2,1:T(8,128)(2,1)S(1)}, u32[]{:S(2)}, u32[]{:S(2)}) collective-permute-start(bf16[32,1,8,16]{0,3,2,1:T(8,128)(2,1)S(1)} %copy.223), channel_id=1, source_target_pairs={{0,128},{1,129},{2,130},{3,131},{4,132},{5,133},{6,134},{7,135},{8... | collective-permute-start | bytes 24584 | tf_op jit(solution)/shard_map/ppermute | solution.py:19
  14.3 1.8 collective-permute-done.1
  16.1 1.8 copy.187
  19.2 3.2 %collective-permute-start.2 = (bf16[32,34,1,16]{1,0,3,2:T(8,128)(2,1)S(1)}, bf16[32,34,1,16]{1,0,3,2:T(8,128)(2,1)S(1)}, u32[]{:S(2)}, u32[]{:S(2)}) collective-permute-start(bf16[32,34,1,16]{1,0,3,2:T(8,128)(2,1)S(1)} %get-tuple-element.54), channel_id=1, source_target_pairs={{0,16},{16,32},{32,48},{48,64},{64,80},{80,96},{96,112},{1,17},{17... | collective-permute-start | bytes 104456 | tf_op jit(solution)/shard_map/ppermute | solution.py:19
  24.4 3.8 %collective-permute-done.3 = bf16[32,34,1,16]{1,0,3,2:T(8,128)(2,1)S(1)} collective-permute-done((bf16[32,34,1,16]{1,0,3,2:T(8,128)(2,1)S(1)}, bf16[32,34,1,16]{1,0,3,2:T(8,128)(2,1)S(1)}, u32[]{:S(2)}, u32[]{:S(2)}) %collective-permute-start.3) | collective-permute-done | bytes 34848 | tf_op jit(solution)/shard_map/ppermute | solution.py:22
  28.3 7.0 %collective-permute-start.4 = (bf16[32,34,10,1]{1,0,3,2:T(8,128)(2,1)S(1)}, bf16[32,34,10,1]{1,0,3,2:T(8,128)(2,1)S(1)}, u32[]{:S(2)}, u32[]{:S(2)}) collective-permute-start(bf16[32,34,10,1]{1,0,3,2:T(8,128)(2,1)S(1)} %get-tuple-element.52), channel_id=1, source_target_pairs={{0,1},{1,2},{2,3},{3,4},{4,5},{5,6},{6,7},{7,8},{8,9},{9,10},{10,1... | collective-permute-start | bytes 65288 | tf_op jit(solution)/shard_map/ppermute | solution.py:19
  35.3 2.1 collective-permute-start.5
  37.4 3.6 %collective-permute-done.5 = bf16[32,34,10,1]{1,0,3,2:T(8,128)(2,1)S(1)} collective-permute-done((bf16[32,34,10,1]{1,0,3,2:T(8,128)(2,1)S(1)}, bf16[32,34,10,1]{1,0,3,2:T(8,128)(2,1)S(1)}, u32[]{:S(2)}, u32[]{:S(2)}) %collective-permute-start.5) | collective-permute-done | bytes 21792 | tf_op jit(solution)/shard_map/ppermute | solution.py:22
  42.1 1.7 pad.5
  43.8 4.9 %copy.189 = bf16[32,34,10,1,8,3]{0,4,5,2,1,3:T(8,128)(2,1)} copy(bf16[32,34,10,1,8,3]{1,0,5,4,2,3:T(8,128)(2,1)} %bitcast.93) | data formatting | bytes 1044480 | tf_op jit(solution)/shard_map/conv_general_dilated | solution.py:77
  48.7 1.7 slice.117
  50.4 8.4 %multiply_add_fusion = (f32[32,8,8,3,64]{4,2,3,1,0:T(8,128)}, f32[32,8,8,3,64]{4,2,3,1,0:T(8,128)S(1)}) fusion(f32[64]{0:T(128)S(1)} %copy-done.14, bf16[3,3,3,32,64]{4,3,2,1,0:T(8,128)(2,1)S(1)} %copy-done.16, bf16[32,34,10,1,7,2]{0,4,5,2,1,3:T(8,128)(2,1)S(1)} %slice.117, bf16[32,34,10,1,8,3]{0,4,5,2,1,3:T(8,128)(2,1)} %copy.189, ...), kind=kOutput, calls=%fused_computation.17 | convolution fusion | flops 685627392 | bytes 4083480 | tf_op jit(solution)/shard_map/conv_general_dilated | solution.py:77
  63.7 3.1 %collective-permute-done.7 = bf16[64,1,4,8]{0,3,2,1:T(8,128)(2,1)S(1)} collective-permute-done((bf16[64,1,4,8]{0,3,2,1:T(8,128)(2,1)S(1)}, bf16[64,1,4,8]{0,3,2,1:T(8,128)(2,1)S(1)}, u32[]{:S(2)}, u32[]{:S(2)}) %collective-permute-start.7) | collective-permute-done | bytes 4128 | tf_op jit(solution)/shard_map/ppermute | solution.py:22
  66.8 3.2 %collective-permute-start.8 = (bf16[64,18,1,8]{0,3,2,1:T(8,128)(2,1)S(1)}, bf16[64,18,1,8]{0,3,2,1:T(8,128)(2,1)S(1)}, u32[]{:S(2)}, u32[]{:S(2)}) collective-permute-start(bf16[64,18,1,8]{0,3,2,1:T(8,128)(2,1)S(1)} %get-tuple-element.70), channel_id=1, source_target_pairs={{0,16},{16,32},{32,48},{48,64},{64,80},{80,96},{96,112},{1,17},{17... | collective-permute-start | bytes 55304 | tf_op jit(solution)/shard_map/ppermute | solution.py:19
  72.1 9.8 %all-to-all-start.2 = ((bf16[128,1,4,128]{0,2,1,3:T(4,128)(2,1)}), bf16[128,1,4,128]{0,2,1,3:T(4,128)(2,1)S(1)}, u32[]{:S(2)}, u32[]{:S(2)}) async-start(bf16[128,1,4,128]{0,2,1,3:T(4,128)(2,1)} %copy.198), calls=%async_computation.2 | async-start | bytes 262144 | tf_op jit(solution)/shard_map/all_to_all | solution.py:138
  82.1 3.5 %collective-permute-start.10 = (bf16[64,18,6,1]{0,3,2,1:T(2,128)(2,1)S(1)}, bf16[64,18,6,1]{0,3,2,1:T(2,128)(2,1)S(1)}, u32[]{:S(2)}, u32[]{:S(2)}) collective-permute-start(bf16[64,18,6,1]{0,3,2,1:T(2,128)(2,1)S(1)} %get-tuple-element.66), channel_id=1, source_target_pairs={{0,1},{1,2},{2,3},{3,4},{4,5},{5,6},{6,7},{7,8},{8,9},{9,10},{10,1... | collective-permute-start | bytes 41480 | tf_op jit(solution)/shard_map/ppermute | solution.py:19
  85.6 2.4 collective-permute-start.11
  88.0 3.4 %fusion.58 = bf16[1,32,34,10,18]{2,1,4,3,0:T(8,128)(2,1)} fusion(bf16[32,34,10,1]{1,0,3,2:T(8,128)(2,1)S(1)} %collective-permute-done.5, bf16[32,34,1,16]{1,0,3,2:T(8,128)(2,1)S(1)} %collective-permute-done.3, bf16[32,1,8,16]{1,0,3,2:T(8,128)(2,1)} %copy.187, bf16[32,32,8,16]{1,0,3,2:T(8,128)(2,1)S(1)} %copy.186, bf16[32,1,8,16]{1,0,3,2:T(8,128)(2,1)S(1)} %copy.185, ...), kind=kLoop, calls=%fused_computation.100 | loop fusion | flops 2741760 | bytes 783360 | tf_op jit(solution)/shard_map/broadcast_in_dim | solution.py:78
  91.4 7.7 %copy.208 = bf16[1,32,34,10,18]{1,0,4,3,2:T(2,128)(2,1)} copy(bf16[1,32,34,10,18]{2,1,4,3,0:T(8,128)(2,1)} %fusion.58) | data formatting | bytes 783360 | tf_op jit(solution)/shard_map/broadcast_in_dim | solution.py:78
  99.1 4.2 %copy.207 = f32[32,8,8,3,64]{4,1,3,2,0:T(8,128)} copy(f32[32,8,8,3,64]{4,2,3,1,0:T(8,128)} %get-tuple-element.76) | data formatting | bytes 3145728 | tf_op jit(solution)/shard_map/add | solution.py:73
  103.6 1.9 fusion.34
  109.0 3.5 %all_to_all.29 = bf16[8,2,128,1,4,8]{2,5,4,0,3,1:T(8,128)(2,1)S(1)} all-to-all(bf16[8,2,128,1,4,8]{2,5,4,0,3,1:T(8,128)(2,1)S(1)} %copy.195), channel_id=1, replica_groups=mesh['gx'=2,'gy'=8,'gz_0'=8,'gz_1'=2] {'gz_1'}, dimensions={1} | all-to-all | bytes 262144 | tf_op jit(solution)/shard_map/all_to_all | solution.py:43
  113.2 8.5 %all-to-all-start.1 = ((bf16[8,2,128,1,4,8]{2,5,4,1,3,0:T(8,128)(2,1)}), bf16[8,2,128,1,4,8]{2,5,4,1,3,0:T(8,128)(2,1)}, u32[]{:S(2)}, u32[]{:S(2)}) async-start(bf16[8,2,128,1,4,8]{2,5,4,1,3,0:T(8,128)(2,1)} %copy.196), calls=%async_computation.1 | async-start | bytes 262144 | tf_op jit(solution)/shard_map/all_to_all | solution.py:43
  121.7 4.3 %collective-permute-start.14 = (bf16[128,18,1,8]{0,3,2,1:T(8,128)(2,1)S(1)}, bf16[128,18,1,8]{0,3,2,1:T(8,128)(2,1)S(1)}, u32[]{:S(2)}, u32[]{:S(2)}) collective-permute-start(bf16[128,18,1,8]{0,3,2,1:T(8,128)(2,1)S(1)} %get-tuple-element.68), channel_id=1, source_target_pairs={{0,16},{16,32},{32,48},{48,64},{64,80},{80,96},{96,112},{1,17},{17... | collective-permute-start | bytes 110600 | tf_op jit(solution)/shard_map/ppermute | solution.py:19
  127.4 6.5 %collective-permute-done.15 = bf16[128,18,1,8]{0,3,2,1:T(8,128)(2,1)S(1)} collective-permute-done((bf16[128,18,1,8]{0,3,2,1:T(8,128)(2,1)S(1)}, bf16[128,18,1,8]{0,3,2,1:T(8,128)(2,1)S(1)}, u32[]{:S(2)}, u32[]{:S(2)}) %collective-permute-start.15) | collective-permute-done | bytes 36896 | tf_op jit(solution)/shard_map/ppermute | solution.py:22
  134.0 5.3 %collective-permute-start.16 = (bf16[128,18,6,1]{0,3,2,1:T(2,128)(2,1)S(1)}, bf16[128,18,6,1]{0,3,2,1:T(2,128)(2,1)S(1)}, u32[]{:S(2)}, u32[]{:S(2)}) collective-permute-start(bf16[128,18,6,1]{0,3,2,1:T(2,128)(2,1)S(1)} %get-tuple-element.64), channel_id=1, source_target_pairs={{0,1},{1,2},{2,3},{3,4},{4,5},{5,6},{6,7},{7,8},{8,9},{9,10},{10,1... | collective-permute-start | bytes 82952 | tf_op jit(solution)/shard_map/ppermute | solution.py:19
  139.3 1.9 collective-permute-start.17
  141.2 4.0 %convolution_convert_fusion = bf16[3,3,3,64,128]{4,3,2,1,0:T(8,128)(2,1)} fusion(bf16[1,64,18,6,10]{1,4,3,2,0:T(8,128)(2,1)S(1)} %maximum_bitcast_fusion.1, bf16[1,128,16,4,8]{1,4,3,2,0:T(8,128)(2,1)S(1)} %fusion.36), kind=kOutput, calls=%fused_computation.32 | convolution fusion | flops 226713600 | bytes 711680 | tf_op jit(solution)/shard_map/transpose | solution.py:115
  145.5 2.8 fusion.31
  151.8 24.0 %fusion.27 = bf16[3,3,3,32,64]{4,3,2,1,0:T(8,128)(2,1)S(1)} fusion(bf16[1,32,34,10,18]{1,0,4,3,2:T(2,128)(2,1)S(1)} %copy-done.8, bf16[1,64,32,8,16]{1,3,4,2,0:T(8,128)(2,1)S(1)} %get-tuple-element.51), kind=kOutput, calls=%fused_computation.33 | convolution fusion | flops 453040128 | bytes 1026560 | tf_op jit(solution)/shard_map/transpose | solution.py:115
  176.0 8.1 %concatenate.51 = bf16[276672]{0:T(1024)(128)(2,1)} concatenate(bf16[55296]{0:T(1024)(128)(2,1)S(1)} %convert_element_type.135, bf16[64]{0:T(256)(128)(2,1)S(1)} %copy-done.13, bf16[221184]{0:T(1024)(128)(2,1)S(1)} %bitcast.101, bf16[128]{0:T(256)(128)(2,1)S(1)} %copy-done.12), dimensions={0} | concatenate | bytes 1106688 | tf_op jit(solution)/shard_map/concatenate | solution.py:58
  186.3 20.5 %all-to-all-start.3 = ((bf16[256,2,640]{2,1,0:T(2,128)(2,1)}), bf16[256,2,640]{2,1,0:T(2,128)(2,1)S(1)}, u32[]{:S(2)}, u32[]{:S(2)}) async-start(bf16[256,2,640]{2,1,0:T(2,128)(2,1)} %reshape.135), calls=%async_computation.3 | async-start | bytes 1310720 | tf_op jit(solution)/shard_map/all_to_all | solution.py:60
  206.8 2.4 multiply_convert_fusion
  209.3 3.3 %collective-permute-start.18 = (bf16[64,1,8,16]{0,2,3,1:T(8,128)(2,1)S(1)}, bf16[64,1,8,16]{0,2,3,1:T(8,128)(2,1)S(1)}, u32[]{:S(2)}, u32[]{:S(2)}) collective-permute-start(bf16[64,1,8,16]{0,2,3,1:T(8,128)(2,1)S(1)} %get-tuple-element.60), channel_id=1, source_target_pairs={{0,128},{1,129},{2,130},{3,131},{4,132},{5,133},{6,134},{7,135},{8... | collective-permute-start | bytes 49160 | tf_op jit(solution)/shard_map/ppermute | solution.py:19
  213.8 3.9 %collective-permute-done.19 = bf16[64,1,8,16]{0,2,3,1:T(8,128)(2,1)S(1)} collective-permute-done((bf16[64,1,8,16]{0,2,3,1:T(8,128)(2,1)S(1)}, bf16[64,1,8,16]{0,2,3,1:T(8,128)(2,1)S(1)}, u32[]{:S(2)}, u32[]{:S(2)}) %collective-permute-start.19) | collective-permute-done | bytes 16416 | tf_op jit(solution)/shard_map/ppermute | solution.py:22
  218.2 3.1 %collective-permute-start.20 = (bf16[64,34,1,16]{0,2,3,1:T(2,128)(2,1)S(1)}, bf16[64,34,1,16]{0,2,3,1:T(2,128)(2,1)S(1)}, u32[]{:S(2)}, u32[]{:S(2)}) collective-permute-start(bf16[64,34,1,16]{0,2,3,1:T(2,128)(2,1)S(1)} %get-tuple-element.58), channel_id=1, source_target_pairs={{0,16},{16,32},{32,48},{48,64},{64,80},{80,96},{96,112},{1,17},{17... | collective-permute-start | bytes 208904 | tf_op jit(solution)/shard_map/ppermute | solution.py:19
  222.6 4.8 %collective-permute-done.20 = bf16[64,34,1,16]{0,2,3,1:T(2,128)(2,1)S(1)} collective-permute-done((bf16[64,34,1,16]{0,2,3,1:T(2,128)(2,1)S(1)}, bf16[64,34,1,16]{0,2,3,1:T(2,128)(2,1)S(1)}, u32[]{:S(2)}, u32[]{:S(2)}) %collective-permute-start.20) | collective-permute-done | bytes 69664 | tf_op jit(solution)/shard_map/ppermute | solution.py:19
  227.4 3.0 %collective-permute-done.21 = bf16[64,34,1,16]{0,2,3,1:T(2,128)(2,1)S(1)} collective-permute-done((bf16[64,34,1,16]{0,2,3,1:T(2,128)(2,1)S(1)}, bf16[64,34,1,16]{0,2,3,1:T(2,128)(2,1)S(1)}, u32[]{:S(2)}, u32[]{:S(2)}) %collective-permute-start.21) | collective-permute-done | bytes 69664 | tf_op jit(solution)/shard_map/ppermute | solution.py:22
  230.6 5.4 %collective-permute-start.22 = (bf16[64,34,10,1]{0,2,3,1:T(8,128)(2,1)S(1)}, bf16[64,34,10,1]{0,2,3,1:T(8,128)(2,1)S(1)}, u32[]{:S(2)}, u32[]{:S(2)}) collective-permute-start(bf16[64,34,10,1]{0,2,3,1:T(8,128)(2,1)S(1)} %get-tuple-element.56), channel_id=1, source_target_pairs={{0,1},{1,2},{2,3},{3,4},{4,5},{5,6},{6,7},{7,8},{8,9},{9,10},{10,1... | collective-permute-start | bytes 130568 | tf_op jit(solution)/shard_map/ppermute | solution.py:19
  236.0 1.9 collective-permute-start.23
  239.7 2.7 collective-permute-done.23
  242.4 3.9 %maximum_bitcast_fusion = bf16[64,34,10,1,18]{0,2,4,1,3:T(8,128)(2,1)S(1)} fusion(bf16[64,34,10,1]{0,2,3,1:T(8,128)(2,1)S(1)} %collective-permute-done.23, bf16[64,34,1,16]{0,2,3,1:T(2,128)(2,1)S(1)} %collective-permute-done.21, bf16[64,1,8,16]{0,2,3,1:T(8,128)(2,1)S(1)} %collective-permute-done.19, bf16[64,32,8,16]{0,2,3,1:T(8,128)(2,1)} %copy-done.4, ...), kind=kLoop, calls=%fused_computation.18 | loop fusion | flops 5483520 | bytes 1566720 | tf_op jit(solution)/shard_map/broadcast_in_dim | solution.py:78
  251.0 15.4 %all-to-all-start.4 = ((bf16[256,2,640]{2,1,0:T(2,128)(2,1)}), bf16[256,2,640]{2,1,0:T(2,128)(2,1)S(1)}, u32[]{:S(2)}, u32[]{:S(2)}) async-start(bf16[256,2,640]{2,1,0:T(2,128)(2,1)} %broadcast_in_dim.17), calls=%async_computation.4 | async-start | bytes 1310720 | tf_op jit(solution)/shard_map/all_to_all | solution.py:63
  266.4 12.4 %select_convert_fusion = bf16[32,8,8,3,32]{4,2,3,1,0:T(8,128)(2,1)S(1)} fusion(pred[8,3]{0,1:T(4,128)(4,1)S(1)} %copy-done.19, bf16[3,3,3,32,64]{4,3,2,1,0:T(8,128)(2,1)S(1)} %copy-done.17, bf16[64,34,10,1,7,2]{0,4,5,2,1,3:T(8,128)(2,1)} %slice.125, bf16[64,34,10,1,8,3]{0,4,5,2,1,3:T(8,128)(2,1)S(1)} %copy.205), kind=kOutput, calls=%fused_computation.16 | convolution fusion | flops 685092864 | bytes 2157592 | tf_op jit(solution)/shard_map/conv_general_dilated | solution.py:77
  279.3 2.9 copy.215
  282.2 6.9 %all-to-all-done.4 = bf16[256,2,640]{2,1,0:T(2,128)(2,1)S(1)} async-done(((bf16[256,2,640]{2,1,0:T(2,128)(2,1)}), bf16[256,2,640]{2,1,0:T(2,128)(2,1)S(1)}, u32[]{:S(2)}, u32[]{:S(2)}) %all-to-all-start.4) | async-done | bytes 655392 | tf_op jit(solution)/shard_map/all_to_all | solution.py:63
  (116 shorter events, 41.1 us)
Async XLA Ops:
  0.6 103.0 %copy-start = (bf16[3,3,3,64,128]{4,3,2,1,0:T(8,128)(2,1)S(1)}, bf16[3,3,3,64,128]{4,3,2,1,0:T(8,128)(2,1)}, u32[]{:S(2)}) copy-start(bf16[3,3,3,64,128]{4,3,2,1,0:T(8,128)(2,1)} %param.9) | copy-start | bytes 1327108
  0.6 12.1 %copy-start.6 = (bf16[32,32,8,16]{1,3,2,0:T(8,128)(2,1)S(1)}, bf16[32,32,8,16]{1,3,2,0:T(8,128)(2,1)}, u32[]{:S(2)}) copy-start(bf16[32,32,8,16]{1,3,2,0:T(8,128)(2,1)} %param.6) | copy-start | bytes 786436
  6.3 7.2 %collective-permute-start = (bf16[32,1,8,16]{0,3,2,1:T(8,128)(2,1)S(1)}, bf16[32,1,8,16]{0,3,2,1:T(8,128)(2,1)S(1)}, u32[]{:S(2)}, u32[]{:S(2)}) collective-permute-start(bf16[32,1,8,16]{0,3,2,1:T(8,128)(2,1)S(1)} %copy.223), channel_id=1, source_target_pairs={{0,128},{1,129},{2,130},{3,131},{4,132},{5,133},{6,134},{7,135},{8... | collective-permute-start | bytes 24584 | tf_op jit(solution)/shard_map/ppermute | solution.py:19
  11.5 4.7 %collective-permute-start.1 = (bf16[32,1,8,16]{0,3,2,1:T(8,128)(2,1)S(1)}, bf16[32,1,8,16]{0,3,2,1:T(8,128)(2,1)S(1)}, u32[]{:S(2)}, u32[]{:S(2)}) collective-permute-start(bf16[32,1,8,16]{0,3,2,1:T(8,128)(2,1)S(1)} %copy.224), channel_id=1, source_target_pairs={{128,0},{129,1},{130,2},{131,3},{132,4},{133,5},{134,6},{135,7},{1... | collective-permute-start | bytes 24584 | tf_op jit(solution)/shard_map/ppermute | solution.py:22
  17.9 10.2 %copy-start.1 = (bf16[32,1,8,16]{1,0,3,2:T(8,128)(2,1)S(1)}, bf16[32,1,8,16]{1,0,3,2:T(8,128)(2,1)}, u32[]{:S(2)}) copy-start(bf16[32,1,8,16]{1,0,3,2:T(8,128)(2,1)} %copy.187) | copy-start | bytes 24580
  19.2 5.1 %collective-permute-start.2 = (bf16[32,34,1,16]{1,0,3,2:T(8,128)(2,1)S(1)}, bf16[32,34,1,16]{1,0,3,2:T(8,128)(2,1)S(1)}, u32[]{:S(2)}, u32[]{:S(2)}) collective-permute-start(bf16[32,34,1,16]{1,0,3,2:T(8,128)(2,1)S(1)} %get-tuple-element.54), channel_id=1, source_target_pairs={{0,16},{16,32},{32,48},{48,64},{64,80},{80,96},{96,112},{1,17},{17... | collective-permute-start | bytes 104456 | tf_op jit(solution)/shard_map/ppermute | solution.py:19
  22.4 5.7 %collective-permute-start.3 = (bf16[32,34,1,16]{1,0,3,2:T(8,128)(2,1)S(1)}, bf16[32,34,1,16]{1,0,3,2:T(8,128)(2,1)S(1)}, u32[]{:S(2)}, u32[]{:S(2)}) collective-permute-start(bf16[32,34,1,16]{1,0,3,2:T(8,128)(2,1)S(1)} %get-tuple-element.55), channel_id=1, source_target_pairs={{16,0},{32,16},{48,32},{64,48},{80,64},{96,80},{112,96},{17,1},{33... | collective-permute-start | bytes 104456 | tf_op jit(solution)/shard_map/ppermute | solution.py:22
  28.3 9.1 %collective-permute-start.4 = (bf16[32,34,10,1]{1,0,3,2:T(8,128)(2,1)S(1)}, bf16[32,34,10,1]{1,0,3,2:T(8,128)(2,1)S(1)}, u32[]{:S(2)}, u32[]{:S(2)}) collective-permute-start(bf16[32,34,10,1]{1,0,3,2:T(8,128)(2,1)S(1)} %get-tuple-element.52), channel_id=1, source_target_pairs={{0,1},{1,2},{2,3},{3,4},{4,5},{5,6},{6,7},{7,8},{8,9},{9,10},{10,1... | collective-permute-start | bytes 65288 | tf_op jit(solution)/shard_map/ppermute | solution.py:19
  35.3 5.8 %collective-permute-start.5 = (bf16[32,34,10,1]{1,0,3,2:T(8,128)(2,1)S(1)}, bf16[32,34,10,1]{1,0,3,2:T(8,128)(2,1)S(1)}, u32[]{:S(2)}, u32[]{:S(2)}) collective-permute-start(bf16[32,34,10,1]{1,0,3,2:T(8,128)(2,1)S(1)} %get-tuple-element.53), channel_id=1, source_target_pairs={{1,0},{2,1},{3,2},{4,3},{5,4},{6,5},{7,6},{8,7},{9,8},{10,9},{11,1... | collective-permute-start | bytes 65288 | tf_op jit(solution)/shard_map/ppermute | solution.py:22
  43.8 6.6 %copy-start.14 = (f32[64]{0:T(128)S(1)}, f32[64]{0:T(128)}, u32[]{:S(2)}) copy-start(f32[64]{0:T(128)} %param.8) | copy-start | bytes 772
  43.8 6.6 %copy-start.16 = (bf16[3,3,3,32,64]{4,3,2,1,0:T(8,128)(2,1)S(1)}, bf16[3,3,3,32,64]{4,3,2,1,0:T(8,128)(2,1)}, u32[]{:S(2)}) copy-start(bf16[3,3,3,32,64]{4,3,2,1,0:T(8,128)(2,1)} %param.7) | copy-start | bytes 331780
  43.8 6.6 %copy-start.18 = (pred[8,3]{0,1:T(4,128)(4,1)S(1)}, pred[8,3]{0,1:T(4,128)(4,1)}, u32[]{:S(2)}) copy-start(pred[8,3]{0,1:T(4,128)(4,1)} %constant.32) | copy-start | bytes 76
  59.4 1.7 copy-start.5
  59.4 12.0 %copy-start.10 = (bf16[128,1,4,128]{3,2,1,0:T(4,128)(2,1)S(1)}, bf16[128,1,4,128]{3,2,1,0:T(4,128)(2,1)}, u32[]{:S(2)}) copy-start(bf16[128,1,4,128]{3,2,1,0:T(4,128)(2,1)} %param.11) | copy-start | bytes 393220
  61.1 2.6 collective-permute-start.6
  62.4 4.4 %collective-permute-start.7 = (bf16[64,1,4,8]{0,3,2,1:T(8,128)(2,1)S(1)}, bf16[64,1,4,8]{0,3,2,1:T(8,128)(2,1)S(1)}, u32[]{:S(2)}, u32[]{:S(2)}) collective-permute-start(bf16[64,1,4,8]{0,3,2,1:T(8,128)(2,1)S(1)} %get-tuple-element.75), channel_id=1, source_target_pairs={{128,0},{129,1},{130,2},{131,3},{132,4},{133,5},{134,6},{135,7},{1... | collective-permute-start | bytes 12296 | tf_op jit(solution)/shard_map/ppermute | solution.py:22
  66.8 15.1 %collective-permute-start.8 = (bf16[64,18,1,8]{0,3,2,1:T(8,128)(2,1)S(1)}, bf16[64,18,1,8]{0,3,2,1:T(8,128)(2,1)S(1)}, u32[]{:S(2)}, u32[]{:S(2)}) collective-permute-start(bf16[64,18,1,8]{0,3,2,1:T(8,128)(2,1)S(1)} %get-tuple-element.70), channel_id=1, source_target_pairs={{0,16},{16,32},{32,48},{48,64},{64,80},{80,96},{96,112},{1,17},{17... | collective-permute-start | bytes 55304 | tf_op jit(solution)/shard_map/ppermute | solution.py:19
  70.0 11.9 %collective-permute-start.9 = (bf16[64,18,1,8]{0,3,2,1:T(8,128)(2,1)S(1)}, bf16[64,18,1,8]{0,3,2,1:T(8,128)(2,1)S(1)}, u32[]{:S(2)}, u32[]{:S(2)}) collective-permute-start(bf16[64,18,1,8]{0,3,2,1:T(8,128)(2,1)S(1)} %get-tuple-element.71), channel_id=1, source_target_pairs={{16,0},{32,16},{48,32},{64,48},{80,64},{96,80},{112,96},{17,1},{33... | collective-permute-start | bytes 55304 | tf_op jit(solution)/shard_map/ppermute | solution.py:22
  72.1 33.4 %all-to-all-start.2 = ((bf16[128,1,4,128]{0,2,1,3:T(4,128)(2,1)}), bf16[128,1,4,128]{0,2,1,3:T(4,128)(2,1)S(1)}, u32[]{:S(2)}, u32[]{:S(2)}) async-start(bf16[128,1,4,128]{0,2,1,3:T(4,128)(2,1)} %copy.198), calls=%async_computation.2 | async-start | bytes 262144 | tf_op jit(solution)/shard_map/all_to_all | solution.py:138
  82.1 21.2 %collective-permute-start.10 = (bf16[64,18,6,1]{0,3,2,1:T(2,128)(2,1)S(1)}, bf16[64,18,6,1]{0,3,2,1:T(2,128)(2,1)S(1)}, u32[]{:S(2)}, u32[]{:S(2)}) collective-permute-start(bf16[64,18,6,1]{0,3,2,1:T(2,128)(2,1)S(1)} %get-tuple-element.66), channel_id=1, source_target_pairs={{0,1},{1,2},{2,3},{3,4},{4,5},{5,6},{6,7},{7,8},{8,9},{9,10},{10,1... | collective-permute-start | bytes 41480 | tf_op jit(solution)/shard_map/ppermute | solution.py:19
  85.6 17.7 %collective-permute-start.11 = (bf16[64,18,6,1]{0,3,2,1:T(2,128)(2,1)S(1)}, bf16[64,18,6,1]{0,3,2,1:T(2,128)(2,1)S(1)}, u32[]{:S(2)}, u32[]{:S(2)}) collective-permute-start(bf16[64,18,6,1]{0,3,2,1:T(2,128)(2,1)S(1)} %get-tuple-element.67), channel_id=1, source_target_pairs={{1,0},{2,1},{3,2},{4,3},{5,4},{6,5},{7,6},{8,7},{9,8},{10,9},{11,1... | collective-permute-start | bytes 41480 | tf_op jit(solution)/shard_map/ppermute | solution.py:22
  103.3 2.3 copy-start.11
  106.2 15.4 %collective-permute-start.12 = (bf16[128,1,4,8]{0,3,2,1:T(8,128)(2,1)S(1)}, bf16[128,1,4,8]{0,3,2,1:T(8,128)(2,1)S(1)}, u32[]{:S(2)}, u32[]{:S(2)}) collective-permute-start(bf16[128,1,4,8]{0,3,2,1:T(8,128)(2,1)S(1)} %get-tuple-element.72), channel_id=1, source_target_pairs={{0,128},{1,129},{2,130},{3,131},{4,132},{5,133},{6,134},{7,135},{8... | collective-permute-start | bytes 24584 | tf_op jit(solution)/shard_map/ppermute | solution.py:19
  107.6 14.1 %collective-permute-start.13 = (bf16[128,1,4,8]{0,3,2,1:T(8,128)(2,1)S(1)}, bf16[128,1,4,8]{0,3,2,1:T(8,128)(2,1)S(1)}, u32[]{:S(2)}, u32[]{:S(2)}) collective-permute-start(bf16[128,1,4,8]{0,3,2,1:T(8,128)(2,1)S(1)} %get-tuple-element.73), channel_id=1, source_target_pairs={{128,0},{129,1},{130,2},{131,3},{132,4},{133,5},{134,6},{135,7},{1... | collective-permute-start | bytes 24584 | tf_op jit(solution)/shard_map/ppermute | solution.py:22
  113.2 73.1 %all-to-all-start.1 = ((bf16[8,2,128,1,4,8]{2,5,4,1,3,0:T(8,128)(2,1)}), bf16[8,2,128,1,4,8]{2,5,4,1,3,0:T(8,128)(2,1)}, u32[]{:S(2)}, u32[]{:S(2)}) async-start(bf16[8,2,128,1,4,8]{2,5,4,1,3,0:T(8,128)(2,1)} %copy.196), calls=%async_computation.1 | async-start | bytes 262144 | tf_op jit(solution)/shard_map/all_to_all | solution.py:43
  121.7 5.7 %collective-permute-start.14 = (bf16[128,18,1,8]{0,3,2,1:T(8,128)(2,1)S(1)}, bf16[128,18,1,8]{0,3,2,1:T(8,128)(2,1)S(1)}, u32[]{:S(2)}, u32[]{:S(2)}) collective-permute-start(bf16[128,18,1,8]{0,3,2,1:T(8,128)(2,1)S(1)} %get-tuple-element.68), channel_id=1, source_target_pairs={{0,16},{16,32},{32,48},{48,64},{64,80},{80,96},{96,112},{1,17},{17... | collective-permute-start | bytes 110600 | tf_op jit(solution)/shard_map/ppermute | solution.py:19
  126.0 7.9 %collective-permute-start.15 = (bf16[128,18,1,8]{0,3,2,1:T(8,128)(2,1)S(1)}, bf16[128,18,1,8]{0,3,2,1:T(8,128)(2,1)S(1)}, u32[]{:S(2)}, u32[]{:S(2)}) collective-permute-start(bf16[128,18,1,8]{0,3,2,1:T(8,128)(2,1)S(1)} %get-tuple-element.69), channel_id=1, source_target_pairs={{16,0},{32,16},{48,32},{64,48},{80,64},{96,80},{112,96},{17,1},{33... | collective-permute-start | bytes 110600 | tf_op jit(solution)/shard_map/ppermute | solution.py:22
  134.0 11.2 %collective-permute-start.16 = (bf16[128,18,6,1]{0,3,2,1:T(2,128)(2,1)S(1)}, bf16[128,18,6,1]{0,3,2,1:T(2,128)(2,1)S(1)}, u32[]{:S(2)}, u32[]{:S(2)}) collective-permute-start(bf16[128,18,6,1]{0,3,2,1:T(2,128)(2,1)S(1)} %get-tuple-element.64), channel_id=1, source_target_pairs={{0,1},{1,2},{2,3},{3,4},{4,5},{5,6},{6,7},{7,8},{8,9},{9,10},{10,1... | collective-permute-start | bytes 82952 | tf_op jit(solution)/shard_map/ppermute | solution.py:19
  139.3 5.9 %collective-permute-start.17 = (bf16[128,18,6,1]{0,3,2,1:T(2,128)(2,1)S(1)}, bf16[128,18,6,1]{0,3,2,1:T(2,128)(2,1)S(1)}, u32[]{:S(2)}, u32[]{:S(2)}) collective-permute-start(bf16[128,18,6,1]{0,3,2,1:T(2,128)(2,1)S(1)} %get-tuple-element.65), channel_id=1, source_target_pairs={{1,0},{2,1},{3,2},{4,3},{5,4},{6,5},{7,6},{8,7},{9,8},{10,9},{11,1... | collective-permute-start | bytes 82952 | tf_op jit(solution)/shard_map/ppermute | solution.py:22
  145.5 5.0 %copy-start.7 = (f32[32,8,8,3,64]{4,1,3,2,0:T(8,128)S(1)}, f32[32,8,8,3,64]{4,1,3,2,0:T(8,128)}, u32[]{:S(2)}) copy-start(f32[32,8,8,3,64]{4,1,3,2,0:T(8,128)} %copy.207) | copy-start | bytes 4718596
  149.1 1.3 copy-start.2
  149.2 2.6 copy-start.8
  151.8 24.1 %copy-start.9 = (bf16[3,3,3,64,128]{4,3,2,1,0:T(8,128)(2,1)S(1)}, bf16[3,3,3,64,128]{4,3,2,1,0:T(8,128)(2,1)}, u32[]{:S(2)}) copy-start(bf16[3,3,3,64,128]{4,3,2,1,0:T(8,128)(2,1)} %convolution_convert_fusion) | copy-start | bytes 1327108
  151.8 24.1 %copy-start.12 = (bf16[128]{0:T(256)(128)(2,1)S(1)}, bf16[128]{0:T(256)(128)(2,1)}, u32[]{:S(2)}) copy-start(bf16[128]{0:T(256)(128)(2,1)} %get-tuple-element.48) | copy-start | bytes 772
  151.8 24.1 %copy-start.13 = (bf16[64]{0:T(256)(128)(2,1)S(1)}, bf16[64]{0:T(256)(128)(2,1)}, u32[]{:S(2)}) copy-start(bf16[64]{0:T(256)(128)(2,1)} %get-tuple-element.50) | copy-start | bytes 388
  175.8 31.0 %copy-start.3 = (f32[64,16,2,4,2,8,2]{0,4,3,6,5,2,1:T(2,128)S(1)}, f32[64,16,2,4,2,8,2]{0,4,3,6,5,2,1:T(2,128)}, u32[]{:S(2)}) copy-start(f32[64,16,2,4,2,8,2]{0,4,3,6,5,2,1:T(2,128)} %copy-done.2) | copy-start | bytes 3145732
  175.8 31.0 %copy-start.15 = (f32[64]{0:T(128)S(1)}, f32[64]{0:T(128)}, u32[]{:S(2)}) copy-start(f32[64]{0:T(128)} %param.8) | copy-start | bytes 772
  186.3 62.9 %all-to-all-start.3 = ((bf16[256,2,640]{2,1,0:T(2,128)(2,1)}), bf16[256,2,640]{2,1,0:T(2,128)(2,1)S(1)}, u32[]{:S(2)}, u32[]{:S(2)}) async-start(bf16[256,2,640]{2,1,0:T(2,128)(2,1)} %reshape.135), calls=%async_computation.3 | async-start | bytes 1310720 | tf_op jit(solution)/shard_map/all_to_all | solution.py:60
  209.2 21.2 %copy-start.4 = (bf16[64,32,8,16]{0,2,3,1:T(8,128)(2,1)}, bf16[64,32,8,16]{0,2,3,1:T(8,128)(2,1)S(1)}, u32[]{:S(2)}) copy-start(bf16[64,32,8,16]{0,2,3,1:T(8,128)(2,1)S(1)} %multiply_convert_fusion) | copy-start | bytes 1572868
  209.3 4.6 %collective-permute-start.18 = (bf16[64,1,8,16]{0,2,3,1:T(8,128)(2,1)S(1)}, bf16[64,1,8,16]{0,2,3,1:T(8,128)(2,1)S(1)}, u32[]{:S(2)}, u32[]{:S(2)}) collective-permute-start(bf16[64,1,8,16]{0,2,3,1:T(8,128)(2,1)S(1)} %get-tuple-element.60), channel_id=1, source_target_pairs={{0,128},{1,129},{2,130},{3,131},{4,132},{5,133},{6,134},{7,135},{8... | collective-permute-start | bytes 49160 | tf_op jit(solution)/shard_map/ppermute | solution.py:19
  212.5 5.2 %collective-permute-start.19 = (bf16[64,1,8,16]{0,2,3,1:T(8,128)(2,1)S(1)}, bf16[64,1,8,16]{0,2,3,1:T(8,128)(2,1)S(1)}, u32[]{:S(2)}, u32[]{:S(2)}) collective-permute-start(bf16[64,1,8,16]{0,2,3,1:T(8,128)(2,1)S(1)} %get-tuple-element.61), channel_id=1, source_target_pairs={{128,0},{129,1},{130,2},{131,3},{132,4},{133,5},{134,6},{135,7},{1... | collective-permute-start | bytes 49160 | tf_op jit(solution)/shard_map/ppermute | solution.py:22
  218.2 9.2 %collective-permute-start.20 = (bf16[64,34,1,16]{0,2,3,1:T(2,128)(2,1)S(1)}, bf16[64,34,1,16]{0,2,3,1:T(2,128)(2,1)S(1)}, u32[]{:S(2)}, u32[]{:S(2)}) collective-permute-start(bf16[64,34,1,16]{0,2,3,1:T(2,128)(2,1)S(1)} %get-tuple-element.58), channel_id=1, source_target_pairs={{0,16},{16,32},{32,48},{48,64},{64,80},{80,96},{96,112},{1,17},{17... | collective-permute-start | bytes 208904 | tf_op jit(solution)/shard_map/ppermute | solution.py:19
  221.3 9.1 %collective-permute-start.21 = (bf16[64,34,1,16]{0,2,3,1:T(2,128)(2,1)S(1)}, bf16[64,34,1,16]{0,2,3,1:T(2,128)(2,1)S(1)}, u32[]{:S(2)}, u32[]{:S(2)}) collective-permute-start(bf16[64,34,1,16]{0,2,3,1:T(2,128)(2,1)S(1)} %get-tuple-element.59), channel_id=1, source_target_pairs={{16,0},{32,16},{48,32},{64,48},{80,64},{96,80},{112,96},{17,1},{33... | collective-permute-start | bytes 208904 | tf_op jit(solution)/shard_map/ppermute | solution.py:22
  230.6 9.1 %collective-permute-start.22 = (bf16[64,34,10,1]{0,2,3,1:T(8,128)(2,1)S(1)}, bf16[64,34,10,1]{0,2,3,1:T(8,128)(2,1)S(1)}, u32[]{:S(2)}, u32[]{:S(2)}) collective-permute-start(bf16[64,34,10,1]{0,2,3,1:T(8,128)(2,1)S(1)} %get-tuple-element.56), channel_id=1, source_target_pairs={{0,1},{1,2},{2,3},{3,4},{4,5},{5,6},{6,7},{7,8},{8,9},{9,10},{10,1... | collective-permute-start | bytes 130568 | tf_op jit(solution)/shard_map/ppermute | solution.py:19
  236.0 6.4 %collective-permute-start.23 = (bf16[64,34,10,1]{0,2,3,1:T(8,128)(2,1)S(1)}, bf16[64,34,10,1]{0,2,3,1:T(8,128)(2,1)S(1)}, u32[]{:S(2)}, u32[]{:S(2)}) collective-permute-start(bf16[64,34,10,1]{0,2,3,1:T(8,128)(2,1)S(1)} %get-tuple-element.57), channel_id=1, source_target_pairs={{1,0},{2,1},{3,2},{4,3},{5,4},{6,5},{7,6},{8,7},{9,8},{10,9},{11,1... | collective-permute-start | bytes 130568 | tf_op jit(solution)/shard_map/ppermute | solution.py:22
  247.7 18.7 %copy-start.17 = (bf16[3,3,3,32,64]{4,3,2,1,0:T(8,128)(2,1)S(1)}, bf16[3,3,3,32,64]{4,3,2,1,0:T(8,128)(2,1)}, u32[]{:S(2)}) copy-start(bf16[3,3,3,32,64]{4,3,2,1,0:T(8,128)(2,1)} %param.7) | copy-start | bytes 331780
  247.7 18.7 %copy-start.19 = (pred[8,3]{0,1:T(4,128)(4,1)S(1)}, pred[8,3]{0,1:T(4,128)(4,1)}, u32[]{:S(2)}) copy-start(pred[8,3]{0,1:T(4,128)(4,1)} %constant.32) | copy-start | bytes 76
  251.0 38.1 %all-to-all-start.4 = ((bf16[256,2,640]{2,1,0:T(2,128)(2,1)}), bf16[256,2,640]{2,1,0:T(2,128)(2,1)S(1)}, u32[]{:S(2)}, u32[]{:S(2)}) async-start(bf16[256,2,640]{2,1,0:T(2,128)(2,1)} %broadcast_in_dim.17), calls=%async_computation.4 | async-start | bytes 1310720 | tf_op jit(solution)/shard_map/all_to_all | solution.py:63

commit v2 on v0

v2 whole, which is shorter than its diff:
```python
import math

import jax
import jax.numpy as jnp
from jax import lax
from jax.experimental import pallas as pl
from jax.experimental.pallas import tpu as pltpu
from jax.sharding import Mesh
from jax.sharding import PartitionSpec as P

ALL = ("gx", "gy", "gz_0", "gz_1")
GZ = ("gz_0", "gz_1")
GX_GZ = ("gx", "gz_0", "gz_1")
BF16 = jnp.bfloat16
F32 = jnp.float32
TAPS = [(dx, dy) for dx in range(3) for dy in range(3)]


def call(body, outs, scratch, *args, flops=10**8):
    vmem = pl.BlockSpec(memory_space=pltpu.VMEM)
    smem = pl.BlockSpec(memory_space=pltpu.SMEM)
    return pl.pallas_call(
        body,
        out_shape=outs,
        in_specs=[smem if a.dtype == jnp.int32 else vmem for a in args],
        out_specs=jax.tree.map(lambda _: vmem, outs),
        scratch_shapes=scratch,
        compiler_params=pltpu.CompilerParams(vmem_limit_bytes=60 * 2**20),
        cost_estimate=pl.CostEstimate(flops=flops, bytes_accessed=10**6, transcendentals=0),
    )(*args)


def sds(*shape, dtype=BF16):
    return jax.ShapeDtypeStruct(shape, dtype)


def blocks(wa_ref, wb_ref):
    low = lax.broadcasted_iota(jnp.int32, (32, 128), 1) < 64
    zero_a = jnp.zeros((32, 128), BF16)
    zero_b = jnp.zeros((64, 128), BF16)

    def wa(dx, dy, dz):
        return wa_ref[(dx * 3 + dy) * 3 + dz] if 0 <= dz <= 2 else zero_a

    def wb(dx, dy, dz):
        return wb_ref[(dx * 3 + dy) * 3 + dz] if 0 <= dz <= 2 else zero_b

    def pair(first, second):
        return jnp.where(low, first.astype(F32), second.astype(F32)).astype(BF16)

    return wa, wb, pair, zero_b


def banded_ahead(wa_ref, wb_ref, a_ref, b_ref):
    wa, wb, pair, _ = blocks(wa_ref, wb_ref)
    for t, (dx, dy) in enumerate(TAPS):
        for zi in range(8):
            for p in range(2):
                a_ref[t * 256 + zi * 32 : t * 256 + zi * 32 + 32, p * 128 : p * 128 + 128] = pair(
                    wa(dx, dy, zi - 2 * p - 1), wa(dx, dy, zi - 2 * p - 2)
                )
        for zi in range(4):
            for zo in range(2):
                b_ref[t * 256 + zi * 64 : t * 256 + zi * 64 + 64, zo * 128 : zo * 128 + 128] = wb(dx, dy, zi - zo)


def banded_back(wa_ref, wb_ref, bt_ref, at_ref):
    wa, wb, pair, zero_b = blocks(wa_ref, wb_ref)
    for t, (dx, dy) in enumerate(TAPS):
        for z in range(4):
            for zi in range(4):
                dz = zi - z // 2
                block = wb(2 - dx, 2 - dy, 2 - dz) if 0 <= dz <= 2 else zero_b
                bt_ref[z * 64 : z * 64 + 64, t * 512 + zi * 128 : t * 512 + zi * 128 + 128] = block
        for z in range(8):
            for p in range(6):
                dz = 2 * p - z - 1
                at_ref[z * 32 : z * 32 + 32, t * 768 + p * 128 : t * 768 + p * 128 + 128] = pair(
                    wa(2 - dx, 2 - dy, 2 - dz), wa(2 - dx, 2 - dy, 1 - dz)
                )


def position(where_ref):
    code = where_ref[0]
    return code // 128, (code // 16) % 8, code % 16


def iota(shape, dim):
    return lax.broadcasted_iota(jnp.int32, shape, dim)


def sigmoid_of(value):
    return 0.5 * jnp.tanh(0.5 * value) + 0.5


def forward(
    where_ref, v_ref, ylo_ref, yhi_ref, zlo_ref, zhi_ref, a_ref, bias_a_ref, b_ref, bias_b_ref, cot_ref,
    feat_ref, grad_ref, sum_ref, px_ref, vo_ref, slope_ref,
    f_ref, vx_ref, s_ref, p_ref,
):
    gx, gy, gz = position(where_ref)

    def stage(src, rows, y0, q0, nq):
        def step(y, carry):
            f_ref[0:nq, 0:40, :] = src[y].astype(F32)
            for dx in range(3):
                vx_ref[dx, y0 + y, q0 : q0 + nq] = f_ref[0:nq, pl.ds(dx, 48), :].astype(BF16)

            @pl.when(jnp.logical_and(y0 + y >= 2, y0 + y < 12))
            def _():
                for dx in range(3):
                    vo_ref[dx, y0 + y - 2, q0 : q0 + nq] = f_ref[0:nq, pl.ds(dx + 2, 32), :].astype(BF16)

            return carry

        lax.fori_loop(0, rows, step, 0)

    stage(ylo_ref, 3, 0, 1, 4)
    stage(v_ref, 8, 3, 1, 4)
    stage(yhi_ref, 3, 11, 1, 4)
    stage(zlo_ref, 14, 0, 0, 1)
    stage(zhi_ref, 14, 0, 5, 1)

    fold = iota((6, 48, 128), 2) < 64
    shape = (6, 24, 128)
    x = iota(shape, 1) + (gx * 16 - 1)
    y = iota(shape, 0) + (gy * 4 - 1)
    zlane = iota(shape, 2) // 64
    inside_xy = (x >= 0) & (x < 32) & (y >= 0) & (y < 32)

    def conv_a(q, carry):
        parts = []
        for dx, dy in TAPS:
            parts.append(vx_ref[dx, dy : dy + 12, q])
            parts.append(vx_ref[dx, dy : dy + 12, q + 1])
        lhs = jnp.concatenate(parts, axis=-1).reshape(576, 2304)
        before = jnp.dot(lhs, a_ref[...], preferred_element_type=F32) + bias_a_ref[...]
        s = sigmoid_of(before)
        slope_ref[q] = (0.125 * (s * (1.0 + before * (1.0 - s)))).astype(BF16).reshape(12, 48, 256)
        act = (before * s).reshape(6, 2, 48, 256)
        rows = act[:, 0] + act[:, 1]
        lo, hi = rows[..., :128], rows[..., 128:]
        lo = lo + pltpu.roll(lo, 64, 2)
        hi = hi + pltpu.roll(hi, 64, 2)
        s_ref[...] = jnp.where(fold, lo, hi)
        mean = (s_ref[:, pl.ds(0, 24, stride=2), :] + s_ref[:, pl.ds(1, 24, stride=2), :]) * 0.125
        z = zlane + (gz * 8 - 1 + 2 * q)
        p_ref[...] = jnp.where(inside_xy & (z >= 0) & (z < 128), mean, 0.0)
        for dx in range(3):
            px_ref[dx, :, q] = p_ref[:, pl.ds(dx, 16), :].astype(BF16)
        return carry

    lax.fori_loop(0, 5, conv_a, 0)

    parts = []
    for dx, dy in TAPS:
        parts.append(px_ref[dx, dy : dy + 4, 0:4])
        parts.append(px_ref[dx, dy : dy + 4, 1:5])
    lhs = jnp.concatenate(parts, axis=-1).reshape(256, 2304)
    before = jnp.dot(lhs, b_ref[...], preferred_element_type=F32) + bias_b_ref[...]
    s = sigmoid_of(before)
    feat_ref[...] = (before * s).astype(BF16).reshape(4, 4, 16, 256)
    cot = cot_ref[...].reshape(256, 256).astype(F32)
    grad = (cot * (s * (1.0 + before * (1.0 - s)))).astype(BF16)
    grad_ref[...] = grad.reshape(4, 4, 16, 256)
    total = jnp.sum(grad.astype(F32), axis=0, keepdims=True)
    sum_ref[...] = total[:, :128] + total[:, 128:]


TN = (((0,), (0,)), ((), ()))
NT = (((1,), (1,)), ((), ()))


def weight_b_terms(px_ref, grad_ref, out_ref):
    grad = grad_ref[...].reshape(256, 256)
    for t, (dx, dy) in enumerate(TAPS):
        cells = jnp.concatenate([px_ref[dx, dy : dy + 4, 0:4], px_ref[dx, dy : dy + 4, 1:5]], axis=-1)
        terms = lax.dot_general(cells.reshape(256, 256), grad, TN, preferred_element_type=F32)
        for dz in range(3):
            out_ref[3 * t + dz] = (
                terms[dz * 64 : dz * 64 + 64, :128] + terms[dz * 64 + 64 : dz * 64 + 128, 128:]
            ).astype(BF16)


def backward(
    where_ref, g_ref, ylo_ref, yhi_ref, zlo_ref, zhi_ref, bt_ref, slope_ref, vo_ref, wb_ref, sum_b_ref,
    ga_ref, flat_ref,
    f_ref, gx_ref, s_ref, t_ref, own_ref,
):
    gx, gy, gz = position(where_ref)

    def stage(src, rows, y0, q0, nq):
        def step(y, carry):
            for h in range(2):
                f_ref[h, 0:nq, 0:24, :] = src[y, :, :, h * 128 : h * 128 + 128].astype(F32)
                for dx in range(3):
                    gx_ref[dx, y0 + y, q0 : q0 + nq, :, h * 128 : h * 128 + 128] = f_ref[
                        h, 0:nq, pl.ds(dx, 32), :
                    ].astype(BF16)
            return carry

        lax.fori_loop(0, rows, step, 0)

    stage(ylo_ref, 2, 0, 1, 4)
    stage(g_ref, 4, 2, 1, 4)
    stage(yhi_ref, 2, 6, 1, 4)
    stage(zlo_ref, 8, 0, 0, 1)
    stage(zhi_ref, 8, 0, 5, 1)

    shape = (12, 48, 128)
    x = iota(shape, 1) + (gx * 32 - 2)
    y = iota(shape, 0) + (gy * 8 - 2)
    zlane = iota(shape, 2) // 64
    inside_xy = (x >= 0) & (x < 64) & (y >= 0) & (y < 64)

    def conv_b(q, total):
        parts = []
        for dx, dy in TAPS:
            parts.append(gx_ref[dx, dy : dy + 6, q])
            parts.append(gx_ref[dx, dy : dy + 6, q + 1])
        lhs = jnp.concatenate(parts, axis=-1).reshape(192, 4608)
        pooled = lax.dot_general(lhs, bt_ref[...], NT, preferred_element_type=F32)
        pooled = pooled.astype(BF16).astype(F32).reshape(6, 32, 256)[:, :24]
        sums = []
        for h in range(2):
            half = pooled[..., h * 128 : h * 128 + 128]
            s_ref[:, pl.ds(0, 24, stride=2), :] = half
            s_ref[:, pl.ds(1, 24, stride=2), :] = half
            spread = jnp.broadcast_to(s_ref[...].reshape(6, 1, 48, 128), (6, 2, 48, 128)).reshape(12, 48, 128)
            z = zlane + (gz * 16 - 2 + 4 * q + 2 * h)
            slope = slope_ref[q, :, :, h * 128 : h * 128 + 128].astype(F32)
            t_ref[...] = jnp.where(inside_xy & (z >= 0) & (z < 256), spread * slope, 0.0)
            for dx in range(3):
                ga_ref[dx, :, q, :, h * 128 : h * 128 + 128] = t_ref[1:11, pl.ds(dx + 1, 32), :].astype(BF16)
            keep = jnp.where(q == 4 * h, 0.0, 1.0)
            own = (t_ref[2:10, pl.ds(2, 32), :] * keep).astype(BF16)
            own_ref[:, q, :, h * 128 : h * 128 + 128] = own
            sums.append(jnp.sum(own.astype(F32).reshape(256, 128), axis=0, keepdims=True))
        return total + sums[0] + sums[1]

    total = lax.fori_loop(0, 5, conv_b, jnp.zeros((1, 128), F32))
    flat_ref[0:1728] = wb_ref[...].reshape(1728, 128)
    row = iota((16, 128), 0)
    sums = jnp.where(row == 0, sum_b_ref[...], jnp.where(row == 1, total + pltpu.roll(total, 64, 1), 0.0))
    flat_ref[2304:2320] = sums.astype(BF16)
    flat_ref[2320:2560] = jnp.zeros((240, 128), BF16)

    flat = own_ref[...].reshape(1280, 256).T
    for t, (dx, dy) in enumerate(TAPS):
        cells = jnp.concatenate([vo_ref[dx, dy : dy + 8, 0:5], vo_ref[dx, dy : dy + 8, 1:6]], axis=-1)
        terms = jnp.dot(flat, cells.reshape(1280, 256), preferred_element_type=F32)
        block = terms[0:64]
        for zo in range(1, 4):
            block = block + pltpu.roll(terms[zo * 64 : zo * 64 + 64], 256 - 32 * zo, 1)
        flat_ref[1728 + 64 * t : 1792 + 64 * t] = block[:, :128].astype(BF16)


def input_grad(ga_ref, at_ref, out_ref):
    for h in range(2):
        parts = []
        for dx, dy in TAPS:
            for j in range(3):
                parts.append(ga_ref[dx, dy : dy + 8, 2 * h + j])
        lhs = jnp.concatenate(parts, axis=-1).reshape(256, 6912)
        value = lax.dot_general(lhs, at_ref[...], NT, preferred_element_type=F32)
        out_ref[:, h] = value.astype(BF16).reshape(8, 32, 256)


def ends(axis):
    count = lax.axis_size(axis)
    up = [(i, i + 1) for i in range(count - 1)]
    return up, [(b, a) for a, b in up]


def swap_sides(block, width, rows):
    first = lax.axis_index("gx") == 0
    length = block.shape[2]
    face = jnp.where(first, block[:, :, length - width :], block[:, :, :width])
    got = lax.ppermute(face, "gx", [(0, 1), (1, 0)])
    none = jnp.zeros_like(got)
    rest = jnp.zeros(block.shape[:2] + (rows - length - 2 * width,) + block.shape[3:], block.dtype)
    return jnp.concatenate([jnp.where(first, none, got), block, jnp.where(first, got, none), rest], axis=2)


def halo(block, width, x_rows):
    wide = swap_sides(block, width, x_rows)
    up, down = ends("gy")
    ylo = lax.ppermute(wide[wide.shape[0] - width :], "gy", up)
    yhi = lax.ppermute(wide[:width], "gy", down)
    up, down = ends(GZ)
    last = jnp.concatenate([ylo[:, 3:], wide[:, 3:], yhi[:, 3:]], axis=0)
    head = jnp.concatenate([ylo[:, :1], wide[:, :1], yhi[:, :1]], axis=0)
    zlo = lax.ppermute(last, GZ, up)
    zhi = lax.ppermute(head, GZ, down)
    return wide, ylo, yhi, zlo, zhi


def on_device(volume, weight_a, bias_a, weight_b, bias_b, cotangent):
    cells_fine = 64 * 64 * 256
    scale_a = 1.0 / math.sqrt(cells_fine)
    scale_b = 1.0 / math.sqrt(cells_fine // 8)
    where = lax.axis_index(ALL).astype(jnp.int32).reshape(1)

    v = jnp.transpose(volume.reshape(32, 32, 8, 4, 4), (2, 3, 1, 4, 0)).reshape(8, 4, 32, 128)
    sides = halo(v, 3, 40)

    cot = jnp.transpose(cotangent[:, 0], (2, 1, 0)).reshape(16, 8, 4, 128)
    cot = lax.all_to_all(cot, GZ, 0, 0, tiled=True)
    cot = jnp.transpose(cot.reshape(16, 4, 2, 4, 128), (3, 1, 0, 2, 4)).reshape(4, 4, 16, 256)

    wa27 = weight_a.reshape(27, 32, 64)
    wa27 = jnp.concatenate([wa27, wa27], axis=-1)
    wb27 = weight_b.reshape(27, 64, 128)
    m_a, m_b = call(banded_ahead, (sds(2304, 256), sds(2304, 256)), [], wa27, wb27, flops=10**7)
    m_bt, m_at = call(banded_back, (sds(256, 4608), sds(256, 6912)), [], wa27, wb27, flops=10**7)

    feat, grad_b, sum_b, px, vo, slope = call(
        forward,
        (
            sds(4, 4, 16, 256), sds(4, 4, 16, 256), sds(1, 128, dtype=F32),
            sds(3, 6, 5, 16, 128), sds(3, 10, 6, 32, 128), sds(5, 12, 48, 256),
        ),
        [
            pltpu.VMEM((4, 56, 128), F32), pltpu.VMEM((3, 14, 6, 48, 128), BF16),
            pltpu.VMEM((6, 48, 128), F32), pltpu.VMEM((6, 24, 128), F32),
        ],
        where, *sides, m_a, jnp.tile(bias_a, 4).reshape(1, 256), m_b, jnp.tile(bias_b, 2).reshape(1, 256), cot,
        flops=2 * 10**9,
    )

    sides_b = halo(grad_b, 2, 24)
    wb = call(weight_b_terms, sds(27, 64, 128), [], px, grad_b, flops=10**9)

    out = jnp.transpose(feat.reshape(4, 4, 16, 2, 128), (2, 1, 3, 0, 4)).reshape(16, 8, 4, 128)
    out = lax.all_to_all(out, GZ, 0, 0, tiled=True).reshape(128, 4, 128)

    ga, flat = call(
        backward,
        (sds(3, 10, 5, 32, 256), sds(2560, 128)),
        [
            pltpu.VMEM((2, 4, 40, 128), F32), pltpu.VMEM((3, 8, 6, 32, 256), BF16),
            pltpu.VMEM((6, 48, 128), F32), pltpu.VMEM((12, 48, 128), F32), pltpu.VMEM((8, 5, 32, 256), BF16),
        ],
        where, *sides_b, m_bt, slope, vo, wb, sum_b, flops=2 * 10**9,
    )

    shares = lax.all_to_all(flat.reshape(256, 5, 2, 128), ALL, 0, 0, tiled=True)
    share = jnp.sum(shares.astype(F32), axis=0).astype(BF16)
    share, out = lax.optimization_barrier((share, out))
    spread = jnp.broadcast_to(share[None], (256, 5, 2, 128))
    total = lax.all_to_all(spread, ALL, 0, 0, tiled=True).reshape(2560, 128).astype(F32)
    features = jnp.transpose(out, (2, 1, 0)).reshape(128, 1, 4, 128)

    gi = call(input_grad, sds(8, 2, 32, 256), [], ga, m_at, flops=2 * 10**9)
    gi = jnp.transpose(gi.reshape(8, 2, 32, 8, 32), (4, 2, 0, 1, 3)).reshape(32, 32, 8, 16)

    total_wb = total[:1728].reshape(3, 3, 3, 64, 128) * scale_b
    total_wa = jnp.transpose(total[1728:2304].reshape(9, 64, 4, 32)[:, :, 1:], (0, 2, 3, 1)) * scale_a
    return (
        features,
        gi,
        total_wa.reshape(3, 3, 3, 32, 64),
        total[2305, :64] * scale_a,
        total_wb,
        total[2304] * scale_b,
    )


def solution(mesh):
    finer = Mesh(
        mesh.devices.reshape(mesh.shape["gx"], mesh.shape["gy"], 8, 2), ("gx", "gy", "gz_0", "gz_1")
    )
    return jax.shard_map(
        on_device,
        mesh=finer,
        in_specs=(P(None, "gx", "gy", GZ), P(), P(), P(), P(), P(None, GX_GZ, "gy", None)),
        out_specs=(P(None, GX_GZ, "gy", None), P(None, "gx", "gy", GZ), P(), P(), P(), P()),
        check_vma=False,
    )
```

time: 512 us -> 175 us (0.34); the launches traced: 506 us -> 174 us
  waiting for transfers between devices: 277 us -> 41.1 us
  matrix products: 53.1 us -> 0 us
  Pallas kernels: 0 us -> 36.8 us
  local copies, waits for them, and re-layouts: 51.9 us -> 16 us
  other arithmetic: 22 us -> 5.92 us
  between operations: 15.1 us -> 1.05 us
  starting transfers between devices: 82.7 us -> 73.6 us
    psum x1 -> x0, waiting for transfers between devices: 243 us -> none  [together(): total = lax.psum(jnp.concatenate([a.ravel() for a in arrays]), axis)]
    ppermute x24 -> x10, starting transfers between devices: 66.9 us -> 27.5 us  [the longest x2 9.93 us: halo(): zlo = lax.ppermute(last, GZ, up)]
    pallas_call x0 -> x6, Pallas kernels: none -> 36.8 us  [call(): pl.pallas_call(body, out_shape=outs, in_specs=[smem if a.dtype == jnp.int...]
    all_to_all x2 -> x4, starting transfers between devices: 15.8 us -> 46.1 us  [the longest x1 20.8 us: on_device(): shares = lax.all_to_all(flat.reshape(256, 5, 2, 128), ALL, 0, 0, tiled=True)]
    all_to_all x2 -> x4, waiting for transfers between devices: 5.73 us -> 34.9 us  [the longest x1 22.7 us: on_device(): shares = lax.all_to_all(flat.reshape(256, 5, 2, 128), ALL, 0, 0, tiled=True)]
    transpose x2 -> x0, matrix products: 28.6 us -> none  [weight_terms(): return jnp.transpose(result, (2, 3, 4, 0, 1))]
    conv_general_dilated x4 -> x0, matrix products: 24.5 us -> none  [conv_valid(): lax.conv_general_dilated(padded[None], weight, (1, 1, 1), 'VALID', dimens...]
    ppermute x24 -> x10, waiting for transfers between devices: 28.1 us -> 6.22 us  [the longest x2 2.55 us: halo(): ylo = lax.ppermute(wide[wide.shape[0] - width:], 'gy', up)]
  transfers between devices with their start and end apart: 27 -> 14, of which waited for: 11 -> 6; matrix products, arithmetic and copies ran while one was open for 18% -> 6% of each run, Pallas kernels for 0% -> 15%
where the time goes in v2:
time: 175 us; the launch traced here: 174 us
  starting transfers between devices  73.6 us (42%)
  waiting for transfers between devices  41.1 us (23%)
  Pallas kernels  36.8 us (21%)
  local copies, waits for them, and re-layouts  16 us (9%)
  other arithmetic  5.92 us (3%)
    pallas_call x6, Pallas kernels, call(): pl.pallas_call(body, out_shape=outs, in_specs=[smem if a.dtype == jnp.int...  36.8 us
    all_to_all x1, waiting for transfers between devices, on_device(): shares = lax.all_to_all(flat.reshape(256, 5, 2, 128), ALL, 0, 0, tiled=True)  22.7 us
    all_to_all x1, starting transfers between devices, on_device(): shares = lax.all_to_all(flat.reshape(256, 5, 2, 128), ALL, 0, 0, tiled=True)  20.8 us
    all_to_all x1, waiting for transfers between devices, on_device(): lax.all_to_all(spread, ALL, 0, 0, tiled=True).reshape(2560, 128).astype(F32)  12.2 us
    ppermute x2, starting transfers between devices, halo(): zlo = lax.ppermute(last, GZ, up)  9.93 us
    all_to_all x1, starting transfers between devices, on_device(): out = lax.all_to_all(out, GZ, 0, 0, tiled=True).reshape(128, 4, 128)  9.77 us
    all_to_all x1, starting transfers between devices, on_device(): cot = lax.all_to_all(cot, GZ, 0, 0, tiled=True)  9.56 us
    ppermute x2, starting transfers between devices, halo(): ylo = lax.ppermute(wide[wide.shape[0] - width:], 'gy', up)  8.71 us
  transfers between devices with their start and end apart: 14, of which 6 were waited for; matrix products, arithmetic and copies ran while one was open for 6% of the time, Pallas kernels for 15%

profile of v2, /device:TPU:1, one launch (start us, length us, event | category | flops | bytes accessed | tf_op | source)
XLA Modules:
  0.0 174.5 jit_solution(10699719804713044533)
XLA Ops:
  0.6 3.1 %copy.35 = bf16[32,32,8,4,4]{0,4,1,3,2:T(4,128)(2,1)S(1)} copy(bf16[32,32,8,4,4]{1,4,3,2,0:T(4,128)(2,1)} %bitcast.48) | data formatting | bytes 524288 | tf_op jit(solution)/shard_map/reshape | solution.py:304
  3.7 0.5 reshape.78
  4.3 2.1 %collective-permute-start = (bf16[8,4,3,128]{3,2,1,0:T(4,128)(2,1)S(1)}, bf16[8,4,3,128]{3,2,1,0:T(4,128)(2,1)S(1)}, u32[]{:S(2)}, u32[]{:S(2)}) collective-permute-start(bf16[8,4,3,128]{3,2,1,0:T(4,128)(2,1)S(1)} %slice_select_fusion), channel_id=1, source_target_pairs={{0,128},{128,0},{1,129},{129,1},{2,130},{130,2},{3,131},{131,3},{4... | collective-permute-start | bytes 73736 | tf_op jit(solution)/shard_map/ppermute | solution.py:279
  6.6 0.7 copy.37
  7.2 9.6 %all-to-all-start = ((bf16[16,8,4,128]{3,1,2,0:T(8,128)(2,1)}), bf16[16,8,4,128]{3,1,2,0:T(8,128)(2,1)S(1)}, u32[]{:S(2)}, u32[]{:S(2)}) async-start(bf16[16,8,4,128]{3,1,2,0:T(8,128)(2,1)} %copy.37), calls=%async_computation | async-start | bytes 262144 | tf_op jit(solution)/shard_map/all_to_all | solution.py:308
  16.9 0.2 maximum_maximum_fusion.v_ref
  17.2 1.3 collective-permute-start.2
  18.5 4.0 %collective-permute-start.1 = (bf16[3,4,40,128]{3,2,1,0:T(8,128)(2,1)S(1)}, bf16[3,4,40,128]{3,2,1,0:T(8,128)(2,1)S(1)}, u32[]{:S(2)}, u32[]{:S(2)}) collective-permute-start(bf16[3,4,40,128]{3,2,1,0:T(8,128)(2,1)S(1)} %get-tuple-element.55), channel_id=1, source_target_pairs={{0,16},{16,32},{32,48},{48,64},{64,80},{80,96},{96,112},{1,17},{17... | collective-permute-start | bytes 368648 | tf_op jit(solution)/shard_map/ppermute | solution.py:288
  22.5 1.3 collective-permute-done.2.yhi_ref
  23.9 0.9 collective-permute-done.1.ylo_ref
  24.8 4.4 %collective-permute-start.3 = (bf16[14,1,40,128]{3,2,1,0:T(8,128)(2,1)S(1)}, bf16[14,1,40,128]{3,2,1,0:T(8,128)(2,1)S(1)}, u32[]{:S(2)}, u32[]{:S(2)}) collective-permute-start(bf16[14,1,40,128]{3,2,1,0:T(8,128)(2,1)S(1)} %pad_maximum_fusion.1), channel_id=1, source_target_pairs={{0,1},{1,2},{2,3},{3,4},{4,5},{5,6},{6,7},{7,8},{8,9},{9,10},{10,1... | collective-permute-start | bytes 430088 | tf_op jit(solution)/shard_map/ppermute | solution.py:293
  29.2 1.9 %collective-permute-start.4 = (bf16[14,1,40,128]{3,2,1,0:T(8,128)(2,1)S(1)}, bf16[14,1,40,128]{3,2,1,0:T(8,128)(2,1)S(1)}, u32[]{:S(2)}, u32[]{:S(2)}) collective-permute-start(bf16[14,1,40,128]{3,2,1,0:T(8,128)(2,1)S(1)} %pad_maximum_fusion.2), channel_id=1, source_target_pairs={{1,0},{2,1},{3,2},{4,3},{5,4},{6,5},{7,6},{8,7},{9,8},{10,9},{11,1... | collective-permute-start | bytes 430088 | tf_op jit(solution)/shard_map/ppermute | solution.py:294
  31.2 0.7 reshape_tile.6.bias_a_ref
  31.9 0.8 pad_maximum_fusion.wa_ref
  32.7 2.8 %shard_map.109 = (bf16[2304,256]{1,0:T(8,128)(2,1)}, bf16[2304,256]{1,0:T(8,128)(2,1)}) custom-call(bf16[27,32,128]{2,1,0:T(8,128)(2,1)} %pad_maximum_fusion.wa_ref, bf16[27,64,128]{2,1,0:T(8,128)(2,1)} %bitcast.46), custom_call_target="tpu_custom_call" | custom-call | flops 10000000 | bytes 1000000 | tf_op jit(solution)/shard_map/pallas_call | solution.py:22
  35.7 0.7 reshape.83.cot_ref
  36.5 0.7 tile.5
  37.2 10.0 %shard_map.110 = (bf16[4,4,16,256]{3,2,1,0:T(8,128)(2,1)}, bf16[4,4,16,256]{3,2,1,0:T(8,128)(2,1)}, f32[1,128]{1,0:T(1,128)}, bf16[3,6,5,16,128]{4,3,2,1,0:T(8,1...) custom-call(s32[1]{0:T(128)} %bitcast.where_ref, bf16[8,4,40,128]{3,2,1,0:T(8,128)(2,1)} %copy-done, ...), custom_call_target="tpu_custom_call" | custom-call | flops 2000000000 | bytes 1000000 | tf_op jit(solution)/shard_map/pallas_call | solution.py:22
  47.3 0.9 broadcast_select_fusion.4
  48.2 0.3 collective-permute-start.5
  48.6 2.3 %collective-permute-done.5 = bf16[4,4,2,256]{3,2,1,0:T(2,128)(2,1)S(1)} collective-permute-done((bf16[4,4,2,256]{3,2,1,0:T(2,128)(2,1)S(1)}, bf16[4,4,2,256]{3,2,1,0:T(2,128)(2,1)S(1)}, u32[]{:S(2)}, u32[]{:S(2)}) %collective-permute-start.5) | collective-permute-done | bytes 16416 | tf_op jit(solution)/shard_map/ppermute | solution.py:279
  50.9 1.0 maximum_maximum_fusion.1.g_ref
  52.0 1.3 collective-permute-start.7
  53.3 4.7 %collective-permute-start.6 = (bf16[2,4,24,256]{3,2,1,0:T(8,128)(2,1)S(1)}, bf16[2,4,24,256]{3,2,1,0:T(8,128)(2,1)S(1)}, u32[]{:S(2)}, u32[]{:S(2)}) collective-permute-start(bf16[2,4,24,256]{3,2,1,0:T(8,128)(2,1)S(1)} %get-tuple-element.59), channel_id=1, source_target_pairs={{0,16},{16,32},{32,48},{48,64},{64,80},{80,96},{96,112},{1,17},{17... | collective-permute-start | bytes 294920 | tf_op jit(solution)/shard_map/ppermute | solution.py:288
  58.1 1.7 collective-permute-done.6.ylo_ref
  59.8 5.5 %collective-permute-start.8 = (bf16[8,1,24,256]{3,2,1,0:T(8,128)(2,1)S(1)}, bf16[8,1,24,256]{3,2,1,0:T(8,128)(2,1)S(1)}, u32[]{:S(2)}, u32[]{:S(2)}) collective-permute-start(bf16[8,1,24,256]{3,2,1,0:T(8,128)(2,1)S(1)} %pad_maximum_fusion.3), channel_id=1, source_target_pairs={{0,1},{1,2},{2,3},{3,4},{4,5},{5,6},{6,7},{7,8},{8,9},{9,10},{10,1... | collective-permute-start | bytes 294920 | tf_op jit(solution)/shard_map/ppermute | solution.py:293
  65.3 1.9 %collective-permute-start.9 = (bf16[8,1,24,256]{3,2,1,0:T(8,128)(2,1)S(1)}, bf16[8,1,24,256]{3,2,1,0:T(8,128)(2,1)S(1)}, u32[]{:S(2)}, u32[]{:S(2)}) collective-permute-start(bf16[8,1,24,256]{3,2,1,0:T(8,128)(2,1)S(1)} %pad_maximum_fusion.4), channel_id=1, source_target_pairs={{1,0},{2,1},{3,2},{4,3},{5,4},{6,5},{7,6},{8,7},{9,8},{10,9},{11,1... | collective-permute-start | bytes 294920 | tf_op jit(solution)/shard_map/ppermute | solution.py:294
  67.3 4.3 %shard_map.111 = (bf16[256,4608]{1,0:T(8,128)(2,1)}, bf16[256,6912]{1,0:T(8,128)(2,1)}) custom-call(bf16[27,32,128]{2,1,0:T(8,128)(2,1)} %pad_maximum_fusion.wa_ref, bf16[27,64,128]{2,1,0:T(8,128)(2,1)} %bitcast.47), custom_call_target="tpu_custom_call" | custom-call | flops 10000000 | bytes 1000000 | tf_op jit(solution)/shard_map/pallas_call | solution.py:22
  71.7 0.7 copy.41
  72.4 9.8 %all-to-all-start.2 = ((bf16[16,8,4,128]{3,2,1,0:T(4,128)(2,1)}), bf16[16,8,4,128]{3,2,1,0:T(4,128)(2,1)S(1)}, u32[]{:S(2)}, u32[]{:S(2)}) async-start(bf16[16,8,4,128]{3,2,1,0:T(4,128)(2,1)} %copy.41), calls=%async_computation.2 | async-start | bytes 262144 | tf_op jit(solution)/shard_map/all_to_all | solution.py:335
  82.2 2.3 %shard_map.112.wb_ref = bf16[27,64,128]{2,1,0:T(8,128)(2,1)} custom-call(bf16[3,6,5,16,128]{4,3,2,1,0:T(8,128)(2,1)} %get-tuple-element.26.px_ref, bf16[4,4,16,256]{3,2,1,0:T(8,128)(2,1)} %get-tuple-element.22.grad_ref), custom_call_target="tpu_custom_call" | custom-call | flops 1000000000 | bytes 1000000 | tf_op jit(solution)/shard_map/pallas_call | solution.py:22
  84.5 0.6 copy-done.12
  85.2 11.8 %shard_map.113 = (bf16[3,10,5,32,256]{4,3,2,1,0:T(8,128)(2,1)}, bf16[2560,128]{1,0:T(8,128)(2,1)}) custom-call(s32[1]{0:T(128)} %bitcast.where_ref, bf16[4,4,24,256]{3,2,1,0:T(8,128)(2,1)} %copy-done.1, bf16[2,4,24,256]{3,2,1,0:T(8,128)(2,1)} %copy-done.8, bf16[2,4,24,256]{3,2,1,0:T(8,128)(2,1)} %copy-done.7, bf16[8,1,24,256]{3,2,1,0:T(8,128)(2,1)} %copy-done.12, ...), custom_call_target="tpu_custom_call" | custom-call | flops 2000000000 | bytes 1000000 | tf_op jit(solution)/shard_map/pallas_call | solution.py:22
  97.0 20.8 %all-to-all-start.1 = ((bf16[256,5,2,128]{3,2,1,0:T(2,128)(2,1)}), bf16[256,5,2,128]{3,2,1,0:T(2,128)(2,1)S(1)}, u32[]{:S(2)}, u32[]{:S(2)}) async-start(bf16[256,5,2,128]{3,2,1,0:T(2,128)(2,1)} %bitcast.51), calls=%async_computation.1 | async-start | bytes 1310720 | tf_op jit(solution)/shard_map/all_to_all | solution.py:347
  117.8 22.7 %all-to-all-done.1 = bf16[256,5,2,128]{3,2,1,0:T(2,128)(2,1)S(1)} async-done(((bf16[256,5,2,128]{3,2,1,0:T(2,128)(2,1)}), bf16[256,5,2,128]{3,2,1,0:T(2,128)(2,1)S(1)}, u32[]{:S(2)}, u32[]{:S(2)}) %all-to-all-start.1) | async-done | bytes 655392 | tf_op jit(solution)/shard_map/all_to_all | solution.py:347
  140.5 0.6 reduce_sum.12
  141.2 1.2 broadcast_in_dim.22
  142.3 6.0 %all-to-all-start.3 = ((bf16[256,5,2,128]{3,2,1,0:T(2,128)(2,1)}), bf16[256,5,2,128]{3,2,1,0:T(2,128)(2,1)S(1)}, u32[]{:S(2)}, u32[]{:S(2)}) async-start(bf16[256,5,2,128]{3,2,1,0:T(2,128)(2,1)} %broadcast_in_dim.22), calls=%async_computation.3 | async-start | bytes 1310720 | tf_op jit(solution)/shard_map/all_to_all | solution.py:351
  148.3 5.5 %shard_map.114 = bf16[8,2,32,256]{3,2,1,0:T(8,128)(2,1)} custom-call(bf16[3,10,5,32,256]{4,3,2,1,0:T(8,128)(2,1)} %get-tuple-element.31.ga_ref, bf16[256,6912]{1,0:T(8,128)(2,1)} %get-tuple-element.32.at_ref), custom_call_target="tpu_custom_call" | custom-call | flops 2000000000 | bytes 1000000 | tf_op jit(solution)/shard_map/pallas_call | solution.py:22
  153.8 1.7 reshape.89
  155.4 2.6 %copy.43 = bf16[32,32,8,2,8]{1,4,3,2,0:T(8,128)(2,1)} copy(bf16[32,32,8,2,8]{0,4,1,3,2:T(8,128)(2,1)S(1)} %bitcast.42) | data formatting | bytes 524288 | tf_op jit(solution)/shard_map/transpose | solution.py:355
  158.1 0.8 copy.46
  158.9 12.2 %all-to-all-done.3 = bf16[256,5,2,128]{3,2,1,0:T(2,128)(2,1)S(1)} async-done(((bf16[256,5,2,128]{3,2,1,0:T(2,128)(2,1)}), bf16[256,5,2,128]{3,2,1,0:T(2,128)(2,1)S(1)}, u32[]{:S(2)}, u32[]{:S(2)}) %all-to-all-start.3) | async-done | bytes 655392 | tf_op jit(solution)/shard_map/all_to_all | solution.py:351
  171.2 0.5 fusion.2
  171.7 0.5 fusion.1
  172.2 1.0 slice_multiply_fusion
  173.3 0.2 reshape.91
  173.6 0.9 copy.45
  (67 shorter events, 1.3 us)
Async XLA Ops:
  0.6 5.8 %copy-start.3 = (bf16[128,1,4,128]{3,2,1,0:T(4,128)(2,1)S(1)}, bf16[128,1,4,128]{3,2,1,0:T(4,128)(2,1)}, u32[]{:S(2)}) copy-start(bf16[128,1,4,128]{3,2,1,0:T(4,128)(2,1)} %param.11) | copy-start | bytes 393220
  4.3 12.6 %collective-permute-start = (bf16[8,4,3,128]{3,2,1,0:T(4,128)(2,1)S(1)}, bf16[8,4,3,128]{3,2,1,0:T(4,128)(2,1)S(1)}, u32[]{:S(2)}, u32[]{:S(2)}) collective-permute-start(bf16[8,4,3,128]{3,2,1,0:T(4,128)(2,1)S(1)} %slice_select_fusion), channel_id=1, source_target_pairs={{0,128},{128,0},{1,129},{129,1},{2,130},{130,2},{3,131},{131,3},{4... | collective-permute-start | bytes 73736 | tf_op jit(solution)/shard_map/ppermute | solution.py:279
  7.2 23.9 %copy-start.9 = (f32[64]{0:T(128)S(1)}, f32[64]{0:T(128)}, u32[]{:S(2)}) copy-start(f32[64]{0:T(128)} %param.8) | copy-start | bytes 772
  7.2 24.6 %copy-start.2 = (bf16[3,3,3,32,64]{4,3,2,1,0:T(8,128)(2,1)S(1)}, bf16[3,3,3,32,64]{4,3,2,1,0:T(8,128)(2,1)}, u32[]{:S(2)}) copy-start(bf16[3,3,3,32,64]{4,3,2,1,0:T(8,128)(2,1)} %param.7) | copy-start | bytes 331780
  7.2 28.3 %all-to-all-start = ((bf16[16,8,4,128]{3,1,2,0:T(8,128)(2,1)}), bf16[16,8,4,128]{3,1,2,0:T(8,128)(2,1)S(1)}, u32[]{:S(2)}, u32[]{:S(2)}) async-start(bf16[16,8,4,128]{3,1,2,0:T(8,128)(2,1)} %copy.37), calls=%async_computation | async-start | bytes 262144 | tf_op jit(solution)/shard_map/all_to_all | solution.py:308
  17.2 18.4 %copy-start = (bf16[8,4,40,128]{3,2,1,0:T(8,128)(2,1)}, bf16[8,4,40,128]{3,2,1,0:T(8,128)(2,1)S(1)}, u32[]{:S(2)}) copy-start(bf16[8,4,40,128]{3,2,1,0:T(8,128)(2,1)S(1)} %maximum_maximum_fusion.v_ref) | copy-start | bytes 983044
  17.2 6.7 %collective-permute-start.2 = (bf16[3,4,40,128]{3,2,1,0:T(8,128)(2,1)S(1)}, bf16[3,4,40,128]{3,2,1,0:T(8,128)(2,1)S(1)}, u32[]{:S(2)}, u32[]{:S(2)}) collective-permute-start(bf16[3,4,40,128]{3,2,1,0:T(8,128)(2,1)S(1)} %get-tuple-element.54), channel_id=1, source_target_pairs={{16,0},{32,16},{48,32},{64,48},{80,64},{96,80},{112,96},{17,1},{33... | collective-permute-start | bytes 368648 | tf_op jit(solution)/shard_map/ppermute | solution.py:289
  18.5 6.3 %collective-permute-start.1 = (bf16[3,4,40,128]{3,2,1,0:T(8,128)(2,1)S(1)}, bf16[3,4,40,128]{3,2,1,0:T(8,128)(2,1)S(1)}, u32[]{:S(2)}, u32[]{:S(2)}) collective-permute-start(bf16[3,4,40,128]{3,2,1,0:T(8,128)(2,1)S(1)} %get-tuple-element.55), channel_id=1, source_target_pairs={{0,16},{16,32},{32,48},{48,64},{64,80},{80,96},{96,112},{1,17},{17... | collective-permute-start | bytes 368648 | tf_op jit(solution)/shard_map/ppermute | solution.py:288
  23.9 12.6 %copy-start.5 = (bf16[3,4,40,128]{3,2,1,0:T(8,128)(2,1)}, bf16[3,4,40,128]{3,2,1,0:T(8,128)(2,1)S(1)}, u32[]{:S(2)}) copy-start(bf16[3,4,40,128]{3,2,1,0:T(8,128)(2,1)S(1)} %collective-permute-done.2.yhi_ref) | copy-start | bytes 368644
  23.9 12.6 %copy-start.14 = (f32[128]{0:T(128)S(1)}, f32[128]{0:T(128)}, u32[]{:S(2)}) copy-start(f32[128]{0:T(128)} %param.10) | copy-start | bytes 1540
  24.8 11.7 %copy-start.6 = (bf16[3,4,40,128]{3,2,1,0:T(8,128)(2,1)}, bf16[3,4,40,128]{3,2,1,0:T(8,128)(2,1)S(1)}, u32[]{:S(2)}) copy-start(bf16[3,4,40,128]{3,2,1,0:T(8,128)(2,1)S(1)} %collective-permute-done.1.ylo_ref) | copy-start | bytes 368644
  24.8 11.7 %collective-permute-start.3 = (bf16[14,1,40,128]{3,2,1,0:T(8,128)(2,1)S(1)}, bf16[14,1,40,128]{3,2,1,0:T(8,128)(2,1)S(1)}, u32[]{:S(2)}, u32[]{:S(2)}) collective-permute-start(bf16[14,1,40,128]{3,2,1,0:T(8,128)(2,1)S(1)} %pad_maximum_fusion.1), channel_id=1, source_target_pairs={{0,1},{1,2},{2,3},{3,4},{4,5},{5,6},{6,7},{7,8},{8,9},{9,10},{10,1... | collective-permute-start | bytes 430088 | tf_op jit(solution)/shard_map/ppermute | solution.py:293
  29.2 7.3 %collective-permute-start.4 = (bf16[14,1,40,128]{3,2,1,0:T(8,128)(2,1)S(1)}, bf16[14,1,40,128]{3,2,1,0:T(8,128)(2,1)S(1)}, u32[]{:S(2)}, u32[]{:S(2)}) collective-permute-start(bf16[14,1,40,128]{3,2,1,0:T(8,128)(2,1)S(1)} %pad_maximum_fusion.2), channel_id=1, source_target_pairs={{1,0},{2,1},{3,2},{4,3},{5,4},{6,5},{7,6},{8,7},{9,8},{10,9},{11,1... | collective-permute-start | bytes 430088 | tf_op jit(solution)/shard_map/ppermute | solution.py:294
  36.5 0.8 copy-start.10
  36.5 0.7 copy-start.11
  47.3 24.4 %copy-start.4 = (bf16[4,4,16,256]{3,2,1,0:T(8,128)(2,1)S(1)}, bf16[4,4,16,256]{3,2,1,0:T(8,128)(2,1)}, u32[]{:S(2)}) copy-start(bf16[4,4,16,256]{3,2,1,0:T(8,128)(2,1)} %get-tuple-element.29) | copy-start | bytes 393220
  48.2 2.7 %collective-permute-start.5 = (bf16[4,4,2,256]{3,2,1,0:T(2,128)(2,1)S(1)}, bf16[4,4,2,256]{3,2,1,0:T(2,128)(2,1)S(1)}, u32[]{:S(2)}, u32[]{:S(2)}) collective-permute-start(bf16[4,4,2,256]{3,2,1,0:T(2,128)(2,1)S(1)} %broadcast_select_fusion.4), channel_id=1, source_target_pairs={{0,128},{128,0},{1,129},{129,1},{2,130},{130,2},{3,131},{131,3},{4... | collective-permute-start | bytes 49160 | tf_op jit(solution)/shard_map/ppermute | solution.py:279
  51.9 20.5 %copy-start.1 = (bf16[4,4,24,256]{3,2,1,0:T(8,128)(2,1)}, bf16[4,4,24,256]{3,2,1,0:T(8,128)(2,1)S(1)}, u32[]{:S(2)}) copy-start(bf16[4,4,24,256]{3,2,1,0:T(8,128)(2,1)S(1)} %maximum_maximum_fusion.1.g_ref) | copy-start | bytes 589828
  52.0 6.1 %collective-permute-start.7 = (bf16[2,4,24,256]{3,2,1,0:T(8,128)(2,1)S(1)}, bf16[2,4,24,256]{3,2,1,0:T(8,128)(2,1)S(1)}, u32[]{:S(2)}, u32[]{:S(2)}) collective-permute-start(bf16[2,4,24,256]{3,2,1,0:T(8,128)(2,1)S(1)} %get-tuple-element.58), channel_id=1, source_target_pairs={{16,0},{32,16},{48,32},{64,48},{80,64},{96,80},{112,96},{17,1},{33... | collective-permute-start | bytes 294920 | tf_op jit(solution)/shard_map/ppermute | solution.py:289
  53.3 6.4 %collective-permute-start.6 = (bf16[2,4,24,256]{3,2,1,0:T(8,128)(2,1)S(1)}, bf16[2,4,24,256]{3,2,1,0:T(8,128)(2,1)S(1)}, u32[]{:S(2)}, u32[]{:S(2)}) collective-permute-start(bf16[2,4,24,256]{3,2,1,0:T(8,128)(2,1)S(1)} %get-tuple-element.59), channel_id=1, source_target_pairs={{0,16},{16,32},{32,48},{48,64},{64,80},{80,96},{96,112},{1,17},{17... | collective-permute-start | bytes 294920 | tf_op jit(solution)/shard_map/ppermute | solution.py:288
  58.1 26.4 %copy-start.7 = (bf16[2,4,24,256]{3,2,1,0:T(8,128)(2,1)}, bf16[2,4,24,256]{3,2,1,0:T(8,128)(2,1)S(1)}, u32[]{:S(2)}) copy-start(bf16[2,4,24,256]{3,2,1,0:T(8,128)(2,1)S(1)} %collective-permute-done.7.yhi_ref) | copy-start | bytes 294916
  59.7 24.7 %copy-start.8 = (bf16[2,4,24,256]{3,2,1,0:T(8,128)(2,1)}, bf16[2,4,24,256]{3,2,1,0:T(8,128)(2,1)S(1)}, u32[]{:S(2)}) copy-start(bf16[2,4,24,256]{3,2,1,0:T(8,128)(2,1)S(1)} %collective-permute-done.6.ylo_ref) | copy-start | bytes 294916
  59.8 24.7 %collective-permute-start.8 = (bf16[8,1,24,256]{3,2,1,0:T(8,128)(2,1)S(1)}, bf16[8,1,24,256]{3,2,1,0:T(8,128)(2,1)S(1)}, u32[]{:S(2)}, u32[]{:S(2)}) collective-permute-start(bf16[8,1,24,256]{3,2,1,0:T(8,128)(2,1)S(1)} %pad_maximum_fusion.3), channel_id=1, source_target_pairs={{0,1},{1,2},{2,3},{3,4},{4,5},{5,6},{6,7},{7,8},{8,9},{9,10},{10,1... | collective-permute-start | bytes 294920 | tf_op jit(solution)/shard_map/ppermute | solution.py:293
  65.3 19.2 %collective-permute-start.9 = (bf16[8,1,24,256]{3,2,1,0:T(8,128)(2,1)S(1)}, bf16[8,1,24,256]{3,2,1,0:T(8,128)(2,1)S(1)}, u32[]{:S(2)}, u32[]{:S(2)}) collective-permute-start(bf16[8,1,24,256]{3,2,1,0:T(8,128)(2,1)S(1)} %pad_maximum_fusion.4), channel_id=1, source_target_pairs={{1,0},{2,1},{3,2},{4,3},{5,4},{6,5},{7,6},{8,7},{9,8},{10,9},{11,1... | collective-permute-start | bytes 294920 | tf_op jit(solution)/shard_map/ppermute | solution.py:294
  72.4 24.6 %all-to-all-start.2 = ((bf16[16,8,4,128]{3,2,1,0:T(4,128)(2,1)}), bf16[16,8,4,128]{3,2,1,0:T(4,128)(2,1)S(1)}, u32[]{:S(2)}, u32[]{:S(2)}) async-start(bf16[16,8,4,128]{3,2,1,0:T(4,128)(2,1)} %copy.41), calls=%async_computation.2 | async-start | bytes 262144 | tf_op jit(solution)/shard_map/all_to_all | solution.py:335
  84.5 0.6 copy-start.12
  84.5 0.7 copy-start.13
  97.0 43.6 %all-to-all-start.1 = ((bf16[256,5,2,128]{3,2,1,0:T(2,128)(2,1)}), bf16[256,5,2,128]{3,2,1,0:T(2,128)(2,1)S(1)}, u32[]{:S(2)}, u32[]{:S(2)}) async-start(bf16[256,5,2,128]{3,2,1,0:T(2,128)(2,1)} %bitcast.51), calls=%async_computation.1 | async-start | bytes 1310720 | tf_op jit(solution)/shard_map/all_to_all | solution.py:347
  142.3 28.7 %all-to-all-start.3 = ((bf16[256,5,2,128]{3,2,1,0:T(2,128)(2,1)}), bf16[256,5,2,128]{3,2,1,0:T(2,128)(2,1)S(1)}, u32[]{:S(2)}, u32[]{:S(2)}) async-start(bf16[256,5,2,128]{3,2,1,0:T(2,128)(2,1)} %broadcast_in_dim.22), calls=%async_computation.3 | async-start | bytes 1310720 | tf_op jit(solution)/shard_map/all_to_all | solution.py:351

commit v3 on v2

--- a/solution.py
+++ b/solution.py
@@ -1,3 +1,4 @@
+import functools
 import math
 
 import jax
@@ -25,7 +26,7 @@
         in_specs=[smem if a.dtype == jnp.int32 else vmem for a in args],
         out_specs=jax.tree.map(lambda _: vmem, outs),
         scratch_shapes=scratch,
-        compiler_params=pltpu.CompilerParams(vmem_limit_bytes=60 * 2**20),
+        compiler_params=pltpu.CompilerParams(vmem_limit_bytes=24 * 2**20),
         cost_estimate=pl.CostEstimate(flops=flops, bytes_accessed=10**6, transcendentals=0),
     )(*args)
 
@@ -64,14 +65,19 @@
                 b_ref[t * 256 + zi * 64 : t * 256 + zi * 64 + 64, zo * 128 : zo * 128 + 128] = wb(dx, dy, zi - zo)
 
 
-def banded_back(wa_ref, wb_ref, bt_ref, at_ref):
-    wa, wb, pair, zero_b = blocks(wa_ref, wb_ref)
+def banded_back_b(wb_ref, bt_ref):
+    _, wb, _, zero_b = blocks(None, wb_ref)
     for t, (dx, dy) in enumerate(TAPS):
         for z in range(4):
             for zi in range(4):
                 dz = zi - z // 2
                 block = wb(2 - dx, 2 - dy, 2 - dz) if 0 <= dz <= 2 else zero_b
                 bt_ref[z * 64 : z * 64 + 64, t * 512 + zi * 128 : t * 512 + zi * 128 + 128] = block
+
+
+def banded_back_a(wa_ref, at_ref):
+    wa, _, pair, _ = blocks(wa_ref, None)
+    for t, (dx, dy) in enumerate(TAPS):
         for z in range(8):
             for p in range(6):
                 dz = 2 * p - z - 1
@@ -94,9 +100,9 @@
 
 
 def forward(
-    where_ref, v_ref, ylo_ref, yhi_ref, zlo_ref, zhi_ref, a_ref, bias_a_ref, b_ref, bias_b_ref, cot_ref,
-    feat_ref, grad_ref, sum_ref, px_ref, vo_ref, slope_ref,
-    f_ref, vx_ref, s_ref, p_ref,
+    where_ref, v_ref, ynear_ref, yfar_ref, znear_ref, zfar_ref, a_ref, bias_a_ref, b_ref, bias_b_ref, cot_ref,
+    feat_ref, grad_ref, sum_ref, px_ref, vo_ref, slope_ref, face_ref,
+    f_ref, vx_ref, s_ref, p_ref, g_ref,
 ):
     gx, gy, gz = position(where_ref)
 
@@ -104,22 +110,23 @@
         def step(y, carry):
             f_ref[0:nq, 0:40, :] = src[y].astype(F32)
             for dx in range(3):
-                vx_ref[dx, y0 + y, q0 : q0 + nq] = f_ref[0:nq, pl.ds(dx, 48), :].astype(BF16)
+                vx_ref[dx, y0 + y, pl.ds(q0, nq)] = f_ref[0:nq, pl.ds(dx, 48), :].astype(BF16)
 
             @pl.when(jnp.logical_and(y0 + y >= 2, y0 + y < 12))
             def _():
                 for dx in range(3):
-                    vo_ref[dx, y0 + y - 2, q0 : q0 + nq] = f_ref[0:nq, pl.ds(dx + 2, 32), :].astype(BF16)
+                    vo_ref[dx, y0 + y - 2, pl.ds(q0, nq)] = f_ref[0:nq, pl.ds(dx + 2, 32), :].astype(BF16)
 
             return carry
 
         lax.fori_loop(0, rows, step, 0)
 
-    stage(ylo_ref, 3, 0, 1, 4)
+    even_y, even_z = gy % 2 == 0, gz % 2 == 0
     stage(v_ref, 8, 3, 1, 4)
-    stage(yhi_ref, 3, 11, 1, 4)
-    stage(zlo_ref, 14, 0, 0, 1)
-    stage(zhi_ref, 14, 0, 5, 1)
+    stage(ynear_ref, 3, jnp.where(even_y, 11, 0), 1, 4)
+    stage(yfar_ref, 3, jnp.where(even_y, 0, 11), 1, 4)
+    stage(znear_ref, 14, 0, jnp.where(even_z, 5, 0), 1)
+    stage(zfar_ref, 14, 0, jnp.where(even_z, 0, 5), 1)
 
     fold = iota((6, 48, 128), 2) < 64
     shape = (6, 24, 128)
@@ -163,8 +170,13 @@
     cot = cot_ref[...].reshape(256, 256).astype(F32)
     grad = (cot * (s * (1.0 + before * (1.0 - s)))).astype(BF16)
     grad_ref[...] = grad.reshape(4, 4, 16, 256)
-    total = jnp.sum(grad.astype(F32), axis=0, keepdims=True)
+    wide = grad.astype(F32)
+    total = jnp.sum(wide, axis=0, keepdims=True)
     sum_ref[...] = total[:, :128] + total[:, 128:]
+    for h in range(2):
+        lanes = slice(h * 128, h * 128 + 128)
+        g_ref[...] = wide[:, lanes].reshape(4, 4, 16, 128)
+        face_ref[..., lanes] = jnp.where(gx == 0, g_ref[:, :, pl.ds(14, 2), :], g_ref[:, :, pl.ds(0, 2), :]).astype(BF16)
 
 
 TN = (((0,), (0,)), ((), ()))
@@ -183,9 +195,9 @@
 
 
 def backward(
-    where_ref, g_ref, ylo_ref, yhi_ref, zlo_ref, zhi_ref, bt_ref, slope_ref, vo_ref, wb_ref, sum_b_ref,
-    ga_ref, flat_ref,
-    f_ref, gx_ref, s_ref, t_ref, own_ref,
+    where_ref, g_ref, ynear_ref, yfar_ref, znear_ref, zfar_ref, bt_ref, slope_ref, vo_ref, wb_ref, sum_b_ref,
+    ga_ref, keep_ref, send_ref,
+    f_ref, gx_ref, s_ref, t_ref, own_ref, flat_ref,
 ):
     gx, gy, gz = position(where_ref)
 
@@ -194,18 +206,19 @@
             for h in range(2):
                 f_ref[h, 0:nq, 0:24, :] = src[y, :, :, h * 128 : h * 128 + 128].astype(F32)
                 for dx in range(3):
-                    gx_ref[dx, y0 + y, q0 : q0 + nq, :, h * 128 : h * 128 + 128] = f_ref[
+                    gx_ref[dx, y0 + y, pl.ds(q0, nq), :, h * 128 : h * 128 + 128] = f_ref[
                         h, 0:nq, pl.ds(dx, 32), :
                     ].astype(BF16)
             return carry
 
         lax.fori_loop(0, rows, step, 0)
 
-    stage(ylo_ref, 2, 0, 1, 4)
+    even_y, even_z = gy % 2 == 0, gz % 2 == 0
     stage(g_ref, 4, 2, 1, 4)
-    stage(yhi_ref, 2, 6, 1, 4)
-    stage(zlo_ref, 8, 0, 0, 1)
-    stage(zhi_ref, 8, 0, 5, 1)
+    stage(ynear_ref, 2, jnp.where(even_y, 6, 0), 1, 4)
+    stage(yfar_ref, 2, jnp.where(even_y, 0, 6), 1, 4)
+    stage(znear_ref, 8, 0, jnp.where(even_z, 5, 0), 1)
+    stage(zfar_ref, 8, 0, jnp.where(even_z, 0, 5), 1)
 
     shape = (12, 48, 128)
     x = iota(shape, 1) + (gx * 32 - 2)
@@ -254,6 +267,34 @@
             block = block + pltpu.roll(terms[zo * 64 : zo * 64 + 64], 256 - 32 * zo, 1)
         flat_ref[1728 + 64 * t : 1792 + 64 * t] = block[:, :128].astype(BF16)
 
+    half = pl.multiple_of((gz % 2) * 1280, 1280)
+    rest = pl.multiple_of((1 - gz % 2) * 1280, 1280)
+    keep_ref[...] = flat_ref[pl.ds(half, 1280), :]
+    send_ref[...] = flat_ref[pl.ds(rest, 1280), :]
+
+
+def finish(scale_a, scale_b, where_ref, mine_ref, other_ref, wa_ref, ba_ref, wb_ref, bb_ref):
+    core = where_ref[0] % 2
+
+    def put(first_ref, second_ref):
+        wb_ref[0:1280] = first_ref[...].astype(F32) * scale_b
+        wb_ref[1280:1728] = second_ref[0:448].astype(F32) * scale_b
+        for t in range(9):
+            block = second_ref[448 + 64 * t : 512 + 64 * t].astype(F32).T * scale_a
+            for dz in range(3):
+                wa_ref[3 * t + dz] = block[32 + 32 * dz : 64 + 32 * dz]
+        tail = second_ref[1024:1040].astype(F32)
+        bb_ref[...] = tail[0:1] * scale_b
+        ba_ref[...] = tail[1:2, :64] * scale_a
+
+    @pl.when(core == 0)
+    def _():
+        put(mine_ref, other_ref)
+
+    @pl.when(core == 1)
+    def _():
+        put(other_ref, mine_ref)
+
 
 def input_grad(ga_ref, at_ref, out_ref):
     for h in range(2):
@@ -266,33 +307,45 @@
         out_ref[:, h] = value.astype(BF16).reshape(8, 32, 256)
 
 
-def ends(axis):
+def swaps(axis):
     count = lax.axis_size(axis)
-    up = [(i, i + 1) for i in range(count - 1)]
-    return up, [(b, a) for a, b in up]
-
-
-def swap_sides(block, width, rows):
+    near = [(i, i ^ 1) for i in range(count)]
+    far = [(i, i + 1 if i % 2 else i - 1) for i in range(1, count - 1)]
+    return lax.axis_index(axis) % 2 == 0, near, far
+
+
+def halo(block, face, width, x_rows):
     first = lax.axis_index("gx") == 0
-    length = block.shape[2]
-    face = jnp.where(first, block[:, :, length - width :], block[:, :, :width])
     got = lax.ppermute(face, "gx", [(0, 1), (1, 0)])
     none = jnp.zeros_like(got)
-    rest = jnp.zeros(block.shape[:2] + (rows - length - 2 * width,) + block.shape[3:], block.dtype)
-    return jnp.concatenate([jnp.where(first, none, got), block, jnp.where(first, got, none), rest], axis=2)
-
-
-def halo(block, width, x_rows):
-    wide = swap_sides(block, width, x_rows)
-    up, down = ends("gy")
-    ylo = lax.ppermute(wide[wide.shape[0] - width :], "gy", up)
-    yhi = lax.ppermute(wide[:width], "gy", down)
-    up, down = ends(GZ)
+    rest = jnp.zeros(block.shape[:2] + (x_rows - block.shape[2] - 2 * width,) + block.shape[3:], block.dtype)
+    wide = jnp.concatenate([jnp.where(first, none, got), block, jnp.where(first, got, none), rest], axis=2)
+    even, near, far = swaps("gy")
+    low, high = wide[:width], wide[wide.shape[0] - width :]
+    yfar = lax.ppermute(jnp.where(even, low, high), "gy", far)
+    ynear = lax.ppermute(jnp.where(even, high, low), "gy", near)
+    ylo, yhi = jnp.where(even, yfar, ynear), jnp.where(even, ynear, yfar)
+    even, near, far = swaps(GZ)
     last = jnp.concatenate([ylo[:, 3:], wide[:, 3:], yhi[:, 3:]], axis=0)
     head = jnp.concatenate([ylo[:, :1], wide[:, :1], yhi[:, :1]], axis=0)
-    zlo = lax.ppermute(last, GZ, up)
-    zhi = lax.ppermute(head, GZ, down)
-    return wide, ylo, yhi, zlo, zhi
+    zfar = lax.ppermute(jnp.where(even, head, last), GZ, far)
+    znear = lax.ppermute(jnp.where(even, last, head), GZ, near)
+    return wide, ynear, yfar, znear, zfar
+
+
+CHIPS = ("gx", "gy", "gz_0")
+
+
+def to_slabs(pieces):
+    index = lax.axis_index(GZ)
+    shape = pieces.shape
+    for b in range(4):
+        other = 1 - (index >> b) % 2
+        pieces = pieces.reshape((16 >> (b + 1), 2, 1 << b) + shape[1:])
+        part = lax.dynamic_index_in_dim(pieces, other, 1)
+        got = lax.ppermute(part, GZ, [(i, i ^ (1 << b)) for i in range(16)])
+        pieces = lax.dynamic_update_slice_in_dim(pieces, got, other, 1)
+    return pieces.reshape(shape)
 
 
 def on_device(volume, weight_a, bias_a, weight_b, bias_b, cotangent):
@@ -302,7 +355,8 @@
     where = lax.axis_index(ALL).astype(jnp.int32).reshape(1)
 
     v = jnp.transpose(volume.reshape(32, 32, 8, 4, 4), (2, 3, 1, 4, 0)).reshape(8, 4, 32, 128)
-    sides = halo(v, 3, 40)
+    face = jnp.where(lax.axis_index("gx") == 0, v[:, :, 29:32], v[:, :, 0:3])
+    sides = halo(v, face, 3, 40)
 
     cot = jnp.transpose(cotangent[:, 0], (2, 1, 0)).reshape(16, 8, 4, 128)
     cot = lax.all_to_all(cot, GZ, 0, 0, tiled=True)
@@ -312,57 +366,66 @@
     wa27 = jnp.concatenate([wa27, wa27], axis=-1)
     wb27 = weight_b.reshape(27, 64, 128)
     m_a, m_b = call(banded_ahead, (sds(2304, 256), sds(2304, 256)), [], wa27, wb27, flops=10**7)
-    m_bt, m_at = call(banded_back, (sds(256, 4608), sds(256, 6912)), [], wa27, wb27, flops=10**7)
-
-    feat, grad_b, sum_b, px, vo, slope = call(
+    m_bt = call(banded_back_b, sds(256, 4608), [], wb27, flops=10**7)
+    m_at = call(banded_back_a, sds(256, 6912), [], wa27, flops=10**7)
+
+    feat, grad_b, sum_b, px, vo, slope, face_b = call(
         forward,
         (
             sds(4, 4, 16, 256), sds(4, 4, 16, 256), sds(1, 128, dtype=F32),
             sds(3, 6, 5, 16, 128), sds(3, 10, 6, 32, 128), sds(5, 12, 48, 256),
+            sds(4, 4, 2, 256),
         ),
         [
             pltpu.VMEM((4, 56, 128), F32), pltpu.VMEM((3, 14, 6, 48, 128), BF16),
-            pltpu.VMEM((6, 48, 128), F32), pltpu.VMEM((6, 24, 128), F32),
+            pltpu.VMEM((6, 48, 128), F32), pltpu.VMEM((6, 24, 128), F32), pltpu.VMEM((4, 4, 16, 128), F32),
         ],
         where, *sides, m_a, jnp.tile(bias_a, 4).reshape(1, 256), m_b, jnp.tile(bias_b, 2).reshape(1, 256), cot,
         flops=2 * 10**9,
     )
 
-    sides_b = halo(grad_b, 2, 24)
+    sides_b = halo(grad_b, face_b, 2, 24)
     wb = call(weight_b_terms, sds(27, 64, 128), [], px, grad_b, flops=10**9)
 
     out = jnp.transpose(feat.reshape(4, 4, 16, 2, 128), (2, 1, 3, 0, 4)).reshape(16, 8, 4, 128)
-    out = lax.all_to_all(out, GZ, 0, 0, tiled=True).reshape(128, 4, 128)
-
-    ga, flat = call(
+
+    ga, keep, send = call(
         backward,
-        (sds(3, 10, 5, 32, 256), sds(2560, 128)),
+        (sds(3, 10, 5, 32, 256), sds(1280, 128), sds(1280, 128)),
         [
             pltpu.VMEM((2, 4, 40, 128), F32), pltpu.VMEM((3, 8, 6, 32, 256), BF16),
             pltpu.VMEM((6, 48, 128), F32), pltpu.VMEM((12, 48, 128), F32), pltpu.VMEM((8, 5, 32, 256), BF16),
+            pltpu.VMEM((2560, 128), BF16),
         ],
         where, *sides_b, m_bt, slope, vo, wb, sum_b, flops=2 * 10**9,
     )
 
-    shares = lax.all_to_all(flat.reshape(256, 5, 2, 128), ALL, 0, 0, tiled=True)
+    flip = [(0, 1), (1, 0)]
+    count = lax.axis_size(CHIPS)
+    got = lax.ppermute(send, "gz_1", flip)
+    chip = (keep.astype(F32) + got.astype(F32)).astype(BF16)
+    shares = lax.all_to_all(chip.reshape(count, 5, 2, 128), CHIPS, 0, 0, tiled=True)
     share = jnp.sum(shares.astype(F32), axis=0).astype(BF16)
-    share, out = lax.optimization_barrier((share, out))
-    spread = jnp.broadcast_to(share[None], (256, 5, 2, 128))
-    total = lax.all_to_all(spread, ALL, 0, 0, tiled=True).reshape(2560, 128).astype(F32)
-    features = jnp.transpose(out, (2, 1, 0)).reshape(128, 1, 4, 128)
+    spread = jnp.broadcast_to(share[None], (count, 5, 2, 128))
+    mine = lax.all_to_all(spread, CHIPS, 0, 0, tiled=True).reshape(count * 10, 128)
+    other = lax.ppermute(mine, "gz_1", flip)
+    features = jnp.transpose(to_slabs(out).reshape(128, 4, 128), (2, 1, 0)).reshape(128, 1, 4, 128)
 
     gi = call(input_grad, sds(8, 2, 32, 256), [], ga, m_at, flops=2 * 10**9)
     gi = jnp.transpose(gi.reshape(8, 2, 32, 8, 32), (4, 2, 0, 1, 3)).reshape(32, 32, 8, 16)
 
-    total_wb = total[:1728].reshape(3, 3, 3, 64, 128) * scale_b
-    total_wa = jnp.transpose(total[1728:2304].reshape(9, 64, 4, 32)[:, :, 1:], (0, 2, 3, 1)) * scale_a
+    total_wa, total_ba, total_wb, total_bb = call(
+        functools.partial(finish, scale_a, scale_b),
+        (sds(27, 32, 64, dtype=F32), sds(1, 64, dtype=F32), sds(1728, 128, dtype=F32), sds(1, 128, dtype=F32)),
+        [], where, mine, other, flops=10**6,
+    )
     return (
         features,
         gi,
         total_wa.reshape(3, 3, 3, 32, 64),
-        total[2305, :64] * scale_a,
-        total_wb,
-        total[2304] * scale_b,
+        total_ba.reshape(64),
+        total_wb.reshape(3, 3, 3, 64, 128),
+        total_bb.reshape(128),
     )
 
 

time: 175 us -> 151 us (0.86)
  Pallas kernels: 36.8 us -> 21.1 us
  local copies, waits for them, and re-layouts: 16 us -> 26.1 us
  starting transfers between devices: 73.6 us -> 65.3 us
  waiting for transfers between devices: 41.1 us -> 34.4 us
  other arithmetic: 5.92 us -> 1.86 us
    all_to_all x3 -> x2, waiting for transfers between devices: 34.9 us -> 13.7 us  [the longest x1 13.7 us: on_device(): lax.all_to_all(chip.reshape(count, 5, 2, 128), CHIPS, 0, 0, tiled=True)]
    pallas_call x6 -> x8, Pallas kernels: 36.8 us -> 21.1 us  [call(): pl.pallas_call(body, out_shape=outs, in_specs=[smem if a.dtype == jnp.int...]
    ppermute x10 -> x16, waiting for transfers between devices: 6.22 us -> 20.6 us  [the longest x4 10.1 us: to_slabs(): got = lax.ppermute(part, GZ, [(i, i ^ 1 << b) for i in range(16)])]
    all_to_all x3 -> x2, starting transfers between devices: 36.5 us -> 25.4 us  [the longest x1 18.2 us: on_device(): lax.all_to_all(chip.reshape(count, 5, 2, 128), CHIPS, 0, 0, tiled=True)]
    unnamed x32 -> x30, local copies, waits for them, and re-layouts: 1.64 us -> 10.1 us
    dynamic_update_slice x0 -> x4, local copies, waits for them, and re-layouts: none -> 2.99 us  [to_slabs(): pieces = lax.dynamic_update_slice_in_dim(pieces, got, other, 1)]
    ppermute x10 -> x16, starting transfers between devices: 27.5 us -> 30.5 us  [the longest x2 10.1 us: halo(): zfar = lax.ppermute(jnp.where(even, head, last), GZ, far)]
    dynamic_slice x0 -> x4, local copies, waits for them, and re-layouts: none -> 2.16 us  [to_slabs(): part = lax.dynamic_index_in_dim(pieces, other, 1)]
  transfers between devices with their start and end apart: 14 -> 19, of which waited for: 6 -> 9; matrix products, arithmetic and copies ran while one was open for 6% -> 9% of each run, Pallas kernels for 15% -> 2%
where the time goes in v3:
time: 151 us; the launch traced here: 150 us
  starting transfers between devices  65.3 us (43%)
  waiting for transfers between devices  34.4 us (23%)
  local copies, waits for them, and re-layouts  26.1 us (17%)
  Pallas kernels  21.1 us (14%)
  other arithmetic  1.86 us (1%)
    pallas_call x8, Pallas kernels, call(): pl.pallas_call(body, out_shape=outs, in_specs=[smem if a.dtype == jnp.int...  21.1 us
    all_to_all x1, starting transfers between devices, on_device(): lax.all_to_all(chip.reshape(count, 5, 2, 128), CHIPS, 0, 0, tiled=True)  18.2 us
    all_to_all x1, waiting for transfers between devices, on_device(): lax.all_to_all(chip.reshape(count, 5, 2, 128), CHIPS, 0, 0, tiled=True)  13.7 us
    ppermute x4, waiting for transfers between devices, to_slabs(): got = lax.ppermute(part, GZ, [(i, i ^ 1 << b) for i in range(16)])  10.1 us
    unnamed x30, local copies, waits for them, and re-layouts  10.1 us
    ppermute x2, starting transfers between devices, halo(): zfar = lax.ppermute(jnp.where(even, head, last), GZ, far)  10.1 us
    all_to_all x1, starting transfers between devices, on_device(): cot = lax.all_to_all(cot, GZ, 0, 0, tiled=True)  9.43 us
    ppermute x2, starting transfers between devices, halo(): ynear = lax.ppermute(jnp.where(even, high, low), 'gy', near)  8.34 us
  transfers between devices with their start and end apart: 19, of which 9 were waited for; matrix products, arithmetic and copies ran while one was open for 9% of the time, Pallas kernels for 2%

profile of v3, /device:TPU:1, one launch (start us, length us, event | category | flops | bytes accessed | tf_op | source)
XLA Modules:
  0.0 149.8 jit_solution(4155823606982307156)
XLA Ops:
  0.6 3.1 %copy.23 = bf16[32,32,8,4,4]{0,4,1,3,2:T(4,128)(2,1)S(1)} copy(bf16[32,32,8,4,4]{1,4,3,2,0:T(4,128)(2,1)} %bitcast.48) | data formatting | bytes 524288 | tf_op jit(solution)/shard_map/reshape | solution.py:357
  3.7 0.5 reshape.384
  4.3 2.1 %collective-permute-start = (bf16[8,4,3,128]{3,2,1,0:T(4,128)(2,1)S(1)}, bf16[8,4,3,128]{3,2,1,0:T(4,128)(2,1)S(1)}, u32[]{:S(2)}, u32[]{:S(2)}) collective-permute-start(bf16[8,4,3,128]{3,2,1,0:T(4,128)(2,1)S(1)} %slice_select_fusion), channel_id=1, source_target_pairs={{0,128},{128,0},{1,129},{129,1},{2,130},{130,2},{3,131},{131,3},{4... | collective-permute-start | bytes 73736 | tf_op jit(solution)/shard_map/ppermute | solution.py:319
  6.6 0.7 copy.25
  7.2 9.4 %all-to-all-start = ((bf16[16,8,4,128]{3,1,2,0:T(8,128)(2,1)}), bf16[16,8,4,128]{3,1,2,0:T(8,128)(2,1)S(1)}, u32[]{:S(2)}, u32[]{:S(2)}) async-start(bf16[16,8,4,128]{3,1,2,0:T(8,128)(2,1)} %copy.25), calls=%async_computation | async-start | bytes 262144 | tf_op jit(solution)/shard_map/all_to_all | solution.py:362
  17.1 0.7 collective-permute-start.2
  17.8 3.9 %collective-permute-start.1 = (bf16[3,4,40,128]{3,2,1,0:T(8,128)(2,1)S(1)}, bf16[3,4,40,128]{3,2,1,0:T(8,128)(2,1)S(1)}, u32[]{:S(2)}, u32[]{:S(2)}) collective-permute-start(bf16[3,4,40,128]{3,2,1,0:T(8,128)(2,1)S(1)} %get-tuple-element.53), channel_id=1, source_target_pairs={{0,16},{16,0},{32,48},{48,32},{64,80},{80,64},{96,112},{112,96},{1... | collective-permute-start | bytes 368648 | tf_op jit(solution)/shard_map/ppermute | solution.py:326
  21.7 3.3 %collective-permute-done.1.ynear_ref = bf16[3,4,40,128]{3,2,1,0:T(8,128)(2,1)S(1)} collective-permute-done((bf16[3,4,40,128]{3,2,1,0:T(8,128)(2,1)S(1)}, bf16[3,4,40,128]{3,2,1,0:T(8,128)(2,1)S(1)}, u32[]{:S(2)}, u32[]{:S(2)}) %collective-permute-start.1) | collective-permute-done | bytes 122912 | tf_op jit(solution)/shard_map/ppermute | solution.py:326
  25.1 4.1 %collective-permute-start.4 = (bf16[14,1,40,128]{3,2,1,0:T(8,128)(2,1)S(1)}, bf16[14,1,40,128]{3,2,1,0:T(8,128)(2,1)S(1)}, u32[]{:S(2)}, u32[]{:S(2)}) collective-permute-start(bf16[14,1,40,128]{3,2,1,0:T(8,128)(2,1)S(1)} %get-tuple-element.54), channel_id=1, source_target_pairs={{1,2},{2,1},{3,4},{4,3},{5,6},{6,5},{7,8},{8,7},{9,10},{10,9},{11,... | collective-permute-start | bytes 430088 | tf_op jit(solution)/shard_map/ppermute | solution.py:331
  29.9 0.7 copy-done
  30.6 1.1 copy-done.4
  32.0 1.3 copy-done.5
  33.3 7.0 %shard_map.110 = (bf16[4,4,16,256]{3,2,1,0:T(8,128)(2,1)S(1)}, bf16[4,4,16,256]{3,2,1,0:T(8,128)(2,1)S(1)}, f32[1,128]{1,0:T(1,128)S(1)}, bf16[3,6,5,16,128]{4,3...) custom-call(s32[1]{0:T(128)} %bitcast.where_ref, ...), custom_call_target="tpu_custom_call" | custom-call | flops 2000000000 | bytes 1000000 | tf_op jit(solution)/shard_map/pallas_call | solution.py:23
  40.7 2.3 %collective-permute-done.9 = bf16[4,4,2,256]{3,2,1,0:T(2,128)(2,1)S(1)} collective-permute-done((bf16[4,4,2,256]{3,2,1,0:T(2,128)(2,1)S(1)}, bf16[4,4,2,256]{3,2,1,0:T(2,128)(2,1)S(1)}, u32[]{:S(2)}, u32[]{:S(2)}) %collective-permute-start.9) | collective-permute-done | bytes 16416 | tf_op jit(solution)/shard_map/ppermute | solution.py:319
  43.2 0.7 collective-permute-start.11
  43.8 4.4 %collective-permute-start.10 = (bf16[2,4,24,256]{3,2,1,0:T(8,128)(2,1)S(1)}, bf16[2,4,24,256]{3,2,1,0:T(8,128)(2,1)S(1)}, u32[]{:S(2)}, u32[]{:S(2)}) collective-permute-start(bf16[2,4,24,256]{3,2,1,0:T(8,128)(2,1)S(1)} %get-tuple-element.65), channel_id=1, source_target_pairs={{0,16},{16,0},{32,48},{48,32},{64,80},{80,64},{96,112},{112,96},{1... | collective-permute-start | bytes 294920 | tf_op jit(solution)/shard_map/ppermute | solution.py:326
  48.3 2.0 %collective-permute-done.10.ynear_ref = bf16[2,4,24,256]{3,2,1,0:T(8,128)(2,1)S(1)} collective-permute-done((bf16[2,4,24,256]{3,2,1,0:T(8,128)(2,1)S(1)}, bf16[2,4,24,256]{3,2,1,0:T(8,128)(2,1)S(1)}, u32[]{:S(2)}, u32[]{:S(2)}) %collective-permute-start.10) | collective-permute-done | bytes 98336 | tf_op jit(solution)/shard_map/ppermute | solution.py:326
  50.4 5.9 %collective-permute-start.13 = (bf16[8,1,24,256]{3,2,1,0:T(8,128)(2,1)S(1)}, bf16[8,1,24,256]{3,2,1,0:T(8,128)(2,1)S(1)}, u32[]{:S(2)}, u32[]{:S(2)}) collective-permute-start(bf16[8,1,24,256]{3,2,1,0:T(8,128)(2,1)S(1)} %get-tuple-element.58), channel_id=1, source_target_pairs={{1,2},{2,1},{3,4},{4,3},{5,6},{6,5},{7,8},{8,7},{9,10},{10,9},{11,... | collective-permute-start | bytes 294920 | tf_op jit(solution)/shard_map/ppermute | solution.py:331
  56.7 0.5 shard_map.112.wb_ref
  57.2 1.3 collective-permute-done.13.zfar_ref
  58.6 8.1 %shard_map.113 = (bf16[3,10,5,32,256]{4,3,2,1,0:T(8,128)(2,1)S(1)}, bf16[1280,128]{1,0:T(8,128)(2,1)S(1)}, bf16[1280,128]{1,0:T(8,128)(2,1)S(1)}) custom-call(s32[1]{0:T(128)} %bitcast.where_ref, bf16[4,4,24,256]{3,2,1,0:T(8,128)(2,1)S(1)} %maximum_maximum_fusion.1.g_ref, bf16[2,4,24,256]{3,2,1,0:T(8,128)(2,1)S(1)} %collective-permute-done.10.ynear_ref, ...), custom_call_target="tpu_custom_call" | custom-call | flops 2000000000 | bytes 1000000 | tf_op jit(solution)/shard_map/pallas_call | solution.py:23
  66.7 1.4 copy-done.6
  68.2 1.6 %collective-permute-done.14 = bf16[1280,128]{1,0:T(8,128)(2,1)S(1)} collective-permute-done((bf16[1280,128]{1,0:T(8,128)(2,1)S(1)}, bf16[1280,128]{1,0:T(8,128)(2,1)S(1)}, u32[]{:S(2)}, u32[]{:S(2)}) %collective-permute-start.14) | collective-permute-done | bytes 327712 | tf_op jit(solution)/shard_map/ppermute | solution.py:405
  69.8 0.8 add_convert_fusion
  70.6 18.2 %all-to-all-start.1 = ((bf16[128,5,2,128]{3,2,1,0:T(2,128)(2,1)}), bf16[128,5,2,128]{3,2,1,0:T(2,128)(2,1)S(1)}, u32[]{:S(2)}, u32[]{:S(2)}) async-start(bf16[128,5,2,128]{3,2,1,0:T(2,128)(2,1)} %bitcast.22), calls=%async_computation.1 | async-start | bytes 655360 | tf_op jit(solution)/shard_map/all_to_all | solution.py:407
  89.0 0.7 collective-permute-start.5
  89.7 0.9 collective-permute-done.5
  90.6 13.7 %all-to-all-done.1 = bf16[128,5,2,128]{3,2,1,0:T(2,128)(2,1)S(1)} async-done(((bf16[128,5,2,128]{3,2,1,0:T(2,128)(2,1)}), bf16[128,5,2,128]{3,2,1,0:T(2,128)(2,1)S(1)}, u32[]{:S(2)}, u32[]{:S(2)}) %all-to-all-start.1) | async-done | bytes 327712 | tf_op jit(solution)/shard_map/all_to_all | solution.py:407
  104.7 0.9 broadcast_in_dim.22
  105.6 7.2 %all-to-all-start.2 = ((bf16[128,5,2,128]{3,2,1,0:T(2,128)(2,1)}), bf16[128,5,2,128]{3,2,1,0:T(2,128)(2,1)}, u32[]{:S(2)}, u32[]{:S(2)}) async-start(bf16[128,5,2,128]{3,2,1,0:T(2,128)(2,1)} %broadcast_in_dim.22), calls=%async_computation.2 | async-start | bytes 655360 | tf_op jit(solution)/shard_map/all_to_all | solution.py:410
  113.3 6.9 %collective-permute-done.6 = bf16[4,1,2,8,4,128]{5,3,4,2,1,0:T(8,128)(2,1)S(1)} collective-permute-done((bf16[4,1,2,8,4,128]{5,3,4,2,1,0:T(8,128)(2,1)S(1)}, bf16[4,1,2,8,4,128]{5,3,4,2,1,0:T(8,128)(2,1)S(1)}, u32[]{:S(2)}, u32[]{:S(2)}) %collective-permute-start.6) | collective-permute-done | bytes 65568 | tf_op jit(solution)/shard_map/ppermute | solution.py:346
  120.2 0.7 constant_dynamic-slice_fusion.1
  120.9 0.6 collective-permute-start.7
  121.5 0.9 copy-done.1
  123.3 0.7 copy.30
  124.0 2.3 %collective-permute-done.7 = bf16[2,1,4,8,4,128]{5,3,2,1,0,4:T(8,128)(2,1)} collective-permute-done((bf16[2,1,4,8,4,128]{5,3,2,1,0,4:T(8,128)(2,1)}, bf16[2,1,4,8,4,128]{5,3,2,1,0,4:T(8,128)(2,1)}, u32[]{:S(2)}, u32[]{:S(2)}) %collective-permute-start.7) | collective-permute-done | bytes 65568 | tf_op jit(solution)/shard_map/ppermute | solution.py:346
  126.3 1.5 constant_dynamic-update-slice_fusion.1
  127.8 2.8 %collective-permute-start.15 = (bf16[1280,128]{1,0:T(8,128)(2,1)}, bf16[1280,128]{1,0:T(8,128)(2,1)}, u32[]{:S(2)}, u32[]{:S(2)}) collective-permute-start(bf16[1280,128]{1,0:T(8,128)(2,1)} %bitcast.23.mine_ref), channel_id=1, source_target_pairs={{0,1},{1,0},{2,3},{3,2},{4,5},{5,4},{6,7},{7,6},{8,9},{9,8},{10,11... | collective-permute-start | bytes 983048 | tf_op jit(solution)/shard_map/ppermute | solution.py:411
  130.6 1.5 constant_dynamic-slice_fusion
  132.0 3.5 %collective-permute-start.8 = (bf16[1,1,8,8,4,128]{5,3,2,1,4,0:T(8,128)(2,1)}, bf16[1,1,8,8,4,128]{5,3,2,1,4,0:T(8,128)(2,1)}, u32[]{:S(2)}, u32[]{:S(2)}) collective-permute-start(bf16[1,1,8,8,4,128]{5,3,2,1,4,0:T(8,128)(2,1)} %constant_dynamic-slice_fusion), channel_id=1, source_target_pairs={{0,8},{1,9},{2,10},{3,11},{4,12},{5,13},{6,14},{7,15},{8,0},{9,1},... | collective-permute-start | bytes 196616 | tf_op jit(solution)/shard_map/ppermute | solution.py:346
  135.5 1.7 %copy-done.7 = bf16[3,10,5,32,256]{4,3,2,1,0:T(8,128)(2,1)S(1)} copy-done((bf16[3,10,5,32,256]{4,3,2,1,0:T(8,128)(2,1)S(1)}, bf16[3,10,5,32,256]{4,3,2,1,0:T(8,128)(2,1)}, u32[]{:S(2)}) %copy-start.7) | copy-done | bytes 2457624
  137.2 2.0 %shard_map.115 = bf16[8,2,32,256]{3,2,1,0:T(8,128)(2,1)S(1)} custom-call(bf16[3,10,5,32,256]{4,3,2,1,0:T(8,128)(2,1)S(1)} %copy-done.7, bf16[256,6912]{1,0:T(8,128)(2,1)S(1)} %shard_map.114.at_ref), custom_call_target="tpu_custom_call" | custom-call | flops 2000000000 | bytes 1000000 | tf_op jit(solution)/shard_map/pallas_call | solution.py:23
  139.3 0.7 copy-done.3
  140.0 1.7 %reshape.395 = bf16[8,2,32,8,32]{4,3,2,1,0:T(8,128)(2,1)S(1)} reshape(bf16[8,2,32,256]{3,2,1,0:T(8,128)(2,1)} %copy-done.3) | data formatting | bytes 524288 | tf_op jit(solution)/shard_map/reshape | solution.py:415
  141.6 2.6 %copy.31 = bf16[32,32,8,2,8]{1,4,3,2,0:T(8,128)(2,1)} copy(bf16[32,32,8,2,8]{0,4,1,3,2:T(8,128)(2,1)S(1)} %bitcast.40) | data formatting | bytes 524288 | tf_op jit(solution)/shard_map/transpose | solution.py:415
  144.3 1.5 constant_dynamic-update-slice_fusion
  145.8 1.7 %copy.32 = bf16[128,1,4,128]{3,2,1,0:T(4,128)(2,1)} copy(bf16[128,1,4,128]{0,3,2,1:T(8,128)(2,1)} %bitcast.19) | data formatting | bytes 262144
  147.4 2.4 %shard_map.116 = (f32[27,32,64]{2,1,0:T(8,128)}, f32[1,64]{1,0:T(1,128)}, f32[1728,128]{1,0:T(8,128)}, f32[1,128]{1,0:T(1,128)}) custom-call(s32[1]{0:T(128)} %bitcast.where_ref, bf16[1280,128]{1,0:T(8,128)(2,1)} %bitcast.23.mine_ref, bf16[1280,128]{1,0:T(8,128)(2,1)} %collective-permute-done.15.other_ref), custom_call_target="tpu_custom_call" | custom-call | flops 1000000 | bytes 1000000 | tf_op jit(solution)/shard_map/pallas_call | solution.py:23
  (74 shorter events, 4.6 us)
Async XLA Ops:
  0.6 5.8 %copy-start.11 = (bf16[128,1,4,128]{3,2,1,0:T(4,128)(2,1)S(1)}, bf16[128,1,4,128]{3,2,1,0:T(4,128)(2,1)}, u32[]{:S(2)}) copy-start(bf16[128,1,4,128]{3,2,1,0:T(4,128)(2,1)} %param.11) | copy-start | bytes 393220
  4.3 12.5 %collective-permute-start = (bf16[8,4,3,128]{3,2,1,0:T(4,128)(2,1)S(1)}, bf16[8,4,3,128]{3,2,1,0:T(4,128)(2,1)S(1)}, u32[]{:S(2)}, u32[]{:S(2)}) collective-permute-start(bf16[8,4,3,128]{3,2,1,0:T(4,128)(2,1)S(1)} %slice_select_fusion), channel_id=1, source_target_pairs={{0,128},{128,0},{1,129},{129,1},{2,130},{130,2},{3,131},{131,3},{4... | collective-permute-start | bytes 73736 | tf_op jit(solution)/shard_map/ppermute | solution.py:319
  7.2 24.4 %all-to-all-start = ((bf16[16,8,4,128]{3,1,2,0:T(8,128)(2,1)}), bf16[16,8,4,128]{3,1,2,0:T(8,128)(2,1)S(1)}, u32[]{:S(2)}, u32[]{:S(2)}) async-start(bf16[16,8,4,128]{3,1,2,0:T(8,128)(2,1)} %copy.25), calls=%async_computation | async-start | bytes 262144 | tf_op jit(solution)/shard_map/all_to_all | solution.py:362
  16.7 12.7 %copy-start.12 = (f32[64]{0:T(128)S(1)}, f32[64]{0:T(128)}, u32[]{:S(2)}) copy-start(f32[64]{0:T(128)} %param.8) | copy-start | bytes 772
  16.7 12.8 %copy-start.10 = (bf16[3,3,3,32,64]{4,3,2,1,0:T(8,128)(2,1)S(1)}, bf16[3,3,3,32,64]{4,3,2,1,0:T(8,128)(2,1)}, u32[]{:S(2)}) copy-start(bf16[3,3,3,32,64]{4,3,2,1,0:T(8,128)(2,1)} %param.7) | copy-start | bytes 331780
  16.8 12.8 %copy-start.2 = (bf16[3,3,3,64,128]{4,3,2,1,0:T(8,128)(2,1)S(1)}, bf16[3,3,3,64,128]{4,3,2,1,0:T(8,128)(2,1)}, u32[]{:S(2)}) copy-start(bf16[3,3,3,64,128]{4,3,2,1,0:T(8,128)(2,1)} %param.9) | copy-start | bytes 1327108
  17.1 4.6 %collective-permute-start.2 = (bf16[3,4,40,128]{3,2,1,0:T(8,128)(2,1)S(1)}, bf16[3,4,40,128]{3,2,1,0:T(8,128)(2,1)S(1)}, u32[]{:S(2)}, u32[]{:S(2)}) collective-permute-start(bf16[3,4,40,128]{3,2,1,0:T(8,128)(2,1)S(1)} %get-tuple-element.52), channel_id=1, source_target_pairs={{16,32},{32,16},{48,64},{64,48},{80,96},{96,80},{17,33},{33,17},{4... | collective-permute-start | bytes 368648 | tf_op jit(solution)/shard_map/ppermute | solution.py:325
  17.8 7.2 %collective-permute-start.1 = (bf16[3,4,40,128]{3,2,1,0:T(8,128)(2,1)S(1)}, bf16[3,4,40,128]{3,2,1,0:T(8,128)(2,1)S(1)}, u32[]{:S(2)}, u32[]{:S(2)}) collective-permute-start(bf16[3,4,40,128]{3,2,1,0:T(8,128)(2,1)S(1)} %get-tuple-element.53), channel_id=1, source_target_pairs={{0,16},{16,0},{32,48},{48,32},{64,80},{80,64},{96,112},{112,96},{1... | collective-permute-start | bytes 368648 | tf_op jit(solution)/shard_map/ppermute | solution.py:326
  25.0 7.0 %copy-start.13 = (f32[128]{0:T(128)S(1)}, f32[128]{0:T(128)}, u32[]{:S(2)}) copy-start(f32[128]{0:T(128)} %param.10) | copy-start | bytes 1540
  25.1 6.9 %collective-permute-start.4 = (bf16[14,1,40,128]{3,2,1,0:T(8,128)(2,1)S(1)}, bf16[14,1,40,128]{3,2,1,0:T(8,128)(2,1)S(1)}, u32[]{:S(2)}, u32[]{:S(2)}) collective-permute-start(bf16[14,1,40,128]{3,2,1,0:T(8,128)(2,1)S(1)} %get-tuple-element.54), channel_id=1, source_target_pairs={{1,2},{2,1},{3,4},{4,3},{5,6},{6,5},{7,8},{8,7},{9,10},{10,9},{11,... | collective-permute-start | bytes 430088 | tf_op jit(solution)/shard_map/ppermute | solution.py:331
  29.2 2.8 %collective-permute-start.3 = (bf16[14,1,40,128]{3,2,1,0:T(8,128)(2,1)S(1)}, bf16[14,1,40,128]{3,2,1,0:T(8,128)(2,1)S(1)}, u32[]{:S(2)}, u32[]{:S(2)}) collective-permute-start(bf16[14,1,40,128]{3,2,1,0:T(8,128)(2,1)S(1)} %get-tuple-element.55), channel_id=1, source_target_pairs={{0,1},{1,0},{2,3},{3,2},{4,5},{5,4},{6,7},{7,6},{8,9},{9,8},{10,11... | collective-permute-start | bytes 430088 | tf_op jit(solution)/shard_map/ppermute | solution.py:332
  29.9 0.7 copy-start
  30.6 1.1 copy-start.4
  32.0 1.3 copy-start.5
  40.3 2.7 %collective-permute-start.9 = (bf16[4,4,2,256]{3,2,1,0:T(2,128)(2,1)S(1)}, bf16[4,4,2,256]{3,2,1,0:T(2,128)(2,1)S(1)}, u32[]{:S(2)}, u32[]{:S(2)}) collective-permute-start(bf16[4,4,2,256]{3,2,1,0:T(2,128)(2,1)S(1)} %get-tuple-element.25), channel_id=1, source_target_pairs={{0,128},{128,0},{1,129},{129,1},{2,130},{130,2},{3,131},{131,3},{4... | collective-permute-start | bytes 49160 | tf_op jit(solution)/shard_map/ppermute | solution.py:319
  43.2 5.1 %collective-permute-start.11 = (bf16[2,4,24,256]{3,2,1,0:T(8,128)(2,1)S(1)}, bf16[2,4,24,256]{3,2,1,0:T(8,128)(2,1)S(1)}, u32[]{:S(2)}, u32[]{:S(2)}) collective-permute-start(bf16[2,4,24,256]{3,2,1,0:T(8,128)(2,1)S(1)} %get-tuple-element.64), channel_id=1, source_target_pairs={{16,32},{32,16},{48,64},{64,48},{80,96},{96,80},{17,33},{33,17},{4... | collective-permute-start | bytes 294920 | tf_op jit(solution)/shard_map/ppermute | solution.py:325
  43.8 6.4 %collective-permute-start.10 = (bf16[2,4,24,256]{3,2,1,0:T(8,128)(2,1)S(1)}, bf16[2,4,24,256]{3,2,1,0:T(8,128)(2,1)S(1)}, u32[]{:S(2)}, u32[]{:S(2)}) collective-permute-start(bf16[2,4,24,256]{3,2,1,0:T(8,128)(2,1)S(1)} %get-tuple-element.65), channel_id=1, source_target_pairs={{0,16},{16,0},{32,48},{48,32},{64,80},{80,64},{96,112},{112,96},{1... | collective-permute-start | bytes 294920 | tf_op jit(solution)/shard_map/ppermute | solution.py:326
  50.4 8.2 %collective-permute-start.13 = (bf16[8,1,24,256]{3,2,1,0:T(8,128)(2,1)S(1)}, bf16[8,1,24,256]{3,2,1,0:T(8,128)(2,1)S(1)}, u32[]{:S(2)}, u32[]{:S(2)}) collective-permute-start(bf16[8,1,24,256]{3,2,1,0:T(8,128)(2,1)S(1)} %get-tuple-element.58), channel_id=1, source_target_pairs={{1,2},{2,1},{3,4},{4,3},{5,6},{6,5},{7,8},{8,7},{9,10},{10,9},{11,... | collective-permute-start | bytes 294920 | tf_op jit(solution)/shard_map/ppermute | solution.py:331
  56.3 2.3 %collective-permute-start.12 = (bf16[8,1,24,256]{3,2,1,0:T(8,128)(2,1)S(1)}, bf16[8,1,24,256]{3,2,1,0:T(8,128)(2,1)S(1)}, u32[]{:S(2)}, u32[]{:S(2)}) collective-permute-start(bf16[8,1,24,256]{3,2,1,0:T(8,128)(2,1)S(1)} %get-tuple-element.59), channel_id=1, source_target_pairs={{0,1},{1,0},{2,3},{3,2},{4,5},{5,4},{6,7},{7,6},{8,9},{9,8},{10,11... | collective-permute-start | bytes 294920 | tf_op jit(solution)/shard_map/ppermute | solution.py:332
  66.7 1.4 copy-start.6
  68.2 1.6 %collective-permute-start.14 = (bf16[1280,128]{1,0:T(8,128)(2,1)S(1)}, bf16[1280,128]{1,0:T(8,128)(2,1)S(1)}, u32[]{:S(2)}, u32[]{:S(2)}) collective-permute-start(bf16[1280,128]{1,0:T(8,128)(2,1)S(1)} %get-tuple-element.33), channel_id=1, source_target_pairs={{0,1},{1,0},{2,3},{3,2},{4,5},{5,4},{6,7},{7,6},{8,9},{9,8},{10,11... | collective-permute-start | bytes 983048 | tf_op jit(solution)/shard_map/ppermute | solution.py:405
  70.6 33.8 %all-to-all-start.1 = ((bf16[128,5,2,128]{3,2,1,0:T(2,128)(2,1)}), bf16[128,5,2,128]{3,2,1,0:T(2,128)(2,1)S(1)}, u32[]{:S(2)}, u32[]{:S(2)}) async-start(bf16[128,5,2,128]{3,2,1,0:T(2,128)(2,1)} %bitcast.22), calls=%async_computation.1 | async-start | bytes 655360 | tf_op jit(solution)/shard_map/all_to_all | solution.py:407
  89.0 1.6 %collective-permute-start.5 = (bf16[8,1,1,8,4,128]{5,3,4,1,0,2:T(8,128)(2,1)S(1)}, bf16[8,1,1,8,4,128]{5,3,4,1,0,2:T(8,128)(2,1)S(1)}, u32[]{:S(2)}, u32[]{:S(2)}) collective-permute-start(bf16[8,1,1,8,4,128]{5,3,4,1,0,2:T(8,128)(2,1)S(1)} %constant_dynamic-slice_fusion.3), channel_id=1, source_target_pairs={{0,1},{1,0},{2,3},{3,2},{4,5},{5,4},{6,7},{7,6},{8,9},{9,8},{10,11... | collective-permute-start | bytes 196616 | tf_op jit(solution)/shard_map/ppermute | solution.py:346
  105.6 22.2 %all-to-all-start.2 = ((bf16[128,5,2,128]{3,2,1,0:T(2,128)(2,1)}), bf16[128,5,2,128]{3,2,1,0:T(2,128)(2,1)}, u32[]{:S(2)}, u32[]{:S(2)}) async-start(bf16[128,5,2,128]{3,2,1,0:T(2,128)(2,1)} %broadcast_in_dim.22), calls=%async_computation.2 | async-start | bytes 655360 | tf_op jit(solution)/shard_map/all_to_all | solution.py:410
  112.8 7.4 %collective-permute-start.6 = (bf16[4,1,2,8,4,128]{5,3,4,2,1,0:T(8,128)(2,1)S(1)}, bf16[4,1,2,8,4,128]{5,3,4,2,1,0:T(8,128)(2,1)S(1)}, u32[]{:S(2)}, u32[]{:S(2)}) collective-permute-start(bf16[4,1,2,8,4,128]{5,3,4,2,1,0:T(8,128)(2,1)S(1)} %constant_dynamic-slice_fusion.2), channel_id=1, source_target_pairs={{0,2},{1,3},{2,0},{3,1},{4,6},{5,7},{6,4},{7,5},{8,10},{9,11},{10,... | collective-permute-start | bytes 196616 | tf_op jit(solution)/shard_map/ppermute | solution.py:346
  120.2 1.3 copy-start.8
  120.9 5.4 %collective-permute-start.7 = (bf16[2,1,4,8,4,128]{5,3,2,1,0,4:T(8,128)(2,1)}, bf16[2,1,4,8,4,128]{5,3,2,1,0,4:T(8,128)(2,1)}, u32[]{:S(2)}, u32[]{:S(2)}) collective-permute-start(bf16[2,1,4,8,4,128]{5,3,2,1,0,4:T(8,128)(2,1)} %constant_dynamic-slice_fusion.1), channel_id=1, source_target_pairs={{0,4},{1,5},{2,6},{3,7},{4,0},{5,1},{6,2},{7,3},{8,12},{9,13},{10,... | collective-permute-start | bytes 196616 | tf_op jit(solution)/shard_map/ppermute | solution.py:346
  121.5 0.9 copy-start.1
  122.4 0.9 copy-start.9
  127.8 19.7 %collective-permute-start.15 = (bf16[1280,128]{1,0:T(8,128)(2,1)}, bf16[1280,128]{1,0:T(8,128)(2,1)}, u32[]{:S(2)}, u32[]{:S(2)}) collective-permute-start(bf16[1280,128]{1,0:T(8,128)(2,1)} %bitcast.23.mine_ref), channel_id=1, source_target_pairs={{0,1},{1,0},{2,3},{3,2},{4,5},{5,4},{6,7},{7,6},{8,9},{9,8},{10,11... | collective-permute-start | bytes 983048 | tf_op jit(solution)/shard_map/ppermute | solution.py:411
  132.0 12.2 %collective-permute-start.8 = (bf16[1,1,8,8,4,128]{5,3,2,1,4,0:T(8,128)(2,1)}, bf16[1,1,8,8,4,128]{5,3,2,1,4,0:T(8,128)(2,1)}, u32[]{:S(2)}, u32[]{:S(2)}) collective-permute-start(bf16[1,1,8,8,4,128]{5,3,2,1,4,0:T(8,128)(2,1)} %constant_dynamic-slice_fusion), channel_id=1, source_target_pairs={{0,8},{1,9},{2,10},{3,11},{4,12},{5,13},{6,14},{7,15},{8,0},{9,1},... | collective-permute-start | bytes 196616 | tf_op jit(solution)/shard_map/ppermute | solution.py:346
  135.5 1.7 %copy-start.7 = (bf16[3,10,5,32,256]{4,3,2,1,0:T(8,128)(2,1)S(1)}, bf16[3,10,5,32,256]{4,3,2,1,0:T(8,128)(2,1)}, u32[]{:S(2)}) copy-start(bf16[3,10,5,32,256]{4,3,2,1,0:T(8,128)(2,1)} %copy-done.6) | copy-start | bytes 7372804
  139.3 0.7 copy-start.3

commit v4 on v3

--- a/solution.py
+++ b/solution.py
@@ -17,22 +17,33 @@
 TAPS = [(dx, dy) for dx in range(3) for dy in range(3)]
 
 
-def call(body, outs, scratch, *args, flops=10**8):
+def call(body, outs, scratch, *args, flops=10**8, room=8, far_args=0, far_outs=0):
     vmem = pl.BlockSpec(memory_space=pltpu.VMEM)
     smem = pl.BlockSpec(memory_space=pltpu.SMEM)
+    far = pl.BlockSpec(memory_space=pltpu.HBM)
+    near = [smem if a.dtype == jnp.int32 else vmem for a in args[: len(args) - far_args]]
+    if isinstance(outs, tuple):
+        out_specs = (vmem,) * (len(outs) - far_outs) + (far,) * far_outs
+    else:
+        out_specs = vmem
     return pl.pallas_call(
         body,
         out_shape=outs,
-        in_specs=[smem if a.dtype == jnp.int32 else vmem for a in args],
-        out_specs=jax.tree.map(lambda _: vmem, outs),
+        in_specs=near + [far] * far_args,
+        out_specs=out_specs,
         scratch_shapes=scratch,
-        compiler_params=pltpu.CompilerParams(vmem_limit_bytes=24 * 2**20),
+        compiler_params=pltpu.CompilerParams(vmem_limit_bytes=room * 2**20),
         cost_estimate=pl.CostEstimate(flops=flops, bytes_accessed=10**6, transcendentals=0),
     )(*args)
 
 
 def sds(*shape, dtype=BF16):
     return jax.ShapeDtypeStruct(shape, dtype)
+
+
+def doubled(w_ref, out_ref):
+    w = w_ref[...].astype(F32)
+    out_ref[...] = jnp.concatenate([w, w], axis=-1).astype(BF16)
 
 
 def blocks(wa_ref, wb_ref):
@@ -52,14 +63,20 @@
     return wa, wb, pair, zero_b
 
 
-def banded_ahead(wa_ref, wb_ref, a_ref, b_ref):
-    wa, wb, pair, _ = blocks(wa_ref, wb_ref)
+def banded_ahead_a(w_ref, a_ref, double_ref):
+    doubled(w_ref, double_ref)
+    wa, _, pair, _ = blocks(double_ref, None)
     for t, (dx, dy) in enumerate(TAPS):
         for zi in range(8):
             for p in range(2):
                 a_ref[t * 256 + zi * 32 : t * 256 + zi * 32 + 32, p * 128 : p * 128 + 128] = pair(
                     wa(dx, dy, zi - 2 * p - 1), wa(dx, dy, zi - 2 * p - 2)
                 )
+
+
+def banded_ahead_b(wb_ref, b_ref):
+    _, wb, _, _ = blocks(None, wb_ref)
+    for t, (dx, dy) in enumerate(TAPS):
         for zi in range(4):
             for zo in range(2):
                 b_ref[t * 256 + zi * 64 : t * 256 + zi * 64 + 64, zo * 128 : zo * 128 + 128] = wb(dx, dy, zi - zo)
@@ -99,11 +116,23 @@
     return 0.5 * jnp.tanh(0.5 * value) + 0.5
 
 
+def in_rows(v_ref, out_ref, f_ref):
+    for y in range(8):
+        f_ref[y % 2] = v_ref[:, y].astype(F32).reshape(512, 32)
+        for q in range(4):
+            columns = [f_ref[y % 2, pl.ds(4 * q + z, 32, stride=16), :] for z in range(4)]
+            out_ref[y, q] = jnp.concatenate(columns, axis=0).T.astype(BF16)
+
+
 def forward(
-    where_ref, v_ref, ynear_ref, yfar_ref, znear_ref, zfar_ref, a_ref, bias_a_ref, b_ref, bias_b_ref, cot_ref,
-    feat_ref, grad_ref, sum_ref, px_ref, vo_ref, slope_ref, face_ref,
-    f_ref, vx_ref, s_ref, p_ref, g_ref,
+    where_ref, v_ref, ynear_ref, yfar_ref, znear_ref, zfar_ref, a_ref, bias_a_ref, wb_ref, bias_b_ref, cot_ref,
+    feat_ref, grad_ref, sum_ref, px_ref, face_ref, vo_hbm, slope_hbm,
+    f_ref, vx_ref, s_ref, p_ref, g_ref, b_ref, vo_ref, slope_ref, sem,
 ):
+    banded_ahead_b(wb_ref, b_ref)
+    twice = jnp.concatenate([bias_a_ref[...], bias_a_ref[...]], axis=-1)
+    bias_a = jnp.concatenate([twice, twice], axis=-1)
+    bias_b = jnp.concatenate([bias_b_ref[...], bias_b_ref[...]], axis=-1)
     gx, gy, gz = position(where_ref)
 
     def stage(src, rows, y0, q0, nq):
@@ -114,8 +143,7 @@
 
             @pl.when(jnp.logical_and(y0 + y >= 2, y0 + y < 12))
             def _():
-                for dx in range(3):
-                    vo_ref[dx, y0 + y - 2, pl.ds(q0, nq)] = f_ref[0:nq, pl.ds(dx + 2, 32), :].astype(BF16)
+                vo_ref[y0 + y - 2, pl.ds(q0, nq)] = f_ref[0:nq, pl.ds(2, 40), :].astype(BF16)
 
             return carry
 
@@ -128,6 +156,12 @@
     stage(znear_ref, 14, 0, jnp.where(even_z, 5, 0), 1)
     stage(zfar_ref, 14, 0, jnp.where(even_z, 0, 5), 1)
 
+    save_vo = pltpu.make_async_copy(vo_ref, vo_hbm, sem.at[5])
+    save_vo.start()
+
+    def save_slope(q):
+        return pltpu.make_async_copy(slope_ref.at[q], slope_hbm.at[q], sem.at[q])
+
     fold = iota((6, 48, 128), 2) < 64
     shape = (6, 24, 128)
     x = iota(shape, 1) + (gx * 16 - 1)
@@ -141,9 +175,11 @@
             parts.append(vx_ref[dx, dy : dy + 12, q])
             parts.append(vx_ref[dx, dy : dy + 12, q + 1])
         lhs = jnp.concatenate(parts, axis=-1).reshape(576, 2304)
-        before = jnp.dot(lhs, a_ref[...], preferred_element_type=F32) + bias_a_ref[...]
+        before = jnp.dot(lhs, a_ref[...], preferred_element_type=F32) + bias_a
         s = sigmoid_of(before)
-        slope_ref[q] = (0.125 * (s * (1.0 + before * (1.0 - s)))).astype(BF16).reshape(12, 48, 256)
+        slope = (0.125 * (s * (1.0 + before * (1.0 - s)))).astype(BF16)
+        slope_ref[q] = slope.reshape(12, 48, 256)[1:11]
+        save_slope(q).start()
         act = (before * s).reshape(6, 2, 48, 256)
         rows = act[:, 0] + act[:, 1]
         lo, hi = rows[..., :128], rows[..., 128:]
@@ -164,7 +200,7 @@
         parts.append(px_ref[dx, dy : dy + 4, 0:4])
         parts.append(px_ref[dx, dy : dy + 4, 1:5])
     lhs = jnp.concatenate(parts, axis=-1).reshape(256, 2304)
-    before = jnp.dot(lhs, b_ref[...], preferred_element_type=F32) + bias_b_ref[...]
+    before = jnp.dot(lhs, b_ref[...], preferred_element_type=F32) + bias_b
     s = sigmoid_of(before)
     feat_ref[...] = (before * s).astype(BF16).reshape(4, 4, 16, 256)
     cot = cot_ref[...].reshape(256, 256).astype(F32)
@@ -177,6 +213,9 @@
         lanes = slice(h * 128, h * 128 + 128)
         g_ref[...] = wide[:, lanes].reshape(4, 4, 16, 128)
         face_ref[..., lanes] = jnp.where(gx == 0, g_ref[:, :, pl.ds(14, 2), :], g_ref[:, :, pl.ds(0, 2), :]).astype(BF16)
+    for q in range(5):
+        save_slope(q).wait()
+    save_vo.wait()
 
 
 TN = (((0,), (0,)), ((), ()))
@@ -195,10 +234,11 @@
 
 
 def backward(
-    where_ref, g_ref, ynear_ref, yfar_ref, znear_ref, zfar_ref, bt_ref, slope_ref, vo_ref, wb_ref, sum_b_ref,
-    ga_ref, keep_ref, send_ref,
-    f_ref, gx_ref, s_ref, t_ref, own_ref, flat_ref,
+    where_ref, g_ref, ynear_ref, yfar_ref, znear_ref, zfar_ref, w_ref, wb_ref, sum_b_ref, slope_ref, vo_ref,
+    keep_ref, send_ref, ga_hbm,
+    f_ref, gx_ref, s_ref, t_ref, own_ref, flat_ref, vx_ref, v_ref, bt_ref, ga_ref, sem,
 ):
+    banded_back_b(w_ref, bt_ref)
     gx, gy, gz = position(where_ref)
 
     def stage(src, rows, y0, q0, nq):
@@ -220,11 +260,22 @@
     stage(znear_ref, 8, 0, jnp.where(even_z, 5, 0), 1)
     stage(zfar_ref, 8, 0, jnp.where(even_z, 0, 5), 1)
 
-    shape = (12, 48, 128)
+    def stage_v(y, carry):
+        v_ref[...] = vo_ref[y].astype(F32)
+        for dx in range(3):
+            vx_ref[dx, y] = v_ref[:, pl.ds(dx, 32), :].astype(BF16)
+        return carry
+
+    lax.fori_loop(0, 10, stage_v, 0)
+
+    shape = (10, 48, 128)
     x = iota(shape, 1) + (gx * 32 - 2)
-    y = iota(shape, 0) + (gy * 8 - 2)
+    y = iota(shape, 0) + (gy * 8 - 1)
     zlane = iota(shape, 2) // 64
     inside_xy = (x >= 0) & (x < 64) & (y >= 0) & (y < 64)
+
+    def save_ga(q):
+        return pltpu.make_async_copy(ga_ref.at[q], ga_hbm.at[q], sem.at[q])
 
     def conv_b(q, total):
         parts = []
@@ -239,16 +290,16 @@
             half = pooled[..., h * 128 : h * 128 + 128]
             s_ref[:, pl.ds(0, 24, stride=2), :] = half
             s_ref[:, pl.ds(1, 24, stride=2), :] = half
-            spread = jnp.broadcast_to(s_ref[...].reshape(6, 1, 48, 128), (6, 2, 48, 128)).reshape(12, 48, 128)
+            spread = jnp.broadcast_to(s_ref[...].reshape(6, 1, 48, 128), (6, 2, 48, 128)).reshape(12, 48, 128)[1:11]
             z = zlane + (gz * 16 - 2 + 4 * q + 2 * h)
             slope = slope_ref[q, :, :, h * 128 : h * 128 + 128].astype(F32)
             t_ref[...] = jnp.where(inside_xy & (z >= 0) & (z < 256), spread * slope, 0.0)
-            for dx in range(3):
-                ga_ref[dx, :, q, :, h * 128 : h * 128 + 128] = t_ref[1:11, pl.ds(dx + 1, 32), :].astype(BF16)
+            ga_ref[q, :, :, h * 128 : h * 128 + 128] = t_ref[:, pl.ds(1, 40), :].astype(BF16)
             keep = jnp.where(q == 4 * h, 0.0, 1.0)
-            own = (t_ref[2:10, pl.ds(2, 32), :] * keep).astype(BF16)
+            own = (t_ref[1:9, pl.ds(2, 32), :] * keep).astype(BF16)
             own_ref[:, q, :, h * 128 : h * 128 + 128] = own
             sums.append(jnp.sum(own.astype(F32).reshape(256, 128), axis=0, keepdims=True))
+        save_ga(q).start()
         return total + sums[0] + sums[1]
 
     total = lax.fori_loop(0, 5, conv_b, jnp.zeros((1, 128), F32))
@@ -260,7 +311,7 @@
 
     flat = own_ref[...].reshape(1280, 256).T
     for t, (dx, dy) in enumerate(TAPS):
-        cells = jnp.concatenate([vo_ref[dx, dy : dy + 8, 0:5], vo_ref[dx, dy : dy + 8, 1:6]], axis=-1)
+        cells = jnp.concatenate([vx_ref[dx, dy : dy + 8, 0:5], vx_ref[dx, dy : dy + 8, 1:6]], axis=-1)
         terms = jnp.dot(flat, cells.reshape(1280, 256), preferred_element_type=F32)
         block = terms[0:64]
         for zo in range(1, 4):
@@ -271,6 +322,8 @@
     rest = pl.multiple_of((1 - gz % 2) * 1280, 1280)
     keep_ref[...] = flat_ref[pl.ds(half, 1280), :]
     send_ref[...] = flat_ref[pl.ds(rest, 1280), :]
+    for q in range(5):
+        save_ga(q).wait()
 
 
 def finish(scale_a, scale_b, where_ref, mine_ref, other_ref, wa_ref, ba_ref, wb_ref, bb_ref):
@@ -296,12 +349,29 @@
         put(other_ref, mine_ref)
 
 
-def input_grad(ga_ref, at_ref, out_ref):
+def spread_sum(shares_ref, out_ref):
+    total = jnp.sum(shares_ref[...].astype(F32), axis=0, keepdims=True).astype(BF16)
+    out_ref[...] = jnp.broadcast_to(total, out_ref.shape)
+
+
+def input_grad(ga_ref, wa_ref, out_ref, f_ref, gx_ref, w_ref, at_ref):
+    doubled(wa_ref, w_ref)
+    banded_back_a(w_ref, at_ref)
+
+    def stage(y, carry):
+        for h in range(2):
+            lanes = slice(h * 128, h * 128 + 128)
+            f_ref[...] = ga_ref[:, y, :, lanes].astype(F32)
+            for dx in range(3):
+                gx_ref[dx, y, :, :, lanes] = f_ref[:, pl.ds(dx, 32), :].astype(BF16)
+        return carry
+
+    lax.fori_loop(0, 10, stage, 0)
     for h in range(2):
         parts = []
         for dx, dy in TAPS:
             for j in range(3):
-                parts.append(ga_ref[dx, dy : dy + 8, 2 * h + j])
+                parts.append(gx_ref[dx, dy : dy + 8, 2 * h + j])
         lhs = jnp.concatenate(parts, axis=-1).reshape(256, 6912)
         value = lax.dot_general(lhs, at_ref[...], NT, preferred_element_type=F32)
         out_ref[:, h] = value.astype(BF16).reshape(8, 32, 256)
@@ -311,40 +381,47 @@
     count = lax.axis_size(axis)
     near = [(i, i ^ 1) for i in range(count)]
     far = [(i, i + 1 if i % 2 else i - 1) for i in range(1, count - 1)]
-    return lax.axis_index(axis) % 2 == 0, near, far
-
-
-def halo(block, face, width, x_rows):
-    first = lax.axis_index("gx") == 0
+    return near, far
+
+
+def places():
+    index = lax.axis_index(GZ)
+    bits = tuple((1 - (index >> b) % 2).astype(jnp.uint32) for b in range(4))
+    odd = tuple(lax.axis_index(axis) % 2 == 0 for axis in ("gx", "gy", GZ))
+    return lax.axis_index(ALL).astype(jnp.int32).reshape(1), odd, bits
+
+
+def halo(block, face, width, x_rows, evens):
+    first, even, even_z = evens
     got = lax.ppermute(face, "gx", [(0, 1), (1, 0)])
     none = jnp.zeros_like(got)
     rest = jnp.zeros(block.shape[:2] + (x_rows - block.shape[2] - 2 * width,) + block.shape[3:], block.dtype)
     wide = jnp.concatenate([jnp.where(first, none, got), block, jnp.where(first, got, none), rest], axis=2)
-    even, near, far = swaps("gy")
+    near, far = swaps("gy")
     low, high = wide[:width], wide[wide.shape[0] - width :]
     yfar = lax.ppermute(jnp.where(even, low, high), "gy", far)
     ynear = lax.ppermute(jnp.where(even, high, low), "gy", near)
     ylo, yhi = jnp.where(even, yfar, ynear), jnp.where(even, ynear, yfar)
-    even, near, far = swaps(GZ)
+    near, far = swaps(GZ)
     last = jnp.concatenate([ylo[:, 3:], wide[:, 3:], yhi[:, 3:]], axis=0)
     head = jnp.concatenate([ylo[:, :1], wide[:, :1], yhi[:, :1]], axis=0)
-    zfar = lax.ppermute(jnp.where(even, head, last), GZ, far)
-    znear = lax.ppermute(jnp.where(even, last, head), GZ, near)
+    zfar = lax.ppermute(jnp.where(even_z, head, last), GZ, far)
+    znear = lax.ppermute(jnp.where(even_z, last, head), GZ, near)
     return wide, ynear, yfar, znear, zfar
 
 
 CHIPS = ("gx", "gy", "gz_0")
 
 
-def to_slabs(pieces):
-    index = lax.axis_index(GZ)
+def to_slabs(pieces, others):
     shape = pieces.shape
-    for b in range(4):
-        other = 1 - (index >> b) % 2
+    zero = jnp.zeros((), jnp.uint32)
+    for b, other in enumerate(others):
         pieces = pieces.reshape((16 >> (b + 1), 2, 1 << b) + shape[1:])
-        part = lax.dynamic_index_in_dim(pieces, other, 1)
+        start = (zero, other) + (zero,) * (pieces.ndim - 2)
+        part = lax.dynamic_slice(pieces, start, pieces.shape[:1] + (1,) + pieces.shape[2:])
         got = lax.ppermute(part, GZ, [(i, i ^ (1 << b)) for i in range(16)])
-        pieces = lax.dynamic_update_slice_in_dim(pieces, got, other, 1)
+        pieces = lax.dynamic_update_slice(pieces, got, start)
     return pieces.reshape(shape)
 
 
@@ -352,52 +429,55 @@
     cells_fine = 64 * 64 * 256
     scale_a = 1.0 / math.sqrt(cells_fine)
     scale_b = 1.0 / math.sqrt(cells_fine // 8)
-    where = lax.axis_index(ALL).astype(jnp.int32).reshape(1)
-
-    v = jnp.transpose(volume.reshape(32, 32, 8, 4, 4), (2, 3, 1, 4, 0)).reshape(8, 4, 32, 128)
-    face = jnp.where(lax.axis_index("gx") == 0, v[:, :, 29:32], v[:, :, 0:3])
-    sides = halo(v, face, 3, 40)
+    volume, cotangent, (where, evens, others) = lax.optimization_barrier((volume, cotangent, places()))
+
+    v = call(
+        in_rows, sds(8, 4, 32, 128), [pltpu.VMEM((2, 512, 32), F32)], jnp.transpose(volume, (0, 2, 3, 1)), flops=10**6
+    )
+    face = jnp.where(evens[0], v[:, :, 29:32], v[:, :, 0:3])
+    sides = halo(v, face, 3, 40, evens)
 
     cot = jnp.transpose(cotangent[:, 0], (2, 1, 0)).reshape(16, 8, 4, 128)
     cot = lax.all_to_all(cot, GZ, 0, 0, tiled=True)
     cot = jnp.transpose(cot.reshape(16, 4, 2, 4, 128), (3, 1, 0, 2, 4)).reshape(4, 4, 16, 256)
 
     wa27 = weight_a.reshape(27, 32, 64)
-    wa27 = jnp.concatenate([wa27, wa27], axis=-1)
     wb27 = weight_b.reshape(27, 64, 128)
-    m_a, m_b = call(banded_ahead, (sds(2304, 256), sds(2304, 256)), [], wa27, wb27, flops=10**7)
-    m_bt = call(banded_back_b, sds(256, 4608), [], wb27, flops=10**7)
-    m_at = call(banded_back_a, sds(256, 6912), [], wa27, flops=10**7)
-
-    feat, grad_b, sum_b, px, vo, slope, face_b = call(
+
+    m_a = call(banded_ahead_a, sds(2304, 256), [pltpu.VMEM((27, 32, 128), BF16)], wa27, flops=10**7)
+
+    feat, grad_b, sum_b, px, face_b, vo, slope = call(
         forward,
         (
-            sds(4, 4, 16, 256), sds(4, 4, 16, 256), sds(1, 128, dtype=F32),
-            sds(3, 6, 5, 16, 128), sds(3, 10, 6, 32, 128), sds(5, 12, 48, 256),
-            sds(4, 4, 2, 256),
+            sds(4, 4, 16, 256), sds(4, 4, 16, 256), sds(1, 128, dtype=F32), sds(3, 6, 5, 16, 128), sds(4, 4, 2, 256),
+            pltpu.HBM((10, 6, 40, 128), BF16), pltpu.HBM((5, 10, 48, 256), BF16),
         ),
         [
             pltpu.VMEM((4, 56, 128), F32), pltpu.VMEM((3, 14, 6, 48, 128), BF16),
             pltpu.VMEM((6, 48, 128), F32), pltpu.VMEM((6, 24, 128), F32), pltpu.VMEM((4, 4, 16, 128), F32),
+            pltpu.VMEM((2304, 256), BF16),
+            pltpu.VMEM((10, 6, 40, 128), BF16), pltpu.VMEM((5, 10, 48, 256), BF16), pltpu.SemaphoreType.DMA((6,)),
         ],
-        where, *sides, m_a, jnp.tile(bias_a, 4).reshape(1, 256), m_b, jnp.tile(bias_b, 2).reshape(1, 256), cot,
-        flops=2 * 10**9,
-    )
-
-    sides_b = halo(grad_b, face_b, 2, 24)
+        where, *sides, m_a, bias_a.reshape(1, 64), wb27, bias_b.reshape(1, 128), cot,
+        flops=2 * 10**9, room=24, far_outs=2,
+    )
+
+    sides_b = halo(grad_b, face_b, 2, 24, evens)
     wb = call(weight_b_terms, sds(27, 64, 128), [], px, grad_b, flops=10**9)
 
     out = jnp.transpose(feat.reshape(4, 4, 16, 2, 128), (2, 1, 3, 0, 4)).reshape(16, 8, 4, 128)
 
-    ga, keep, send = call(
+    keep, send, ga = call(
         backward,
-        (sds(3, 10, 5, 32, 256), sds(1280, 128), sds(1280, 128)),
+        (sds(1280, 128), sds(1280, 128), pltpu.HBM((5, 10, 40, 256), BF16)),
         [
             pltpu.VMEM((2, 4, 40, 128), F32), pltpu.VMEM((3, 8, 6, 32, 256), BF16),
-            pltpu.VMEM((6, 48, 128), F32), pltpu.VMEM((12, 48, 128), F32), pltpu.VMEM((8, 5, 32, 256), BF16),
-            pltpu.VMEM((2560, 128), BF16),
+            pltpu.VMEM((6, 48, 128), F32), pltpu.VMEM((10, 48, 128), F32), pltpu.VMEM((8, 5, 32, 256), BF16),
+            pltpu.VMEM((2560, 128), BF16), pltpu.VMEM((3, 10, 6, 32, 128), BF16), pltpu.VMEM((6, 40, 128), F32),
+            pltpu.VMEM((256, 4608), BF16),
+            pltpu.VMEM((5, 10, 40, 256), BF16), pltpu.SemaphoreType.DMA((5,)),
         ],
-        where, *sides_b, m_bt, slope, vo, wb, sum_b, flops=2 * 10**9,
+        where, *sides_b, wb27, wb, sum_b, slope, vo, flops=2 * 10**9, room=24, far_outs=1,
     )
 
     flip = [(0, 1), (1, 0)]
@@ -405,13 +485,16 @@
     got = lax.ppermute(send, "gz_1", flip)
     chip = (keep.astype(F32) + got.astype(F32)).astype(BF16)
     shares = lax.all_to_all(chip.reshape(count, 5, 2, 128), CHIPS, 0, 0, tiled=True)
-    share = jnp.sum(shares.astype(F32), axis=0).astype(BF16)
-    spread = jnp.broadcast_to(share[None], (count, 5, 2, 128))
+    spread = call(spread_sum, sds(count, 5, 2, 128), [], shares, flops=10**6)
     mine = lax.all_to_all(spread, CHIPS, 0, 0, tiled=True).reshape(count * 10, 128)
     other = lax.ppermute(mine, "gz_1", flip)
-    features = jnp.transpose(to_slabs(out).reshape(128, 4, 128), (2, 1, 0)).reshape(128, 1, 4, 128)
-
-    gi = call(input_grad, sds(8, 2, 32, 256), [], ga, m_at, flops=2 * 10**9)
+    features = jnp.transpose(to_slabs(out, others).reshape(128, 4, 128), (2, 1, 0)).reshape(128, 1, 4, 128)
+
+    gi = call(
+        input_grad, sds(8, 2, 32, 256), [pltpu.VMEM((5, 40, 128), F32), pltpu.VMEM((3, 10, 5, 32, 256), BF16),
+         pltpu.VMEM((27, 32, 128), BF16), pltpu.VMEM((256, 6912), BF16)],
+        ga, wa27, flops=2 * 10**9, room=16,
+    )
     gi = jnp.transpose(gi.reshape(8, 2, 32, 8, 32), (4, 2, 0, 1, 3)).reshape(32, 32, 8, 16)
 
     total_wa, total_ba, total_wb, total_bb = call(

time: 151 us -> 138 us (0.914)
  local copies, waits for them, and re-layouts: 26.1 us -> 6.69 us
  waiting for transfers between devices: 34.4 us -> 42.3 us
  starting transfers between devices: 65.3 us -> 63.2 us
  Pallas kernels: 21.1 us -> 22.8 us
    unnamed x30 -> x19, local copies, waits for them, and re-layouts: 10.1 us -> 2.06 us
    ppermute x4, waiting for transfers between devices: 10.1 us -> 13.8 us  [to_slabs(): got = lax.ppermute(part, GZ, [(i, i ^ 1 << b) for i in range(16)])]
    reshape x2 -> x0, local copies, waits for them, and re-layouts: 3.59 us -> none  [the longest x1 3.09 us: on_device(): volume.reshape(32, 32, 8, 4, 4)]
    dynamic_update_slice x4, local copies, waits for them, and re-layouts: 2.99 us -> 0.05 us  [to_slabs(): pieces = lax.dynamic_update_slice(pieces, got, start)]
    ppermute x4, waiting for transfers between devices: 1.39 us -> 3.75 us  [the longest x2 3.74 us: halo(): zfar = lax.ppermute(jnp.where(even_z, head, last), GZ, far)]
    dynamic_slice x4, local copies, waits for them, and re-layouts: 2.16 us -> 0.05 us  [to_slabs(): lax.dynamic_slice(pieces, start, pieces.shape[:1] + (1,) + pieces.shape[2:])]
    ppermute x4, starting transfers between devices: 5.32 us -> 3.44 us  [to_slabs(): got = lax.ppermute(part, GZ, [(i, i ^ 1 << b) for i in range(16)])]
    pallas_call x8, Pallas kernels: 21.1 us -> 22.8 us  [call(): pl.pallas_call(body, out_shape=outs, in_specs=near + [far] * far_args, ou...]
  transfers between devices with their start and end apart: 19 -> 19, of which waited for: 9 -> 12; matrix products, arithmetic and copies ran while one was open for 9% -> 4% of each run, Pallas kernels for 2% -> 3%
where the time goes in v4:
time: 138 us; the launch traced here: 137 us
  starting transfers between devices  63.2 us (46%)
  waiting for transfers between devices  42.3 us (31%)
  Pallas kernels  22.8 us (17%)
  local copies, waits for them, and re-layouts  6.69 us (5%)
  other arithmetic  1.39 us (1%)
    pallas_call x8, Pallas kernels, call(): pl.pallas_call(body, out_shape=outs, in_specs=near + [far] * far_args, ou...  22.8 us
    all_to_all x1, starting transfers between devices, on_device(): lax.all_to_all(chip.reshape(count, 5, 2, 128), CHIPS, 0, 0, tiled=True)  18.2 us
    ppermute x4, waiting for transfers between devices, to_slabs(): got = lax.ppermute(part, GZ, [(i, i ^ 1 << b) for i in range(16)])  13.8 us
    all_to_all x1, waiting for transfers between devices, on_device(): lax.all_to_all(chip.reshape(count, 5, 2, 128), CHIPS, 0, 0, tiled=True)  13.7 us
    all_to_all x1, starting transfers between devices, on_device(): cot = lax.all_to_all(cot, GZ, 0, 0, tiled=True)  9.43 us
    ppermute x2, starting transfers between devices, halo(): zfar = lax.ppermute(jnp.where(even_z, head, last), GZ, far)  9.26 us
    ppermute x2, starting transfers between devices, halo(): ynear = lax.ppermute(jnp.where(even, high, low), 'gy', near)  8.36 us
    ppermute x2, waiting for transfers between devices, halo(): ynear = lax.ppermute(jnp.where(even, high, low), 'gy', near)  6.2 us
  transfers between devices with their start and end apart: 19, of which 12 were waited for; matrix products, arithmetic and copies ran while one was open for 4% of the time, Pallas kernels for 3%

profile of v4, /device:TPU:1, one launch (start us, length us, event | category | flops | bytes accessed | tf_op | source)
XLA Modules:
  0.0 137.4 jit_solution(13013276952975119512)
XLA Ops:
  0.7 1.2 copy-done
  1.9 0.7 shard_map.109
  2.7 2.1 %collective-permute-start = (bf16[8,4,3,128]{3,2,1,0:T(4,128)(2,1)S(1)}, bf16[8,4,3,128]{3,2,1,0:T(4,128)(2,1)S(1)}, u32[]{:S(2)}, u32[]{:S(2)}) collective-permute-start(bf16[8,4,3,128]{3,2,1,0:T(4,128)(2,1)S(1)} %slice_select_fusion), channel_id=1, source_target_pairs={{0,128},{128,0},{1,129},{129,1},{2,130},{130,2},{3,131},{131,3},{4... | collective-permute-start | bytes 73736 | tf_op jit(solution)/shard_map/ppermute | solution.py:396
  4.8 0.1 copy.21
  5.0 0.7 copy.22
  5.7 9.4 %all-to-all-start = ((bf16[16,8,4,128]{3,1,2,0:T(8,128)(2,1)}), bf16[16,8,4,128]{3,1,2,0:T(8,128)(2,1)S(1)}, u32[]{:S(2)}, u32[]{:S(2)}) async-start(bf16[16,8,4,128]{3,1,2,0:T(8,128)(2,1)} %copy.22), calls=%async_computation | async-start | bytes 262144 | tf_op jit(solution)/shard_map/all_to_all | solution.py:441
  15.2 0.2 maximum_maximum_fusion.v_ref
  15.5 0.8 collective-permute-start.2
  16.3 3.9 %collective-permute-start.1 = (bf16[3,4,40,128]{3,2,1,0:T(8,128)(2,1)S(1)}, bf16[3,4,40,128]{3,2,1,0:T(8,128)(2,1)S(1)}, u32[]{:S(2)}, u32[]{:S(2)}) collective-permute-start(bf16[3,4,40,128]{3,2,1,0:T(8,128)(2,1)S(1)} %get-tuple-element.69), channel_id=1, source_target_pairs={{0,16},{16,0},{32,48},{48,32},{64,80},{80,64},{96,112},{112,96},{1... | collective-permute-start | bytes 368648 | tf_op jit(solution)/shard_map/ppermute | solution.py:403
  20.2 3.3 %collective-permute-done.1.ynear_ref = bf16[3,4,40,128]{3,2,1,0:T(8,128)(2,1)S(1)} collective-permute-done((bf16[3,4,40,128]{3,2,1,0:T(8,128)(2,1)S(1)}, bf16[3,4,40,128]{3,2,1,0:T(8,128)(2,1)S(1)}, u32[]{:S(2)}, u32[]{:S(2)}) %collective-permute-start.1) | collective-permute-done | bytes 122912 | tf_op jit(solution)/shard_map/ppermute | solution.py:403
  23.6 4.2 %collective-permute-start.4 = (bf16[14,1,40,128]{3,2,1,0:T(8,128)(2,1)S(1)}, bf16[14,1,40,128]{3,2,1,0:T(8,128)(2,1)S(1)}, u32[]{:S(2)}, u32[]{:S(2)}) collective-permute-start(bf16[14,1,40,128]{3,2,1,0:T(8,128)(2,1)S(1)} %get-tuple-element.70), channel_id=1, source_target_pairs={{1,2},{2,1},{3,4},{4,3},{5,6},{6,5},{7,8},{8,7},{9,10},{10,9},{11,... | collective-permute-start | bytes 430088 | tf_op jit(solution)/shard_map/ppermute | solution.py:408
  27.9 0.1 collective-permute-start.3
  28.0 0.2 shard_map.110.a_ref
  28.3 0.1 copy.24
  28.6 2.1 %collective-permute-done.4.zfar_ref = bf16[14,1,40,128]{3,2,1,0:T(8,128)(2,1)S(1)} collective-permute-done((bf16[14,1,40,128]{3,2,1,0:T(8,128)(2,1)S(1)}, bf16[14,1,40,128]{3,2,1,0:T(8,128)(2,1)S(1)}, u32[]{:S(2)}, u32[]{:S(2)}) %collective-permute-start.4) | collective-permute-done | bytes 143392 | tf_op jit(solution)/shard_map/ppermute | solution.py:408
  30.7 7.1 %shard_map.111 = (bf16[4,4,16,256]{3,2,1,0:T(8,128)(2,1)S(1)}, bf16[4,4,16,256]{3,2,1,0:T(8,128)(2,1)S(1)}, f32[1,128]{1,0:T(1,128)S(1)}, bf16[3,6,5,16,128]{4,3...) custom-call(s32[1]{0:T(128)} %bitcast.where_ref, ...), custom_call_target="tpu_custom_call" | custom-call | flops 2000000000 | bytes 1000000 | tf_op jit(solution)/shard_map/pallas_call | solution.py:29
  37.8 0.3 collective-permute-start.9
  38.3 2.3 %collective-permute-done.9 = bf16[4,4,2,256]{3,2,1,0:T(2,128)(2,1)S(1)} collective-permute-done((bf16[4,4,2,256]{3,2,1,0:T(2,128)(2,1)S(1)}, bf16[4,4,2,256]{3,2,1,0:T(2,128)(2,1)S(1)}, u32[]{:S(2)}, u32[]{:S(2)}) %collective-permute-start.9) | collective-permute-done | bytes 16416 | tf_op jit(solution)/shard_map/ppermute | solution.py:396
  40.5 0.1 maximum_maximum_fusion.1.g_ref
  40.7 0.7 collective-permute-start.11
  41.4 4.4 %collective-permute-start.10 = (bf16[2,4,24,256]{3,2,1,0:T(8,128)(2,1)S(1)}, bf16[2,4,24,256]{3,2,1,0:T(8,128)(2,1)S(1)}, u32[]{:S(2)}, u32[]{:S(2)}) collective-permute-start(bf16[2,4,24,256]{3,2,1,0:T(8,128)(2,1)S(1)} %get-tuple-element.81), channel_id=1, source_target_pairs={{0,16},{16,0},{32,48},{48,32},{64,80},{80,64},{96,112},{112,96},{1... | collective-permute-start | bytes 294920 | tf_op jit(solution)/shard_map/ppermute | solution.py:403
  45.8 2.9 %collective-permute-done.10.ynear_ref = bf16[2,4,24,256]{3,2,1,0:T(8,128)(2,1)S(1)} collective-permute-done((bf16[2,4,24,256]{3,2,1,0:T(8,128)(2,1)S(1)}, bf16[2,4,24,256]{3,2,1,0:T(8,128)(2,1)S(1)}, u32[]{:S(2)}, u32[]{:S(2)}) %collective-permute-start.10) | collective-permute-done | bytes 98336 | tf_op jit(solution)/shard_map/ppermute | solution.py:403
  48.8 5.0 %collective-permute-start.13 = (bf16[8,1,24,256]{3,2,1,0:T(8,128)(2,1)S(1)}, bf16[8,1,24,256]{3,2,1,0:T(8,128)(2,1)S(1)}, u32[]{:S(2)}, u32[]{:S(2)}) collective-permute-start(bf16[8,1,24,256]{3,2,1,0:T(8,128)(2,1)S(1)} %get-tuple-element.74), channel_id=1, source_target_pairs={{1,2},{2,1},{3,4},{4,3},{5,6},{6,5},{7,8},{8,7},{9,10},{10,9},{11,... | collective-permute-start | bytes 294920 | tf_op jit(solution)/shard_map/ppermute | solution.py:408
  53.8 0.1 collective-permute-start.12
  54.0 0.5 shard_map.112.wb_ref
  54.5 1.6 %collective-permute-done.13.zfar_ref = bf16[8,1,24,256]{3,2,1,0:T(8,128)(2,1)S(1)} collective-permute-done((bf16[8,1,24,256]{3,2,1,0:T(8,128)(2,1)S(1)}, bf16[8,1,24,256]{3,2,1,0:T(8,128)(2,1)S(1)}, u32[]{:S(2)}, u32[]{:S(2)}) %collective-permute-start.13) | collective-permute-done | bytes 98336 | tf_op jit(solution)/shard_map/ppermute | solution.py:408
  56.1 8.6 %shard_map.113 = (bf16[1280,128]{1,0:T(8,128)(2,1)S(1)}, bf16[1280,128]{1,0:T(8,128)(2,1)S(1)}, bf16[5,10,40,256]{3,2,1,0:T(8,128)(2,1)}) custom-call(s32[1]{0:T(128)} %bitcast.where_ref, bf16[4,4,24,256]{3,2,1,0:T(8,128)(2,1)S(1)} %maximum_maximum_fusion.1.g_ref, bf16[2,4,24,256]{3,2,1,0:T(8,128)(2,1)S(1)} %collective-permute-done.10.ynear_ref, ...), custom_call_target="tpu_custom_call" | custom-call | flops 2000000000 | bytes 1000000 | tf_op jit(solution)/shard_map/pallas_call | solution.py:29
  64.9 1.6 %collective-permute-done.14 = bf16[1280,128]{1,0:T(8,128)(2,1)S(1)} collective-permute-done((bf16[1280,128]{1,0:T(8,128)(2,1)S(1)}, bf16[1280,128]{1,0:T(8,128)(2,1)S(1)}, u32[]{:S(2)}, u32[]{:S(2)}) %collective-permute-start.14) | collective-permute-done | bytes 327712 | tf_op jit(solution)/shard_map/ppermute | solution.py:485
  66.5 0.8 add_convert_fusion
  67.3 18.2 %all-to-all-start.1 = ((bf16[128,5,2,128]{3,2,1,0:T(2,128)(2,1)}), bf16[128,5,2,128]{3,2,1,0:T(2,128)(2,1)S(1)}, u32[]{:S(2)}, u32[]{:S(2)}) async-start(bf16[128,5,2,128]{3,2,1,0:T(2,128)(2,1)} %bitcast.22), calls=%async_computation.1 | async-start | bytes 655360 | tf_op jit(solution)/shard_map/all_to_all | solution.py:487
  85.7 0.7 collective-permute-start.5
  86.4 0.9 collective-permute-done.5
  87.3 13.7 %all-to-all-done.1.shares_ref = bf16[128,5,2,128]{3,2,1,0:T(2,128)(2,1)S(1)} async-done(((bf16[128,5,2,128]{3,2,1,0:T(2,128)(2,1)}), bf16[128,5,2,128]{3,2,1,0:T(2,128)(2,1)S(1)}, u32[]{:S(2)}, u32[]{:S(2)}) %all-to-all-start.1) | async-done | bytes 327712 | tf_op jit(solution)/shard_map/all_to_all | solution.py:487
  101.1 1.2 shard_map.115
  102.2 6.2 %all-to-all-start.2 = ((bf16[128,5,2,128]{3,2,1,0:T(2,128)(2,1)}), bf16[128,5,2,128]{3,2,1,0:T(2,128)(2,1)S(1)}, u32[]{:S(2)}, u32[]{:S(2)}) async-start(bf16[128,5,2,128]{3,2,1,0:T(2,128)(2,1)} %shard_map.115), calls=%async_computation.2 | async-start | bytes 655360 | tf_op jit(solution)/shard_map/all_to_all | solution.py:489
  108.4 0.5 collective-permute-start.6
  109.0 7.2 %collective-permute-done.6 = bf16[4,1,2,8,4,128]{5,3,4,2,1,0:T(8,128)(2,1)S(1)} collective-permute-done((bf16[4,1,2,8,4,128]{5,3,4,2,1,0:T(8,128)(2,1)S(1)}, bf16[4,1,2,8,4,128]{5,3,4,2,1,0:T(8,128)(2,1)S(1)}, u32[]{:S(2)}, u32[]{:S(2)}) %collective-permute-start.6) | collective-permute-done | bytes 65568 | tf_op jit(solution)/shard_map/ppermute | solution.py:423
  116.2 0.8 collective-permute-start.7
  117.0 4.5 %collective-permute-done.7 = bf16[2,1,4,8,4,128]{5,3,2,1,0,4:T(8,128)(2,1)S(1)} collective-permute-done((bf16[2,1,4,8,4,128]{5,3,2,1,0,4:T(8,128)(2,1)S(1)}, bf16[2,1,4,8,4,128]{5,3,2,1,0,4:T(8,128)(2,1)S(1)}, u32[]{:S(2)}, u32[]{:S(2)}) %collective-permute-start.7) | collective-permute-done | bytes 65568 | tf_op jit(solution)/shard_map/ppermute | solution.py:423
  121.5 0.9 all-to-all-done.2
  122.4 4.1 %collective-permute-start.15 = (bf16[1280,128]{1,0:T(8,128)(2,1)S(1)}, bf16[1280,128]{1,0:T(8,128)(2,1)S(1)}, u32[]{:S(2)}, u32[]{:S(2)}) collective-permute-start(bf16[1280,128]{1,0:T(8,128)(2,1)S(1)} %bitcast.37), channel_id=1, source_target_pairs={{0,1},{1,0},{2,3},{3,2},{4,5},{5,4},{6,7},{7,6},{8,9},{9,8},{10,11... | collective-permute-start | bytes 983048 | tf_op jit(solution)/shard_map/ppermute | solution.py:490
  126.6 1.4 collective-permute-start.8
  127.9 3.1 %shard_map.114 = bf16[8,2,32,256]{3,2,1,0:T(8,128)(2,1)S(1)} custom-call(bf16[5,10,40,256]{3,2,1,0:T(8,128)(2,1)S(1)} %copy-done.6, bf16[27,32,64]{2,1,0:T(8,128)(2,1)S(1)} %bitcast.41), custom_call_target="tpu_custom_call" | custom-call | flops 2000000000 | bytes 1000000 | tf_op jit(solution)/shard_map/pallas_call | solution.py:29
  131.0 0.4 reshape.392
  131.4 2.6 %copy.28 = bf16[32,32,8,2,8]{1,4,3,2,0:T(8,128)(2,1)} copy(bf16[32,32,8,2,8]{0,4,1,3,2:T(8,128)(2,1)S(1)} %bitcast.46) | data formatting | bytes 524288 | tf_op jit(solution)/shard_map/transpose | solution.py:498
  134.1 1.2 collective-permute-done.8
  135.3 0.8 copy.29
  136.1 1.3 shard_map.116
  (56 shorter events, 1.0 us)
Async XLA Ops:
  0.6 4.2 %copy-start.8 = (bf16[128,1,4,128]{3,2,1,0:T(4,128)(2,1)S(1)}, bf16[128,1,4,128]{3,2,1,0:T(4,128)(2,1)}, u32[]{:S(2)}) copy-start(bf16[128,1,4,128]{3,2,1,0:T(4,128)(2,1)} %param.11) | copy-start | bytes 393220
  0.7 1.2 copy-start
  2.7 12.5 %collective-permute-start = (bf16[8,4,3,128]{3,2,1,0:T(4,128)(2,1)S(1)}, bf16[8,4,3,128]{3,2,1,0:T(4,128)(2,1)S(1)}, u32[]{:S(2)}, u32[]{:S(2)}) collective-permute-start(bf16[8,4,3,128]{3,2,1,0:T(4,128)(2,1)S(1)} %slice_select_fusion), channel_id=1, source_target_pairs={{0,128},{128,0},{1,129},{129,1},{2,130},{130,2},{3,131},{131,3},{4... | collective-permute-start | bytes 73736 | tf_op jit(solution)/shard_map/ppermute | solution.py:396
  5.7 22.6 %all-to-all-start = ((bf16[16,8,4,128]{3,1,2,0:T(8,128)(2,1)}), bf16[16,8,4,128]{3,1,2,0:T(8,128)(2,1)S(1)}, u32[]{:S(2)}, u32[]{:S(2)}) async-start(bf16[16,8,4,128]{3,1,2,0:T(8,128)(2,1)} %copy.22), calls=%async_computation | async-start | bytes 262144 | tf_op jit(solution)/shard_map/all_to_all | solution.py:441
  15.4 12.6 %copy-start.1 = (bf16[3,3,3,32,64]{4,3,2,1,0:T(8,128)(2,1)S(1)}, bf16[3,3,3,32,64]{4,3,2,1,0:T(8,128)(2,1)}, u32[]{:S(2)}) copy-start(bf16[3,3,3,32,64]{4,3,2,1,0:T(8,128)(2,1)} %param.7) | copy-start | bytes 331780
  15.5 4.7 %collective-permute-start.2 = (bf16[3,4,40,128]{3,2,1,0:T(8,128)(2,1)S(1)}, bf16[3,4,40,128]{3,2,1,0:T(8,128)(2,1)S(1)}, u32[]{:S(2)}, u32[]{:S(2)}) collective-permute-start(bf16[3,4,40,128]{3,2,1,0:T(8,128)(2,1)S(1)} %get-tuple-element.68), channel_id=1, source_target_pairs={{16,32},{32,16},{48,64},{64,48},{80,96},{96,80},{17,33},{33,17},{4... | collective-permute-start | bytes 368648 | tf_op jit(solution)/shard_map/ppermute | solution.py:402
  16.3 7.2 %collective-permute-start.1 = (bf16[3,4,40,128]{3,2,1,0:T(8,128)(2,1)S(1)}, bf16[3,4,40,128]{3,2,1,0:T(8,128)(2,1)S(1)}, u32[]{:S(2)}, u32[]{:S(2)}) collective-permute-start(bf16[3,4,40,128]{3,2,1,0:T(8,128)(2,1)S(1)} %get-tuple-element.69), channel_id=1, source_target_pairs={{0,16},{16,0},{32,48},{48,32},{64,80},{80,64},{96,112},{112,96},{1... | collective-permute-start | bytes 368648 | tf_op jit(solution)/shard_map/ppermute | solution.py:403
  23.6 7.1 %copy-start.2 = (bf16[3,3,3,64,128]{4,3,2,1,0:T(8,128)(2,1)S(1)}, bf16[3,3,3,64,128]{4,3,2,1,0:T(8,128)(2,1)}, u32[]{:S(2)}) copy-start(bf16[3,3,3,64,128]{4,3,2,1,0:T(8,128)(2,1)} %param.9) | copy-start | bytes 1327108
  23.6 7.1 %copy-start.3 = (f32[64]{0:T(128)S(1)}, f32[64]{0:T(128)}, u32[]{:S(2)}) copy-start(f32[64]{0:T(128)} %param.8) | copy-start | bytes 772
  23.6 7.0 %copy-start.4 = (f32[128]{0:T(128)S(1)}, f32[128]{0:T(128)}, u32[]{:S(2)}) copy-start(f32[128]{0:T(128)} %param.10) | copy-start | bytes 1540
  23.6 7.0 %collective-permute-start.4 = (bf16[14,1,40,128]{3,2,1,0:T(8,128)(2,1)S(1)}, bf16[14,1,40,128]{3,2,1,0:T(8,128)(2,1)S(1)}, u32[]{:S(2)}, u32[]{:S(2)}) collective-permute-start(bf16[14,1,40,128]{3,2,1,0:T(8,128)(2,1)S(1)} %get-tuple-element.70), channel_id=1, source_target_pairs={{1,2},{2,1},{3,4},{4,3},{5,6},{6,5},{7,8},{8,7},{9,10},{10,9},{11,... | collective-permute-start | bytes 430088 | tf_op jit(solution)/shard_map/ppermute | solution.py:408
  27.9 2.8 %collective-permute-start.3 = (bf16[14,1,40,128]{3,2,1,0:T(8,128)(2,1)S(1)}, bf16[14,1,40,128]{3,2,1,0:T(8,128)(2,1)S(1)}, u32[]{:S(2)}, u32[]{:S(2)}) collective-permute-start(bf16[14,1,40,128]{3,2,1,0:T(8,128)(2,1)S(1)} %get-tuple-element.71), channel_id=1, source_target_pairs={{0,1},{1,0},{2,3},{3,2},{4,5},{5,4},{6,7},{7,6},{8,9},{9,8},{10,11... | collective-permute-start | bytes 430088 | tf_op jit(solution)/shard_map/ppermute | solution.py:409
  37.8 2.7 %collective-permute-start.9 = (bf16[4,4,2,256]{3,2,1,0:T(2,128)(2,1)S(1)}, bf16[4,4,2,256]{3,2,1,0:T(2,128)(2,1)S(1)}, u32[]{:S(2)}, u32[]{:S(2)}) collective-permute-start(bf16[4,4,2,256]{3,2,1,0:T(2,128)(2,1)S(1)} %get-tuple-element.41), channel_id=1, source_target_pairs={{0,128},{128,0},{1,129},{129,1},{2,130},{130,2},{3,131},{131,3},{4... | collective-permute-start | bytes 49160 | tf_op jit(solution)/shard_map/ppermute | solution.py:396
  40.7 5.1 %collective-permute-start.11 = (bf16[2,4,24,256]{3,2,1,0:T(8,128)(2,1)S(1)}, bf16[2,4,24,256]{3,2,1,0:T(8,128)(2,1)S(1)}, u32[]{:S(2)}, u32[]{:S(2)}) collective-permute-start(bf16[2,4,24,256]{3,2,1,0:T(8,128)(2,1)S(1)} %get-tuple-element.80), channel_id=1, source_target_pairs={{16,32},{32,16},{48,64},{64,48},{80,96},{96,80},{17,33},{33,17},{4... | collective-permute-start | bytes 294920 | tf_op jit(solution)/shard_map/ppermute | solution.py:402
  41.4 7.4 %collective-permute-start.10 = (bf16[2,4,24,256]{3,2,1,0:T(8,128)(2,1)S(1)}, bf16[2,4,24,256]{3,2,1,0:T(8,128)(2,1)S(1)}, u32[]{:S(2)}, u32[]{:S(2)}) collective-permute-start(bf16[2,4,24,256]{3,2,1,0:T(8,128)(2,1)S(1)} %get-tuple-element.81), channel_id=1, source_target_pairs={{0,16},{16,0},{32,48},{48,32},{64,80},{80,64},{96,112},{112,96},{1... | collective-permute-start | bytes 294920 | tf_op jit(solution)/shard_map/ppermute | solution.py:403
  48.8 7.3 %collective-permute-start.13 = (bf16[8,1,24,256]{3,2,1,0:T(8,128)(2,1)S(1)}, bf16[8,1,24,256]{3,2,1,0:T(8,128)(2,1)S(1)}, u32[]{:S(2)}, u32[]{:S(2)}) collective-permute-start(bf16[8,1,24,256]{3,2,1,0:T(8,128)(2,1)S(1)} %get-tuple-element.74), channel_id=1, source_target_pairs={{1,2},{2,1},{3,4},{4,3},{5,6},{6,5},{7,8},{8,7},{9,10},{10,9},{11,... | collective-permute-start | bytes 294920 | tf_op jit(solution)/shard_map/ppermute | solution.py:408
  53.8 2.3 %collective-permute-start.12 = (bf16[8,1,24,256]{3,2,1,0:T(8,128)(2,1)S(1)}, bf16[8,1,24,256]{3,2,1,0:T(8,128)(2,1)S(1)}, u32[]{:S(2)}, u32[]{:S(2)}) collective-permute-start(bf16[8,1,24,256]{3,2,1,0:T(8,128)(2,1)S(1)} %get-tuple-element.75), channel_id=1, source_target_pairs={{0,1},{1,0},{2,3},{3,2},{4,5},{5,4},{6,7},{7,6},{8,9},{9,8},{10,11... | collective-permute-start | bytes 294920 | tf_op jit(solution)/shard_map/ppermute | solution.py:409
  54.0 2.2 %copy-start.5 = (bf16[5,10,48,256]{3,2,1,0:T(8,128)(2,1)S(1)}, bf16[5,10,48,256]{3,2,1,0:T(8,128)(2,1)}, u32[]{:S(2)}) copy-start(bf16[5,10,48,256]{3,2,1,0:T(8,128)(2,1)} %get-tuple-element.45.slope_ref) | copy-start | bytes 3686404
  54.0 2.2 %copy-start.7 = (bf16[10,6,40,128]{3,2,1,0:T(8,128)(2,1)S(1)}, bf16[10,6,40,128]{3,2,1,0:T(8,128)(2,1)}, u32[]{:S(2)}) copy-start(bf16[10,6,40,128]{3,2,1,0:T(8,128)(2,1)} %get-tuple-element.46.vo_ref) | copy-start | bytes 1843204
  64.8 1.7 %collective-permute-start.14 = (bf16[1280,128]{1,0:T(8,128)(2,1)S(1)}, bf16[1280,128]{1,0:T(8,128)(2,1)S(1)}, u32[]{:S(2)}, u32[]{:S(2)}) collective-permute-start(bf16[1280,128]{1,0:T(8,128)(2,1)S(1)} %get-tuple-element.49), channel_id=1, source_target_pairs={{0,1},{1,0},{2,3},{3,2},{4,5},{5,4},{6,7},{7,6},{8,9},{9,8},{10,11... | collective-permute-start | bytes 983048 | tf_op jit(solution)/shard_map/ppermute | solution.py:485
  67.3 33.7 %all-to-all-start.1 = ((bf16[128,5,2,128]{3,2,1,0:T(2,128)(2,1)}), bf16[128,5,2,128]{3,2,1,0:T(2,128)(2,1)S(1)}, u32[]{:S(2)}, u32[]{:S(2)}) async-start(bf16[128,5,2,128]{3,2,1,0:T(2,128)(2,1)} %bitcast.22), calls=%async_computation.1 | async-start | bytes 655360 | tf_op jit(solution)/shard_map/all_to_all | solution.py:487
  85.6 42.3 %copy-start.6 = (bf16[5,10,40,256]{3,2,1,0:T(8,128)(2,1)S(1)}, bf16[5,10,40,256]{3,2,1,0:T(8,128)(2,1)}, u32[]{:S(2)}) copy-start(bf16[5,10,40,256]{3,2,1,0:T(8,128)(2,1)} %get-tuple-element.47.ga_ref) | copy-start | bytes 3072004
  85.7 1.6 %collective-permute-start.5 = (bf16[8,1,1,8,4,128]{5,3,4,1,0,2:T(8,128)(2,1)S(1)}, bf16[8,1,1,8,4,128]{5,3,4,1,0,2:T(8,128)(2,1)S(1)}, u32[]{:S(2)}, u32[]{:S(2)}) collective-permute-start(bf16[8,1,1,8,4,128]{5,3,4,1,0,2:T(8,128)(2,1)S(1)} %constant_dynamic-slice_fusion.3), channel_id=1, source_target_pairs={{0,1},{1,0},{2,3},{3,2},{4,5},{5,4},{6,7},{7,6},{8,9},{9,8},{10,11... | collective-permute-start | bytes 196616 | tf_op jit(solution)/shard_map/ppermute | solution.py:423
  102.2 20.2 %all-to-all-start.2 = ((bf16[128,5,2,128]{3,2,1,0:T(2,128)(2,1)}), bf16[128,5,2,128]{3,2,1,0:T(2,128)(2,1)S(1)}, u32[]{:S(2)}, u32[]{:S(2)}) async-start(bf16[128,5,2,128]{3,2,1,0:T(2,128)(2,1)} %shard_map.115), calls=%async_computation.2 | async-start | bytes 655360 | tf_op jit(solution)/shard_map/all_to_all | solution.py:489
  108.4 7.7 %collective-permute-start.6 = (bf16[4,1,2,8,4,128]{5,3,4,2,1,0:T(8,128)(2,1)S(1)}, bf16[4,1,2,8,4,128]{5,3,4,2,1,0:T(8,128)(2,1)S(1)}, u32[]{:S(2)}, u32[]{:S(2)}) collective-permute-start(bf16[4,1,2,8,4,128]{5,3,4,2,1,0:T(8,128)(2,1)S(1)} %constant_dynamic-slice_fusion.2), channel_id=1, source_target_pairs={{0,2},{1,3},{2,0},{3,1},{4,6},{5,7},{6,4},{7,5},{8,10},{9,11},{10,... | collective-permute-start | bytes 196616 | tf_op jit(solution)/shard_map/ppermute | solution.py:423
  116.2 5.3 %collective-permute-start.7 = (bf16[2,1,4,8,4,128]{5,3,2,1,0,4:T(8,128)(2,1)S(1)}, bf16[2,1,4,8,4,128]{5,3,2,1,0,4:T(8,128)(2,1)S(1)}, u32[]{:S(2)}, u32[]{:S(2)}) collective-permute-start(bf16[2,1,4,8,4,128]{5,3,2,1,0,4:T(8,128)(2,1)S(1)} %constant_dynamic-slice_fusion.1), channel_id=1, source_target_pairs={{0,4},{1,5},{2,6},{3,7},{4,0},{5,1},{6,2},{7,3},{8,12},{9,13},{10,... | collective-permute-start | bytes 196616 | tf_op jit(solution)/shard_map/ppermute | solution.py:423
  122.4 13.7 %collective-permute-start.15 = (bf16[1280,128]{1,0:T(8,128)(2,1)S(1)}, bf16[1280,128]{1,0:T(8,128)(2,1)S(1)}, u32[]{:S(2)}, u32[]{:S(2)}) collective-permute-start(bf16[1280,128]{1,0:T(8,128)(2,1)S(1)} %bitcast.37), channel_id=1, source_target_pairs={{0,1},{1,0},{2,3},{3,2},{4,5},{5,4},{6,7},{7,6},{8,9},{9,8},{10,11... | collective-permute-start | bytes 983048 | tf_op jit(solution)/shard_map/ppermute | solution.py:490
  126.6 8.7 %collective-permute-start.8 = (bf16[1,1,8,8,4,128]{5,3,2,1,4,0:T(8,128)(2,1)S(1)}, bf16[1,1,8,8,4,128]{5,3,2,1,4,0:T(8,128)(2,1)S(1)}, u32[]{:S(2)}, u32[]{:S(2)}) collective-permute-start(bf16[1,1,8,8,4,128]{5,3,2,1,4,0:T(8,128)(2,1)S(1)} %constant_dynamic-slice_fusion), channel_id=1, source_target_pairs={{0,8},{1,9},{2,10},{3,11},{4,12},{5,13},{6,14},{7,15},{8,0},{9,1},... | collective-permute-start | bytes 196616 | tf_op jit(solution)/shard_map/ppermute | solution.py:423

commit v5 on v4

--- a/solution.py
+++ b/solution.py
@@ -185,15 +185,16 @@
         lo, hi = rows[..., :128], rows[..., 128:]
         lo = lo + pltpu.roll(lo, 64, 2)
         hi = hi + pltpu.roll(hi, 64, 2)
-        s_ref[...] = jnp.where(fold, lo, hi)
-        mean = (s_ref[:, pl.ds(0, 24, stride=2), :] + s_ref[:, pl.ds(1, 24, stride=2), :]) * 0.125
+        s_ref[q % 2] = jnp.where(fold, lo, hi)
+        mean = (s_ref[q % 2, :, pl.ds(0, 24, stride=2), :] + s_ref[q % 2, :, pl.ds(1, 24, stride=2), :]) * 0.125
         z = zlane + (gz * 8 - 1 + 2 * q)
-        p_ref[...] = jnp.where(inside_xy & (z >= 0) & (z < 128), mean, 0.0)
+        p_ref[q % 2] = jnp.where(inside_xy & (z >= 0) & (z < 128), mean, 0.0)
         for dx in range(3):
-            px_ref[dx, :, q] = p_ref[:, pl.ds(dx, 16), :].astype(BF16)
+            px_ref[dx, :, q] = p_ref[q % 2, :, pl.ds(dx, 16), :].astype(BF16)
         return carry
 
-    lax.fori_loop(0, 5, conv_a, 0)
+    for q in range(5):
+        conv_a(q, 0)
 
     parts = []
     for dx, dy in TAPS:
@@ -236,32 +237,30 @@
 def backward(
     where_ref, g_ref, ynear_ref, yfar_ref, znear_ref, zfar_ref, w_ref, wb_ref, sum_b_ref, slope_ref, vo_ref,
     keep_ref, send_ref, ga_hbm,
-    f_ref, gx_ref, s_ref, t_ref, own_ref, flat_ref, vx_ref, v_ref, bt_ref, ga_ref, sem,
+    rows_ref, s_ref, t_ref, own_ref, flat_ref, vx_ref, v_ref, bt_ref, ga_ref, sem,
 ):
     banded_back_b(w_ref, bt_ref)
     gx, gy, gz = position(where_ref)
 
-    def stage(src, rows, y0, q0, nq):
-        def step(y, carry):
-            for h in range(2):
-                f_ref[h, 0:nq, 0:24, :] = src[y, :, :, h * 128 : h * 128 + 128].astype(F32)
-                for dx in range(3):
-                    gx_ref[dx, y0 + y, pl.ds(q0, nq), :, h * 128 : h * 128 + 128] = f_ref[
-                        h, 0:nq, pl.ds(dx, 32), :
-                    ].astype(BF16)
-            return carry
-
-        lax.fori_loop(0, rows, step, 0)
-
     even_y, even_z = gy % 2 == 0, gz % 2 == 0
-    stage(g_ref, 4, 2, 1, 4)
-    stage(ynear_ref, 2, jnp.where(even_y, 6, 0), 1, 4)
-    stage(yfar_ref, 2, jnp.where(even_y, 0, 6), 1, 4)
-    stage(znear_ref, 8, 0, jnp.where(even_z, 5, 0), 1)
-    stage(zfar_ref, 8, 0, jnp.where(even_z, 0, 5), 1)
+
+    def put(src, base):
+        for y in range(src.shape[0]):
+            start = pl.multiple_of(base + 24 * y, 8)
+            rows_ref[1:5, pl.ds(start, 24), :] = src[y].astype(F32)
+
+    put(g_ref, 48)
+    put(ynear_ref, jnp.where(even_y, 144, 0))
+    put(yfar_ref, jnp.where(even_y, 0, 144))
+    for src, q in ((znear_ref, jnp.where(even_z, 5, 0)), (zfar_ref, jnp.where(even_z, 0, 5))):
+        for y in range(8):
+            rows_ref[pl.ds(q, 1), 24 * y : 24 * y + 24, :] = src[y].astype(F32)
 
     def stage_v(y, carry):
-        v_ref[...] = vo_ref[y].astype(F32)
+        groups = vo_ref[y].astype(F32)
+        v_ref[...] = jnp.where(
+            iota((5, 40, 128), 2) < 64, pltpu.roll(groups[0:5], 64, 2), pltpu.roll(groups[1:6], 64, 2)
+        )
         for dx in range(3):
             vx_ref[dx, y] = v_ref[:, pl.ds(dx, 32), :].astype(BF16)
         return carry
@@ -274,45 +273,49 @@
     zlane = iota(shape, 2) // 64
     inside_xy = (x >= 0) & (x < 64) & (y >= 0) & (y < 64)
 
+    parts = []
+    for dx, dy in TAPS:
+        for j in range(2):
+            parts.append(rows_ref[j : j + 5, pl.ds(24 * dy + dx, 144), :].astype(BF16))
+    lhs = jnp.concatenate(parts, axis=-1).reshape(720, 4608)
+    back = lax.dot_general(lhs, bt_ref[...], NT, preferred_element_type=F32)
+
     def save_ga(q):
         return pltpu.make_async_copy(ga_ref.at[q], ga_hbm.at[q], sem.at[q])
 
     def conv_b(q, total):
-        parts = []
-        for dx, dy in TAPS:
-            parts.append(gx_ref[dx, dy : dy + 6, q])
-            parts.append(gx_ref[dx, dy : dy + 6, q + 1])
-        lhs = jnp.concatenate(parts, axis=-1).reshape(192, 4608)
-        pooled = lax.dot_general(lhs, bt_ref[...], NT, preferred_element_type=F32)
-        pooled = pooled.astype(BF16).astype(F32).reshape(6, 32, 256)[:, :24]
+        pooled = back[144 * q : 144 * q + 144].astype(BF16).astype(F32).reshape(6, 24, 256)
         sums = []
         for h in range(2):
             half = pooled[..., h * 128 : h * 128 + 128]
-            s_ref[:, pl.ds(0, 24, stride=2), :] = half
-            s_ref[:, pl.ds(1, 24, stride=2), :] = half
-            spread = jnp.broadcast_to(s_ref[...].reshape(6, 1, 48, 128), (6, 2, 48, 128)).reshape(12, 48, 128)[1:11]
+            slot = 2 * (q % 2) + h
+            s_ref[slot, :, pl.ds(0, 24, stride=2), :] = half
+            s_ref[slot, :, pl.ds(1, 24, stride=2), :] = half
+            spread = jnp.broadcast_to(s_ref[slot].reshape(6, 1, 48, 128), (6, 2, 48, 128)).reshape(12, 48, 128)[1:11]
             z = zlane + (gz * 16 - 2 + 4 * q + 2 * h)
             slope = slope_ref[q, :, :, h * 128 : h * 128 + 128].astype(F32)
-            t_ref[...] = jnp.where(inside_xy & (z >= 0) & (z < 256), spread * slope, 0.0)
-            ga_ref[q, :, :, h * 128 : h * 128 + 128] = t_ref[:, pl.ds(1, 40), :].astype(BF16)
-            keep = jnp.where(q == 4 * h, 0.0, 1.0)
-            own = (t_ref[1:9, pl.ds(2, 32), :] * keep).astype(BF16)
-            own_ref[:, q, :, h * 128 : h * 128 + 128] = own
-            sums.append(jnp.sum(own.astype(F32).reshape(256, 128), axis=0, keepdims=True))
+            t_ref[slot] = jnp.where(inside_xy & (z >= 0) & (z < 256), spread * slope, 0.0)
+            ga_ref[q, :, :, h * 128 : h * 128 + 128] = t_ref[slot, :, pl.ds(1, 40), :].astype(BF16)
+            own = t_ref[slot, 1:9, pl.ds(2, 32), :].astype(BF16)
+            own_ref[:, q + h, :, 128 - h * 128 : 256 - h * 128] = own
+            keep = 0.0 if q == 4 * h else 1.0
+            sums.append(keep * jnp.sum(own.astype(F32).reshape(256, 128), axis=0, keepdims=True))
         save_ga(q).start()
         return total + sums[0] + sums[1]
 
-    total = lax.fori_loop(0, 5, conv_b, jnp.zeros((1, 128), F32))
+    total = jnp.zeros((1, 128), F32)
+    for q in range(5):
+        total = conv_b(q, total)
     flat_ref[0:1728] = wb_ref[...].reshape(1728, 128)
     row = iota((16, 128), 0)
     sums = jnp.where(row == 0, sum_b_ref[...], jnp.where(row == 1, total + pltpu.roll(total, 64, 1), 0.0))
     flat_ref[2304:2320] = sums.astype(BF16)
     flat_ref[2320:2560] = jnp.zeros((240, 128), BF16)
 
-    flat = own_ref[...].reshape(1280, 256).T
+    flat = own_ref[:, 1:5].reshape(1024, 256).T
     for t, (dx, dy) in enumerate(TAPS):
-        cells = jnp.concatenate([vx_ref[dx, dy : dy + 8, 0:5], vx_ref[dx, dy : dy + 8, 1:6]], axis=-1)
-        terms = jnp.dot(flat, cells.reshape(1280, 256), preferred_element_type=F32)
+        cells = jnp.concatenate([vx_ref[dx, dy : dy + 8, 0:4], vx_ref[dx, dy : dy + 8, 1:5]], axis=-1)
+        terms = jnp.dot(flat, cells.reshape(1024, 256), preferred_element_type=F32)
         block = terms[0:64]
         for zo in range(1, 4):
             block = block + pltpu.roll(terms[zo * 64 : zo * 64 + 64], 256 - 32 * zo, 1)
@@ -454,7 +457,7 @@
         ),
         [
             pltpu.VMEM((4, 56, 128), F32), pltpu.VMEM((3, 14, 6, 48, 128), BF16),
-            pltpu.VMEM((6, 48, 128), F32), pltpu.VMEM((6, 24, 128), F32), pltpu.VMEM((4, 4, 16, 128), F32),
+            pltpu.VMEM((2, 6, 48, 128), F32), pltpu.VMEM((2, 6, 24, 128), F32), pltpu.VMEM((4, 4, 16, 128), F32),
             pltpu.VMEM((2304, 256), BF16),
             pltpu.VMEM((10, 6, 40, 128), BF16), pltpu.VMEM((5, 10, 48, 256), BF16), pltpu.SemaphoreType.DMA((6,)),
         ],
@@ -471,13 +474,13 @@
         backward,
         (sds(1280, 128), sds(1280, 128), pltpu.HBM((5, 10, 40, 256), BF16)),
         [
-            pltpu.VMEM((2, 4, 40, 128), F32), pltpu.VMEM((3, 8, 6, 32, 256), BF16),
-            pltpu.VMEM((6, 48, 128), F32), pltpu.VMEM((10, 48, 128), F32), pltpu.VMEM((8, 5, 32, 256), BF16),
-            pltpu.VMEM((2560, 128), BF16), pltpu.VMEM((3, 10, 6, 32, 128), BF16), pltpu.VMEM((6, 40, 128), F32),
+            pltpu.VMEM((6, 200, 256), F32),
+            pltpu.VMEM((4, 6, 48, 128), F32), pltpu.VMEM((4, 10, 48, 128), F32), pltpu.VMEM((8, 6, 32, 256), BF16),
+            pltpu.VMEM((2560, 128), BF16), pltpu.VMEM((3, 10, 5, 32, 128), BF16), pltpu.VMEM((5, 40, 128), F32),
             pltpu.VMEM((256, 4608), BF16),
             pltpu.VMEM((5, 10, 40, 256), BF16), pltpu.SemaphoreType.DMA((5,)),
         ],
-        where, *sides_b, wb27, wb, sum_b, slope, vo, flops=2 * 10**9, room=24, far_outs=1,
+        where, *sides_b, wb27, wb, sum_b, slope, vo, flops=2 * 10**9, room=32, far_outs=1,
     )
 
     flip = [(0, 1), (1, 0)]

time: 138 us -> 136 us (0.986)
  Pallas kernels: 22.8 us -> 21.3 us
    pallas_call x8, Pallas kernels: 22.8 us -> 21.3 us  [call(): pl.pallas_call(body, out_shape=outs, in_specs=near + [far] * far_args, ou...]
where the time goes in v5:
time: 136 us
  starting transfers between devices  63.6 us (47%)
  waiting for transfers between devices  41.9 us (31%)
  Pallas kernels  21.3 us (16%)
  local copies, waits for them, and re-layouts  6.69 us (5%)
  other arithmetic  1.39 us (1%)
    pallas_call x8, Pallas kernels, call(): pl.pallas_call(body, out_shape=outs, in_specs=near + [far] * far_args, ou...  21.3 us
    all_to_all x1, starting transfers between devices, on_device(): lax.all_to_all(chip.reshape(count, 5, 2, 128), CHIPS, 0, 0, tiled=True)  18 us
    ppermute x4, waiting for transfers between devices, to_slabs(): got = lax.ppermute(part, GZ, [(i, i ^ 1 << b) for i in range(16)])  13.7 us
    all_to_all x1, waiting for transfers between devices, on_device(): lax.all_to_all(chip.reshape(count, 5, 2, 128), CHIPS, 0, 0, tiled=True)  13.7 us
    all_to_all x1, starting transfers between devices, on_device(): cot = lax.all_to_all(cot, GZ, 0, 0, tiled=True)  9.43 us
    ppermute x2, starting transfers between devices, halo(): zfar = lax.ppermute(jnp.where(even_z, head, last), GZ, far)  9.25 us
    ppermute x2, starting transfers between devices, halo(): ynear = lax.ppermute(jnp.where(even, high, low), 'gy', near)  8.36 us
    ppermute x2, waiting for transfers between devices, halo(): ynear = lax.ppermute(jnp.where(even, high, low), 'gy', near)  6.2 us
  transfers between devices with their start and end apart: 19, of which 12 were waited for; matrix products, arithmetic and copies ran while one was open for 4% of the time, Pallas kernels for 3%

profile of v5, /device:TPU:1, one launch (start us, length us, event | category | flops | bytes accessed | tf_op | source)
XLA Modules:
  0.0 136.0 jit_solution(10566048614144334229)
XLA Ops:
  0.7 1.2 copy-done
  1.9 0.7 shard_map.109
  2.7 2.1 %collective-permute-start = (bf16[8,4,3,128]{3,2,1,0:T(4,128)(2,1)S(1)}, bf16[8,4,3,128]{3,2,1,0:T(4,128)(2,1)S(1)}, u32[]{:S(2)}, u32[]{:S(2)}) collective-permute-start(bf16[8,4,3,128]{3,2,1,0:T(4,128)(2,1)S(1)} %slice_select_fusion), channel_id=1, source_target_pairs={{0,128},{128,0},{1,129},{129,1},{2,130},{130,2},{3,131},{131,3},{4... | collective-permute-start | bytes 73736 | tf_op jit(solution)/shard_map/ppermute | solution.py:399
  4.8 0.1 copy.21
  5.0 0.7 copy.22
  5.7 9.4 %all-to-all-start = ((bf16[16,8,4,128]{3,1,2,0:T(8,128)(2,1)}), bf16[16,8,4,128]{3,1,2,0:T(8,128)(2,1)S(1)}, u32[]{:S(2)}, u32[]{:S(2)}) async-start(bf16[16,8,4,128]{3,1,2,0:T(8,128)(2,1)} %copy.22), calls=%async_computation | async-start | bytes 262144 | tf_op jit(solution)/shard_map/all_to_all | solution.py:444
  15.2 0.2 maximum_maximum_fusion.v_ref
  15.5 0.8 collective-permute-start.2
  16.3 3.9 %collective-permute-start.1 = (bf16[3,4,40,128]{3,2,1,0:T(8,128)(2,1)S(1)}, bf16[3,4,40,128]{3,2,1,0:T(8,128)(2,1)S(1)}, u32[]{:S(2)}, u32[]{:S(2)}) collective-permute-start(bf16[3,4,40,128]{3,2,1,0:T(8,128)(2,1)S(1)} %get-tuple-element.69), channel_id=1, source_target_pairs={{0,16},{16,0},{32,48},{48,32},{64,80},{80,64},{96,112},{112,96},{1... | collective-permute-start | bytes 368648 | tf_op jit(solution)/shard_map/ppermute | solution.py:406
  20.2 3.3 %collective-permute-done.1.ynear_ref = bf16[3,4,40,128]{3,2,1,0:T(8,128)(2,1)S(1)} collective-permute-done((bf16[3,4,40,128]{3,2,1,0:T(8,128)(2,1)S(1)}, bf16[3,4,40,128]{3,2,1,0:T(8,128)(2,1)S(1)}, u32[]{:S(2)}, u32[]{:S(2)}) %collective-permute-start.1) | collective-permute-done | bytes 122912 | tf_op jit(solution)/shard_map/ppermute | solution.py:406
  23.6 4.2 %collective-permute-start.4 = (bf16[14,1,40,128]{3,2,1,0:T(8,128)(2,1)S(1)}, bf16[14,1,40,128]{3,2,1,0:T(8,128)(2,1)S(1)}, u32[]{:S(2)}, u32[]{:S(2)}) collective-permute-start(bf16[14,1,40,128]{3,2,1,0:T(8,128)(2,1)S(1)} %get-tuple-element.70), channel_id=1, source_target_pairs={{1,2},{2,1},{3,4},{4,3},{5,6},{6,5},{7,8},{8,7},{9,10},{10,9},{11,... | collective-permute-start | bytes 430088 | tf_op jit(solution)/shard_map/ppermute | solution.py:411
  27.9 0.1 collective-permute-start.3
  28.0 0.2 shard_map.110.a_ref
  28.3 0.1 copy.24
  28.6 2.1 %collective-permute-done.4.zfar_ref = bf16[14,1,40,128]{3,2,1,0:T(8,128)(2,1)S(1)} collective-permute-done((bf16[14,1,40,128]{3,2,1,0:T(8,128)(2,1)S(1)}, bf16[14,1,40,128]{3,2,1,0:T(8,128)(2,1)S(1)}, u32[]{:S(2)}, u32[]{:S(2)}) %collective-permute-start.4) | collective-permute-done | bytes 143392 | tf_op jit(solution)/shard_map/ppermute | solution.py:411
  30.7 6.1 %shard_map.111 = (bf16[4,4,16,256]{3,2,1,0:T(8,128)(2,1)S(1)}, bf16[4,4,16,256]{3,2,1,0:T(8,128)(2,1)S(1)}, f32[1,128]{1,0:T(1,128)S(1)}, bf16[3,6,5,16,128]{4,3...) custom-call(s32[1]{0:T(128)} %bitcast.where_ref, ...), custom_call_target="tpu_custom_call" | custom-call | flops 2000000000 | bytes 1000000 | tf_op jit(solution)/shard_map/pallas_call | solution.py:29
  36.8 0.3 collective-permute-start.9
  37.2 2.3 %collective-permute-done.9 = bf16[4,4,2,256]{3,2,1,0:T(2,128)(2,1)S(1)} collective-permute-done((bf16[4,4,2,256]{3,2,1,0:T(2,128)(2,1)S(1)}, bf16[4,4,2,256]{3,2,1,0:T(2,128)(2,1)S(1)}, u32[]{:S(2)}, u32[]{:S(2)}) %collective-permute-start.9) | collective-permute-done | bytes 16416 | tf_op jit(solution)/shard_map/ppermute | solution.py:399
  39.5 0.1 maximum_maximum_fusion.1.g_ref
  39.7 0.7 collective-permute-start.11
  40.3 4.4 %collective-permute-start.10 = (bf16[2,4,24,256]{3,2,1,0:T(8,128)(2,1)S(1)}, bf16[2,4,24,256]{3,2,1,0:T(8,128)(2,1)S(1)}, u32[]{:S(2)}, u32[]{:S(2)}) collective-permute-start(bf16[2,4,24,256]{3,2,1,0:T(8,128)(2,1)S(1)} %get-tuple-element.81), channel_id=1, source_target_pairs={{0,16},{16,0},{32,48},{48,32},{64,80},{80,64},{96,112},{112,96},{1... | collective-permute-start | bytes 294920 | tf_op jit(solution)/shard_map/ppermute | solution.py:406
  44.8 2.9 %collective-permute-done.10.ynear_ref = bf16[2,4,24,256]{3,2,1,0:T(8,128)(2,1)S(1)} collective-permute-done((bf16[2,4,24,256]{3,2,1,0:T(8,128)(2,1)S(1)}, bf16[2,4,24,256]{3,2,1,0:T(8,128)(2,1)S(1)}, u32[]{:S(2)}, u32[]{:S(2)}) %collective-permute-start.10) | collective-permute-done | bytes 98336 | tf_op jit(solution)/shard_map/ppermute | solution.py:406
  47.8 5.0 %collective-permute-start.13 = (bf16[8,1,24,256]{3,2,1,0:T(8,128)(2,1)S(1)}, bf16[8,1,24,256]{3,2,1,0:T(8,128)(2,1)S(1)}, u32[]{:S(2)}, u32[]{:S(2)}) collective-permute-start(bf16[8,1,24,256]{3,2,1,0:T(8,128)(2,1)S(1)} %get-tuple-element.74), channel_id=1, source_target_pairs={{1,2},{2,1},{3,4},{4,3},{5,6},{6,5},{7,8},{8,7},{9,10},{10,9},{11,... | collective-permute-start | bytes 294920 | tf_op jit(solution)/shard_map/ppermute | solution.py:411
  52.8 0.3 collective-permute-start.12
  53.1 0.5 shard_map.112.wb_ref
  53.7 1.4 %collective-permute-done.13.zfar_ref = bf16[8,1,24,256]{3,2,1,0:T(8,128)(2,1)S(1)} collective-permute-done((bf16[8,1,24,256]{3,2,1,0:T(8,128)(2,1)S(1)}, bf16[8,1,24,256]{3,2,1,0:T(8,128)(2,1)S(1)}, u32[]{:S(2)}, u32[]{:S(2)}) %collective-permute-start.13) | collective-permute-done | bytes 98336 | tf_op jit(solution)/shard_map/ppermute | solution.py:411
  55.1 8.2 %shard_map.113 = (bf16[1280,128]{1,0:T(8,128)(2,1)S(1)}, bf16[1280,128]{1,0:T(8,128)(2,1)S(1)}, bf16[5,10,40,256]{3,2,1,0:T(8,128)(2,1)}) custom-call(s32[1]{0:T(128)} %bitcast.where_ref, bf16[4,4,24,256]{3,2,1,0:T(8,128)(2,1)S(1)} %maximum_maximum_fusion.1.g_ref, bf16[2,4,24,256]{3,2,1,0:T(8,128)(2,1)S(1)} %collective-permute-done.10.ynear_ref, ...), custom_call_target="tpu_custom_call" | custom-call | flops 2000000000 | bytes 1000000 | tf_op jit(solution)/shard_map/pallas_call | solution.py:29
  63.4 1.6 %collective-permute-done.14 = bf16[1280,128]{1,0:T(8,128)(2,1)S(1)} collective-permute-done((bf16[1280,128]{1,0:T(8,128)(2,1)S(1)}, bf16[1280,128]{1,0:T(8,128)(2,1)S(1)}, u32[]{:S(2)}, u32[]{:S(2)}) %collective-permute-start.14) | collective-permute-done | bytes 327712 | tf_op jit(solution)/shard_map/ppermute | solution.py:488
  65.0 0.8 add_convert_fusion
  65.9 18.0 %all-to-all-start.1 = ((bf16[128,5,2,128]{3,2,1,0:T(2,128)(2,1)}), bf16[128,5,2,128]{3,2,1,0:T(2,128)(2,1)S(1)}, u32[]{:S(2)}, u32[]{:S(2)}) async-start(bf16[128,5,2,128]{3,2,1,0:T(2,128)(2,1)} %bitcast.22), calls=%async_computation.1 | async-start | bytes 655360 | tf_op jit(solution)/shard_map/all_to_all | solution.py:490
  84.0 0.7 collective-permute-start.5
  84.8 0.9 collective-permute-done.5
  85.7 13.7 %all-to-all-done.1.shares_ref = bf16[128,5,2,128]{3,2,1,0:T(2,128)(2,1)S(1)} async-done(((bf16[128,5,2,128]{3,2,1,0:T(2,128)(2,1)}), bf16[128,5,2,128]{3,2,1,0:T(2,128)(2,1)S(1)}, u32[]{:S(2)}, u32[]{:S(2)}) %all-to-all-start.1) | async-done | bytes 327712 | tf_op jit(solution)/shard_map/all_to_all | solution.py:490
  99.4 1.2 shard_map.115
  100.6 6.2 %all-to-all-start.2 = ((bf16[128,5,2,128]{3,2,1,0:T(2,128)(2,1)}), bf16[128,5,2,128]{3,2,1,0:T(2,128)(2,1)S(1)}, u32[]{:S(2)}, u32[]{:S(2)}) async-start(bf16[128,5,2,128]{3,2,1,0:T(2,128)(2,1)} %shard_map.115), calls=%async_computation.2 | async-start | bytes 655360 | tf_op jit(solution)/shard_map/all_to_all | solution.py:492
  106.8 0.5 collective-permute-start.6
  107.3 7.2 %collective-permute-done.6 = bf16[4,1,2,8,4,128]{5,3,4,2,1,0:T(8,128)(2,1)S(1)} collective-permute-done((bf16[4,1,2,8,4,128]{5,3,4,2,1,0:T(8,128)(2,1)S(1)}, bf16[4,1,2,8,4,128]{5,3,4,2,1,0:T(8,128)(2,1)S(1)}, u32[]{:S(2)}, u32[]{:S(2)}) %collective-permute-start.6) | collective-permute-done | bytes 65568 | tf_op jit(solution)/shard_map/ppermute | solution.py:426
  114.6 1.0 collective-permute-start.7
  115.6 4.4 %collective-permute-done.7 = bf16[2,1,4,8,4,128]{5,3,2,1,0,4:T(8,128)(2,1)S(1)} collective-permute-done((bf16[2,1,4,8,4,128]{5,3,2,1,0,4:T(8,128)(2,1)S(1)}, bf16[2,1,4,8,4,128]{5,3,2,1,0,4:T(8,128)(2,1)S(1)}, u32[]{:S(2)}, u32[]{:S(2)}) %collective-permute-start.7) | collective-permute-done | bytes 65568 | tf_op jit(solution)/shard_map/ppermute | solution.py:426
  120.0 0.7 all-to-all-done.2
  120.8 4.1 %collective-permute-start.15 = (bf16[1280,128]{1,0:T(8,128)(2,1)S(1)}, bf16[1280,128]{1,0:T(8,128)(2,1)S(1)}, u32[]{:S(2)}, u32[]{:S(2)}) collective-permute-start(bf16[1280,128]{1,0:T(8,128)(2,1)S(1)} %bitcast.37), channel_id=1, source_target_pairs={{0,1},{1,0},{2,3},{3,2},{4,5},{5,4},{6,7},{7,6},{8,9},{9,8},{10,11... | collective-permute-start | bytes 983048 | tf_op jit(solution)/shard_map/ppermute | solution.py:493
  124.9 1.6 %collective-permute-start.8 = (bf16[1,1,8,8,4,128]{5,3,2,1,4,0:T(8,128)(2,1)S(1)}, bf16[1,1,8,8,4,128]{5,3,2,1,4,0:T(8,128)(2,1)S(1)}, u32[]{:S(2)}, u32[]{:S(2)}) collective-permute-start(bf16[1,1,8,8,4,128]{5,3,2,1,4,0:T(8,128)(2,1)S(1)} %constant_dynamic-slice_fusion), channel_id=1, source_target_pairs={{0,8},{1,9},{2,10},{3,11},{4,12},{5,13},{6,14},{7,15},{8,0},{9,1},... | collective-permute-start | bytes 196616 | tf_op jit(solution)/shard_map/ppermute | solution.py:426
  126.5 3.0 %shard_map.114 = bf16[8,2,32,256]{3,2,1,0:T(8,128)(2,1)S(1)} custom-call(bf16[5,10,40,256]{3,2,1,0:T(8,128)(2,1)S(1)} %copy-done.6, bf16[27,32,64]{2,1,0:T(8,128)(2,1)S(1)} %bitcast.41), custom_call_target="tpu_custom_call" | custom-call | flops 2000000000 | bytes 1000000 | tf_op jit(solution)/shard_map/pallas_call | solution.py:29
  129.6 0.4 reshape.392
  130.0 2.6 %copy.28 = bf16[32,32,8,2,8]{1,4,3,2,0:T(8,128)(2,1)} copy(bf16[32,32,8,2,8]{0,4,1,3,2:T(8,128)(2,1)S(1)} %bitcast.46) | data formatting | bytes 524288 | tf_op jit(solution)/shard_map/transpose | solution.py:501
  132.6 1.2 collective-permute-done.8
  133.9 0.8 copy.29
  134.7 1.3 shard_map.116
  (56 shorter events, 1.0 us)
Async XLA Ops:
  0.6 4.2 %copy-start.8 = (bf16[128,1,4,128]{3,2,1,0:T(4,128)(2,1)S(1)}, bf16[128,1,4,128]{3,2,1,0:T(4,128)(2,1)}, u32[]{:S(2)}) copy-start(bf16[128,1,4,128]{3,2,1,0:T(4,128)(2,1)} %param.11) | copy-start | bytes 393220
  0.7 1.2 copy-start
  2.7 12.5 %collective-permute-start = (bf16[8,4,3,128]{3,2,1,0:T(4,128)(2,1)S(1)}, bf16[8,4,3,128]{3,2,1,0:T(4,128)(2,1)S(1)}, u32[]{:S(2)}, u32[]{:S(2)}) collective-permute-start(bf16[8,4,3,128]{3,2,1,0:T(4,128)(2,1)S(1)} %slice_select_fusion), channel_id=1, source_target_pairs={{0,128},{128,0},{1,129},{129,1},{2,130},{130,2},{3,131},{131,3},{4... | collective-permute-start | bytes 73736 | tf_op jit(solution)/shard_map/ppermute | solution.py:399
  5.7 22.6 %all-to-all-start = ((bf16[16,8,4,128]{3,1,2,0:T(8,128)(2,1)}), bf16[16,8,4,128]{3,1,2,0:T(8,128)(2,1)S(1)}, u32[]{:S(2)}, u32[]{:S(2)}) async-start(bf16[16,8,4,128]{3,1,2,0:T(8,128)(2,1)} %copy.22), calls=%async_computation | async-start | bytes 262144 | tf_op jit(solution)/shard_map/all_to_all | solution.py:444
  15.4 12.6 %copy-start.1 = (bf16[3,3,3,32,64]{4,3,2,1,0:T(8,128)(2,1)S(1)}, bf16[3,3,3,32,64]{4,3,2,1,0:T(8,128)(2,1)}, u32[]{:S(2)}) copy-start(bf16[3,3,3,32,64]{4,3,2,1,0:T(8,128)(2,1)} %param.7) | copy-start | bytes 331780
  15.5 4.7 %collective-permute-start.2 = (bf16[3,4,40,128]{3,2,1,0:T(8,128)(2,1)S(1)}, bf16[3,4,40,128]{3,2,1,0:T(8,128)(2,1)S(1)}, u32[]{:S(2)}, u32[]{:S(2)}) collective-permute-start(bf16[3,4,40,128]{3,2,1,0:T(8,128)(2,1)S(1)} %get-tuple-element.68), channel_id=1, source_target_pairs={{16,32},{32,16},{48,64},{64,48},{80,96},{96,80},{17,33},{33,17},{4... | collective-permute-start | bytes 368648 | tf_op jit(solution)/shard_map/ppermute | solution.py:405
  16.3 7.2 %collective-permute-start.1 = (bf16[3,4,40,128]{3,2,1,0:T(8,128)(2,1)S(1)}, bf16[3,4,40,128]{3,2,1,0:T(8,128)(2,1)S(1)}, u32[]{:S(2)}, u32[]{:S(2)}) collective-permute-start(bf16[3,4,40,128]{3,2,1,0:T(8,128)(2,1)S(1)} %get-tuple-element.69), channel_id=1, source_target_pairs={{0,16},{16,0},{32,48},{48,32},{64,80},{80,64},{96,112},{112,96},{1... | collective-permute-start | bytes 368648 | tf_op jit(solution)/shard_map/ppermute | solution.py:406
  23.6 7.1 %copy-start.2 = (bf16[3,3,3,64,128]{4,3,2,1,0:T(8,128)(2,1)S(1)}, bf16[3,3,3,64,128]{4,3,2,1,0:T(8,128)(2,1)}, u32[]{:S(2)}) copy-start(bf16[3,3,3,64,128]{4,3,2,1,0:T(8,128)(2,1)} %param.9) | copy-start | bytes 1327108
  23.6 7.1 %copy-start.3 = (f32[64]{0:T(128)S(1)}, f32[64]{0:T(128)}, u32[]{:S(2)}) copy-start(f32[64]{0:T(128)} %param.8) | copy-start | bytes 772
  23.6 7.0 %copy-start.4 = (f32[128]{0:T(128)S(1)}, f32[128]{0:T(128)}, u32[]{:S(2)}) copy-start(f32[128]{0:T(128)} %param.10) | copy-start | bytes 1540
  23.6 7.0 %collective-permute-start.4 = (bf16[14,1,40,128]{3,2,1,0:T(8,128)(2,1)S(1)}, bf16[14,1,40,128]{3,2,1,0:T(8,128)(2,1)S(1)}, u32[]{:S(2)}, u32[]{:S(2)}) collective-permute-start(bf16[14,1,40,128]{3,2,1,0:T(8,128)(2,1)S(1)} %get-tuple-element.70), channel_id=1, source_target_pairs={{1,2},{2,1},{3,4},{4,3},{5,6},{6,5},{7,8},{8,7},{9,10},{10,9},{11,... | collective-permute-start | bytes 430088 | tf_op jit(solution)/shard_map/ppermute | solution.py:411
  27.9 2.8 %collective-permute-start.3 = (bf16[14,1,40,128]{3,2,1,0:T(8,128)(2,1)S(1)}, bf16[14,1,40,128]{3,2,1,0:T(8,128)(2,1)S(1)}, u32[]{:S(2)}, u32[]{:S(2)}) collective-permute-start(bf16[14,1,40,128]{3,2,1,0:T(8,128)(2,1)S(1)} %get-tuple-element.71), channel_id=1, source_target_pairs={{0,1},{1,0},{2,3},{3,2},{4,5},{5,4},{6,7},{7,6},{8,9},{9,8},{10,11... | collective-permute-start | bytes 430088 | tf_op jit(solution)/shard_map/ppermute | solution.py:412
  36.8 2.7 %collective-permute-start.9 = (bf16[4,4,2,256]{3,2,1,0:T(2,128)(2,1)S(1)}, bf16[4,4,2,256]{3,2,1,0:T(2,128)(2,1)S(1)}, u32[]{:S(2)}, u32[]{:S(2)}) collective-permute-start(bf16[4,4,2,256]{3,2,1,0:T(2,128)(2,1)S(1)} %get-tuple-element.41), channel_id=1, source_target_pairs={{0,128},{128,0},{1,129},{129,1},{2,130},{130,2},{3,131},{131,3},{4... | collective-permute-start | bytes 49160 | tf_op jit(solution)/shard_map/ppermute | solution.py:399
  39.7 5.1 %collective-permute-start.11 = (bf16[2,4,24,256]{3,2,1,0:T(8,128)(2,1)S(1)}, bf16[2,4,24,256]{3,2,1,0:T(8,128)(2,1)S(1)}, u32[]{:S(2)}, u32[]{:S(2)}) collective-permute-start(bf16[2,4,24,256]{3,2,1,0:T(8,128)(2,1)S(1)} %get-tuple-element.80), channel_id=1, source_target_pairs={{16,32},{32,16},{48,64},{64,48},{80,96},{96,80},{17,33},{33,17},{4... | collective-permute-start | bytes 294920 | tf_op jit(solution)/shard_map/ppermute | solution.py:405
  40.3 7.4 %collective-permute-start.10 = (bf16[2,4,24,256]{3,2,1,0:T(8,128)(2,1)S(1)}, bf16[2,4,24,256]{3,2,1,0:T(8,128)(2,1)S(1)}, u32[]{:S(2)}, u32[]{:S(2)}) collective-permute-start(bf16[2,4,24,256]{3,2,1,0:T(8,128)(2,1)S(1)} %get-tuple-element.81), channel_id=1, source_target_pairs={{0,16},{16,0},{32,48},{48,32},{64,80},{80,64},{96,112},{112,96},{1... | collective-permute-start | bytes 294920 | tf_op jit(solution)/shard_map/ppermute | solution.py:406
  47.8 7.3 %collective-permute-start.13 = (bf16[8,1,24,256]{3,2,1,0:T(8,128)(2,1)S(1)}, bf16[8,1,24,256]{3,2,1,0:T(8,128)(2,1)S(1)}, u32[]{:S(2)}, u32[]{:S(2)}) collective-permute-start(bf16[8,1,24,256]{3,2,1,0:T(8,128)(2,1)S(1)} %get-tuple-element.74), channel_id=1, source_target_pairs={{1,2},{2,1},{3,4},{4,3},{5,6},{6,5},{7,8},{8,7},{9,10},{10,9},{11,... | collective-permute-start | bytes 294920 | tf_op jit(solution)/shard_map/ppermute | solution.py:411
  52.8 2.3 %collective-permute-start.12 = (bf16[8,1,24,256]{3,2,1,0:T(8,128)(2,1)S(1)}, bf16[8,1,24,256]{3,2,1,0:T(8,128)(2,1)S(1)}, u32[]{:S(2)}, u32[]{:S(2)}) collective-permute-start(bf16[8,1,24,256]{3,2,1,0:T(8,128)(2,1)S(1)} %get-tuple-element.75), channel_id=1, source_target_pairs={{0,1},{1,0},{2,3},{3,2},{4,5},{5,4},{6,7},{7,6},{8,9},{9,8},{10,11... | collective-permute-start | bytes 294920 | tf_op jit(solution)/shard_map/ppermute | solution.py:412
  53.1 2.0 %copy-start.5 = (bf16[5,10,48,256]{3,2,1,0:T(8,128)(2,1)S(1)}, bf16[5,10,48,256]{3,2,1,0:T(8,128)(2,1)}, u32[]{:S(2)}) copy-start(bf16[5,10,48,256]{3,2,1,0:T(8,128)(2,1)} %get-tuple-element.45.slope_ref) | copy-start | bytes 3686404
  53.1 2.0 %copy-start.7 = (bf16[10,6,40,128]{3,2,1,0:T(8,128)(2,1)S(1)}, bf16[10,6,40,128]{3,2,1,0:T(8,128)(2,1)}, u32[]{:S(2)}) copy-start(bf16[10,6,40,128]{3,2,1,0:T(8,128)(2,1)} %get-tuple-element.46.vo_ref) | copy-start | bytes 1843204
  63.3 1.7 %collective-permute-start.14 = (bf16[1280,128]{1,0:T(8,128)(2,1)S(1)}, bf16[1280,128]{1,0:T(8,128)(2,1)S(1)}, u32[]{:S(2)}, u32[]{:S(2)}) collective-permute-start(bf16[1280,128]{1,0:T(8,128)(2,1)S(1)} %get-tuple-element.49), channel_id=1, source_target_pairs={{0,1},{1,0},{2,3},{3,2},{4,5},{5,4},{6,7},{7,6},{8,9},{9,8},{10,11... | collective-permute-start | bytes 983048 | tf_op jit(solution)/shard_map/ppermute | solution.py:488
  65.9 33.6 %all-to-all-start.1 = ((bf16[128,5,2,128]{3,2,1,0:T(2,128)(2,1)}), bf16[128,5,2,128]{3,2,1,0:T(2,128)(2,1)S(1)}, u32[]{:S(2)}, u32[]{:S(2)}) async-start(bf16[128,5,2,128]{3,2,1,0:T(2,128)(2,1)} %bitcast.22), calls=%async_computation.1 | async-start | bytes 655360 | tf_op jit(solution)/shard_map/all_to_all | solution.py:490
  84.0 42.5 %copy-start.6 = (bf16[5,10,40,256]{3,2,1,0:T(8,128)(2,1)S(1)}, bf16[5,10,40,256]{3,2,1,0:T(8,128)(2,1)}, u32[]{:S(2)}) copy-start(bf16[5,10,40,256]{3,2,1,0:T(8,128)(2,1)} %get-tuple-element.47.ga_ref) | copy-start | bytes 3072004
  84.0 1.6 %collective-permute-start.5 = (bf16[8,1,1,8,4,128]{5,3,4,1,0,2:T(8,128)(2,1)S(1)}, bf16[8,1,1,8,4,128]{5,3,4,1,0,2:T(8,128)(2,1)S(1)}, u32[]{:S(2)}, u32[]{:S(2)}) collective-permute-start(bf16[8,1,1,8,4,128]{5,3,4,1,0,2:T(8,128)(2,1)S(1)} %constant_dynamic-slice_fusion.3), channel_id=1, source_target_pairs={{0,1},{1,0},{2,3},{3,2},{4,5},{5,4},{6,7},{7,6},{8,9},{9,8},{10,11... | collective-permute-start | bytes 196616 | tf_op jit(solution)/shard_map/ppermute | solution.py:426
  100.6 20.2 %all-to-all-start.2 = ((bf16[128,5,2,128]{3,2,1,0:T(2,128)(2,1)}), bf16[128,5,2,128]{3,2,1,0:T(2,128)(2,1)S(1)}, u32[]{:S(2)}, u32[]{:S(2)}) async-start(bf16[128,5,2,128]{3,2,1,0:T(2,128)(2,1)} %shard_map.115), calls=%async_computation.2 | async-start | bytes 655360 | tf_op jit(solution)/shard_map/all_to_all | solution.py:492
  106.8 7.7 %collective-permute-start.6 = (bf16[4,1,2,8,4,128]{5,3,4,2,1,0:T(8,128)(2,1)S(1)}, bf16[4,1,2,8,4,128]{5,3,4,2,1,0:T(8,128)(2,1)S(1)}, u32[]{:S(2)}, u32[]{:S(2)}) collective-permute-start(bf16[4,1,2,8,4,128]{5,3,4,2,1,0:T(8,128)(2,1)S(1)} %constant_dynamic-slice_fusion.2), channel_id=1, source_target_pairs={{0,2},{1,3},{2,0},{3,1},{4,6},{5,7},{6,4},{7,5},{8,10},{9,11},{10,... | collective-permute-start | bytes 196616 | tf_op jit(solution)/shard_map/ppermute | solution.py:426
  114.6 5.5 %collective-permute-start.7 = (bf16[2,1,4,8,4,128]{5,3,2,1,0,4:T(8,128)(2,1)S(1)}, bf16[2,1,4,8,4,128]{5,3,2,1,0,4:T(8,128)(2,1)S(1)}, u32[]{:S(2)}, u32[]{:S(2)}) collective-permute-start(bf16[2,1,4,8,4,128]{5,3,2,1,0,4:T(8,128)(2,1)S(1)} %constant_dynamic-slice_fusion.1), channel_id=1, source_target_pairs={{0,4},{1,5},{2,6},{3,7},{4,0},{5,1},{6,2},{7,3},{8,12},{9,13},{10,... | collective-permute-start | bytes 196616 | tf_op jit(solution)/shard_map/ppermute | solution.py:426
  120.8 13.9 %collective-permute-start.15 = (bf16[1280,128]{1,0:T(8,128)(2,1)S(1)}, bf16[1280,128]{1,0:T(8,128)(2,1)S(1)}, u32[]{:S(2)}, u32[]{:S(2)}) collective-permute-start(bf16[1280,128]{1,0:T(8,128)(2,1)S(1)} %bitcast.37), channel_id=1, source_target_pairs={{0,1},{1,0},{2,3},{3,2},{4,5},{5,4},{6,7},{7,6},{8,9},{9,8},{10,11... | collective-permute-start | bytes 983048 | tf_op jit(solution)/shard_map/ppermute | solution.py:493
  124.9 9.0 %collective-permute-start.8 = (bf16[1,1,8,8,4,128]{5,3,2,1,4,0:T(8,128)(2,1)S(1)}, bf16[1,1,8,8,4,128]{5,3,2,1,4,0:T(8,128)(2,1)S(1)}, u32[]{:S(2)}, u32[]{:S(2)}) collective-permute-start(bf16[1,1,8,8,4,128]{5,3,2,1,4,0:T(8,128)(2,1)S(1)} %constant_dynamic-slice_fusion), channel_id=1, source_target_pairs={{0,8},{1,9},{2,10},{3,11},{4,12},{5,13},{6,14},{7,15},{8,0},{9,1},... | collective-permute-start | bytes 196616 | tf_op jit(solution)/shard_map/ppermute | solution.py:426
